TPU v7x, 32 devices: a whole 2x2x4 slice. The times are simulated.
32 devices in a mesh: dp: 16 (over z, y, core), tensor: 2 (over x).
Axes of the slice: x: 2, y: 2, z: 4, core: 2. Of those that a mesh axis runs over, the one named last changes fastest.
Arguments:
- tokens: bfloat16 [8192, 2048], P(('dp', 'tensor')), may hold values from -6 to 6
- cotangent: bfloat16 [8192, 2048], P(('dp', 'tensor')), may hold values from -6 to 6
- norm_gain: bfloat16 [2048], replicated, may hold values from 0.099609375 to 1.8984375
- w_gate: bfloat16 [2048, 4096], P('dp', 'tensor'), may hold values from -0.125 to 0.125
- w_input: bfloat16 [2048, 4096], P('dp', 'tensor'), may hold values from -0.125 to 0.125
- w_state: bfloat16 [2048, 256], P('dp'), may hold values from -0.125 to 0.125
- w_step: bfloat16 [2048, 64], P('dp', 'tensor'), may hold values from -0.125 to 0.125
- conv_weight: bfloat16 [4, 4096], P(None, 'tensor'), may hold values from -3 to 3
- conv_bias: bfloat16 [4096], P('tensor'), may hold values from -3 to 3
- conv_state_weight: bfloat16 [4, 256], replicated, may hold values from -3 to 3
- conv_state_bias: bfloat16 [256], replicated, may hold values from -3 to 3
- step_bias: bfloat16 [64], P('tensor'), may hold values from -6.875 to -2.25
- decay_log: bfloat16 [64], P('tensor'), may hold values from 0 to 2.765625
- skip_gain: bfloat16 [64], P('tensor'), may hold values from -1 to 1
- gate_gain: bfloat16 [4096], P('tensor'), may hold values from 0.099609375 to 1.8984375
- w_out: bfloat16 [2048, 4096], P('dp', 'tensor'), may hold values from -0.09375 to 0.09375
- stats_gate: float32 [32, 64, 2, 64, 64], P('dp', 'tensor'), as said below
- stats_input: float32 [32, 64, 2, 64, 64], P('dp', 'tensor'), as said below
- stats_state: float32 [32, 4, 2, 64, 64], P('dp'), as said below
- stats_out: float32 [32, 64, 2, 64, 64], P('dp', 'tensor'), as said below
- roots_gate: float32 [32, 64, 2, 64, 64], P('dp', 'tensor'), as said below
- roots_input: float32 [32, 64, 2, 64, 64], P('dp', 'tensor'), as said below
- roots_state: float32 [32, 4, 2, 64, 64], P('dp'), as said below
- roots_out: float32 [32, 64, 2, 64, 64], P('dp', 'tensor'), as said below
- seq_lens: int32 [16, 4], P('dp'), may hold values from 1 to 384, 512 in all within a row
- balance_perm: int32 [8192], P('dp'), may hold values from 0 to 8191, as said below
- inverse_perm: int32 [8192], P(('dp', 'tensor')), may hold values from 0 to 8191, as said below
Outputs:
- block_out: float32 [8192, 2048], P(('dp', 'tensor'))
- tokens_grad: float32 [8192, 2048], P(('dp', 'tensor'))
- norm_gain_grad: float32 [2048], replicated
- w_gate_grad: float32 [2048, 4096], P('dp', 'tensor')
- w_input_grad: float32 [2048, 4096], P('dp', 'tensor')
- w_state_grad: float32 [2048, 256], P('dp')
- w_step_grad: float32 [2048, 64], P('dp', 'tensor')
- conv_weight_grad: float32 [4, 4096], P(None, 'tensor')
- conv_bias_grad: float32 [4096], P('tensor')
- conv_state_weight_grad: float32 [4, 256], replicated
- conv_state_bias_grad: float32 [256], replicated
- step_bias_grad: float32 [64], P('tensor')
- decay_log_grad: float32 [64], P('tensor')
- skip_gain_grad: float32 [64], P('tensor')
- gate_gain_grad: float32 [4096], P('tensor')
- w_out_grad: float32 [2048, 4096], P('dp', 'tensor')
- stats_gate_new: float32 [32, 64, 2, 64, 64], P('dp', 'tensor')
- stats_input_new: float32 [32, 64, 2, 64, 64], P('dp', 'tensor')
- stats_state_new: float32 [32, 4, 2, 64, 64], P('dp')
- stats_out_new: float32 [32, 64, 2, 64, 64], P('dp', 'tensor')
- master_gate: float32 [2048, 4096], P('dp', 'tensor')
- master_input: float32 [2048, 4096], P('dp', 'tensor')
- master_state: float32 [2048, 256], P('dp')
- master_out: float32 [2048, 4096], P('dp', 'tensor')
- copy_gate: bfloat16 [2048, 4096], P('dp', 'tensor')
- copy_input: bfloat16 [2048, 4096], P('dp', 'tensor')
- copy_state: bfloat16 [2048, 256], P('dp')
- copy_out: bfloat16 [2048, 4096], P('dp', 'tensor')
Inputs may be any that keep to these rules, and one draw needn't show every extreme that they name: `seq_lens`: row g lists the lengths of the 4 sequences that fill balanced positions g * 512 to (g + 1) * 512 - 1 one after another. balance_perm is a permutation; of the 256 given positions d * 256 to (d + 1) * 256 - 1 of each device d, exactly 16 land in the 512 balanced positions of each group. `inverse_perm`: the inverse permutation of balance_perm. `stats_gate`: both matrices of each block pair are symmetric. `stats_input`: both matrices of each block pair are symmetric. `stats_state`: both matrices of each block pair are symmetric. `stats_out`: both matrices of each block pair are symmetric. `roots_gate`: both matrices of each block pair are symmetric. `roots_input`: both matrices of each block pair are symmetric. `roots_state`: both matrices of each block pair are symmetric. `roots_out`: both matrices of each block pair are symmetric.
All inputs are finite; a program needn't handle non-finite values.
Results may differ from a plain program's by a relative error of at most 0.019.
Values may be sent and summed in bfloat16 or wider, within the bound.
A program may use at most 256 MiB of HBM per device.

v0:
```python
import jax
import jax.numpy as jnp
from jax import lax
from jax.sharding import PartitionSpec as P

D = 2048
STATE = 128
KCONV = 4
SPAN = 256
BLK = 64
INNER = 4096


EPSILON = 1e-05
DECAY_RATE = 0.5
LEARN_RATE = 0.2
HIGHEST = lax.Precision.HIGHEST


def segment_info(lengths, row_count):
    starts = jnp.cumsum(lengths) - lengths
    row_index = jnp.arange(row_count, dtype=jnp.int32)
    passed = row_index[:, None] >= starts[None, :]
    segment = jnp.sum(passed.astype(jnp.int32), axis=1) - 1
    seq_begin = jnp.max(jnp.where(passed, starts[None, :], 0), axis=1)
    return (segment, row_index - seq_begin)


def causal_conv(values, kernel, offset_bias, position):
    summed = jnp.zeros_like(values) + offset_bias[None, :]
    for offset in range(KCONV):
        shifted = jnp.pad(values, ((offset, 0), (0, 0)))[: values.shape[0]]
        inside = (position >= offset).astype(jnp.float32)[:, None]
        summed = summed + kernel[offset][None, :] * shifted * inside
    return summed


def block_scan(state_in, operands):
    inner_act, step_len, decay_step, input_map, output_map, segment, alive_mask = operands
    row_order = jnp.arange(segment.shape[0], dtype=jnp.int32)
    cumulative = jnp.cumsum(decay_step, axis=0).T
    allowed = (segment[:, None] == segment[None, :]) & (row_order[:, None] >= row_order[None, :])
    spread = cumulative[:, :, None] - cumulative[:, None, :]
    weights = jnp.where(allowed[None], jnp.exp(jnp.where(allowed[None], spread, 0.0)), 0.0)
    scores = jnp.dot(output_map, input_map.T, precision=HIGHEST, preferred_element_type=jnp.float32)
    driven = step_len[:, :, None] * inner_act
    within = jnp.einsum("hij,jhp->ihp", weights * scores[None], driven, precision=HIGHEST)
    carried = jnp.einsum("in,hpn->ihp", output_map, state_in, precision=HIGHEST)
    carried = carried * (jnp.exp(cumulative).T * alive_mask[:, None])[:, :, None]
    last_sum = cumulative[:, -1]
    same_last = (segment == segment[-1]).astype(jnp.float32)
    toward = jnp.exp(last_sum[None, :] - cumulative.T) * same_last[:, None]
    fresh_state = jnp.einsum("jh,jhp,jn->hpn", toward, driven, input_map, precision=HIGHEST)
    state_out = state_in * (jnp.exp(last_sum) * alive_mask[-1])[:, None, None] + fresh_state
    return (state_out, within + carried)


def mixer_core(
    gate_proj,
    inner_proj,
    state_proj,
    step_raw,
    conv_weight,
    conv_bias,
    conv_state_weight,
    conv_state_bias,
    step_bias,
    decay_log,
    skip_gain,
    segment,
    position,
):
    row_count = gate_proj.shape[0]
    head_count = skip_gain.shape[0]
    head_width = gate_proj.shape[1] // head_count
    inner_act = jax.nn.silu(causal_conv(inner_proj, conv_weight, conv_bias, position))
    state_act = jax.nn.silu(causal_conv(state_proj, conv_state_weight, conv_state_bias, position))
    input_map = state_act[:, :STATE]
    output_map = state_act[:, STATE:]
    step_len = jax.nn.softplus(step_raw + step_bias[None, :])
    decay_step = -step_len * jnp.exp(decay_log)[None, :]
    block_count = row_count // SPAN
    seg_blocks = segment.reshape(block_count, SPAN)
    previous = jnp.concatenate([jnp.full((1,), -1, jnp.int32), seg_blocks[:-1, -1]])
    alive_mask = (seg_blocks == previous[:, None]).astype(jnp.float32)
    start_state = jnp.zeros((head_count, head_width, STATE), jnp.float32)
    operands = (
        inner_act.reshape(block_count, SPAN, head_count, head_width),
        step_len.reshape(block_count, SPAN, head_count),
        decay_step.reshape(block_count, SPAN, head_count),
        input_map.reshape(block_count, SPAN, STATE),
        output_map.reshape(block_count, SPAN, STATE),
        seg_blocks,
        alive_mask,
    )
    final_state, scanned = lax.scan(jax.checkpoint(block_scan), start_state, operands)
    mixed_out = (
        scanned.reshape(row_count, head_count * head_width)
        + inner_act * jnp.repeat(skip_gain, head_width)[None, :]
    )
    return mixed_out * jax.nn.silu(gate_proj)


def shampoo(weight, gradient, stat_pair, root_pair):
    row_count, col_count = gradient.shape
    blocks = gradient.reshape(row_count // BLK, BLK, col_count // BLK, BLK).transpose(0, 2, 1, 3)
    left_stat = jnp.einsum("abij,abkj->abik", blocks, blocks, precision=HIGHEST)
    right_stat = jnp.einsum("abji,abjk->abik", blocks, blocks, precision=HIGHEST)
    fresh_stats = jnp.stack([left_stat, right_stat], axis=2)
    new_stats = DECAY_RATE * stat_pair + (1.0 - DECAY_RATE) * fresh_stats
    turned = jnp.einsum("abij,abjk->abik", root_pair[:, :, 0], blocks, precision=HIGHEST)
    turned = jnp.einsum("abij,abjk->abik", turned, root_pair[:, :, 1], precision=HIGHEST)
    update_step = turned.transpose(0, 2, 1, 3).reshape(row_count, col_count)
    master = weight - LEARN_RATE * update_step
    return (new_stats, master, master.astype(jnp.bfloat16))


def contract_rows(left_side, right_side):
    return lax.dot_general(
        left_side, right_side, (((0,), (0,)), ((), ())), preferred_element_type=jnp.float32
    )


def contract_cols(left_side, right_side):
    return lax.dot_general(
        left_side, right_side, (((1,), (1,)), ((), ())), preferred_element_type=jnp.float32
    )


def body(
    tokens,
    cotangent,
    norm_gain,
    w_gate,
    w_input,
    w_state,
    w_step,
    conv_weight,
    conv_bias,
    conv_state_weight,
    conv_state_bias,
    step_bias,
    decay_log,
    skip_gain,
    gate_gain,
    w_out,
    stats_gate,
    stats_input,
    stats_state,
    stats_out,
    roots_gate,
    roots_input,
    roots_state,
    roots_out,
    seq_lens,
    balance_perm,
    inverse_perm,
):
    groups = lax.axis_size("dp")
    tensor_ranks = lax.axis_size("tensor")
    local_rows = tokens.shape[0]
    slot_rows = local_rows // groups
    group_rows = local_rows * tensor_ranks
    tokens_f = tokens.astype(jnp.float32)
    scale_in = lax.rsqrt(jnp.mean(tokens_f * tokens_f, axis=1) + EPSILON)
    gain_in = norm_gain.astype(jnp.float32)
    normed = (tokens_f * scale_in[:, None] * gain_in[None, :]).astype(jnp.bfloat16)
    send_order = jnp.argsort(inverse_perm)
    arrived = (
        lax.all_to_all(
            normed[send_order].reshape(groups, slot_rows, D),
            "dp",
            split_axis=0,
            concat_axis=0,
            tiled=True,
        ),
        lax.all_to_all(
            cotangent[send_order].reshape(groups, slot_rows, D),
            "dp",
            split_axis=0,
            concat_axis=0,
            tiled=True,
        ),
    )
    collected = (
        lax.all_gather(arrived[0], "tensor", axis=0, tiled=True),
        lax.all_gather(arrived[1], "tensor", axis=0, tiled=True),
    )
    source = balance_perm // local_rows
    row_key = (source % tensor_ranks * groups + source // tensor_ranks) * group_rows + jnp.arange(
        group_rows, dtype=jnp.int32
    )
    layout = jnp.argsort(row_key)
    placing = jnp.argsort(layout)
    normed_bal = collected[0].reshape(group_rows, D)[placing]
    cot_bal = collected[1].reshape(group_rows, D)[placing]
    segment, position = segment_info(seq_lens[0], group_rows)
    pieces = (
        lax.all_gather(w_gate, "dp", axis=0, tiled=True),
        lax.all_gather(w_input, "dp", axis=0, tiled=True),
        lax.all_gather(w_state, "dp", axis=0, tiled=True),
        lax.all_gather(w_step, "dp", axis=0, tiled=True),
    )
    columns = normed_bal
    gate_proj, inner_proj, state_proj, step_raw = tuple(
        (
            jnp.dot(columns, pieces[member], preferred_element_type=jnp.float32)
            for member in range(4)
        )
    )

    def local_piece(
        gate_v, inner_v, state_v, step_v, conv_w, conv_b, conv_sw, conv_sb, step_b, decay_v, skip_v
    ):
        return mixer_core(
            gate_v,
            inner_v,
            state_v,
            step_v,
            conv_w,
            conv_b,
            conv_sw,
            conv_sb,
            step_b,
            decay_v,
            skip_v,
            segment,
            position,
        )

    gated_out, local_back = jax.vjp(
        local_piece,
        gate_proj,
        inner_proj,
        state_proj,
        step_raw,
        conv_weight.astype(jnp.float32),
        conv_bias.astype(jnp.float32),
        conv_state_weight.astype(jnp.float32),
        conv_state_bias.astype(jnp.float32),
        step_bias.astype(jnp.float32),
        decay_log.astype(jnp.float32),
        skip_gain.astype(jnp.float32),
    )
    whole_square = lax.psum(jnp.sum(gated_out * gated_out, axis=1), "tensor")
    gate_scale = lax.rsqrt(whole_square / INNER + EPSILON)
    gain_gate = gate_gain.astype(jnp.float32)
    normal = (gated_out * gate_scale[:, None] * gain_gate[None, :]).astype(jnp.bfloat16)
    partial_out = contract_cols(normal, lax.all_gather(w_out, "dp", axis=0, tiled=True))
    w_out_part = contract_rows(cot_bal, normal)
    columns = cot_bal
    d_normal = jnp.dot(
        columns, lax.all_gather(w_out, "dp", axis=0, tiled=True), preferred_element_type=jnp.float32
    )
    gain_gate_part = jnp.sum(d_normal * gated_out * gate_scale[:, None], axis=0)
    dot_total = lax.psum(jnp.sum(gated_out * gain_gate[None, :] * d_normal, axis=1), "tensor")
    d_gated = (
        d_normal * gate_scale[:, None] * gain_gate[None, :]
        - gated_out * (gate_scale**3 * dot_total / INNER)[:, None]
    )
    local_grads = local_back(d_gated)
    d_gate = local_grads[0].astype(jnp.bfloat16)
    d_inner = local_grads[1].astype(jnp.bfloat16)
    d_state = local_grads[2].astype(jnp.bfloat16)
    d_step = local_grads[3].astype(jnp.bfloat16)
    summed_grads = (
        lax.psum_scatter(
            contract_rows(normed_bal, d_gate).astype(jnp.bfloat16),
            "dp",
            scatter_dimension=0,
            tiled=True,
        ).astype(jnp.float32),
        lax.psum_scatter(
            contract_rows(normed_bal, d_inner).astype(jnp.bfloat16),
            "dp",
            scatter_dimension=0,
            tiled=True,
        ).astype(jnp.float32),
        lax.psum_scatter(
            contract_rows(normed_bal, d_state).astype(jnp.bfloat16),
            "dp",
            scatter_dimension=0,
            tiled=True,
        ).astype(jnp.float32),
        lax.psum_scatter(
            contract_rows(normed_bal, d_step).astype(jnp.bfloat16),
            "dp",
            scatter_dimension=0,
            tiled=True,
        ).astype(jnp.float32),
        lax.psum_scatter(
            w_out_part.astype(jnp.bfloat16), "dp", scatter_dimension=0, tiled=True
        ).astype(jnp.float32),
    )
    pieces = (
        lax.all_gather(w_gate, "dp", axis=0, tiled=True),
        lax.all_gather(w_input, "dp", axis=0, tiled=True),
        lax.all_gather(w_state, "dp", axis=0, tiled=True),
        lax.all_gather(w_step, "dp", axis=0, tiled=True),
    )
    column_term = (
        contract_cols(d_gate, pieces[0])
        + contract_cols(d_inner, pieces[1])
        + contract_cols(d_state, pieces[2])
        + contract_cols(d_step, pieces[3])
    )
    row_totals = (
        lax.psum_scatter(
            partial_out[layout].astype(jnp.bfloat16), "tensor", scatter_dimension=0, tiled=True
        ).astype(jnp.float32),
        lax.psum_scatter(
            column_term[layout].astype(jnp.bfloat16), "tensor", scatter_dimension=0, tiled=True
        ).astype(jnp.float32),
    )
    returning = (
        lax.all_to_all(
            row_totals[0].astype(jnp.bfloat16).reshape(groups, slot_rows, D),
            "dp",
            split_axis=0,
            concat_axis=0,
            tiled=True,
        ),
        lax.all_to_all(
            row_totals[1].astype(jnp.bfloat16).reshape(groups, slot_rows, D),
            "dp",
            split_axis=0,
            concat_axis=0,
            tiled=True,
        ),
    )
    back_order = jnp.argsort(send_order)
    branch = returning[0].reshape(local_rows, D)[back_order].astype(jnp.float32)
    d_tokens_normed = returning[1].reshape(local_rows, D)[back_order].astype(jnp.float32)
    block_out = tokens_f + branch
    norm_gain_part = jnp.sum(d_tokens_normed * tokens_f * scale_in[:, None], axis=0)
    dot_in = jnp.sum(tokens_f * gain_in[None, :] * d_tokens_normed, axis=1)
    tokens_grad = (
        cotangent.astype(jnp.float32)
        + d_tokens_normed * scale_in[:, None] * gain_in[None, :]
        - tokens_f * (scale_in**3 * dot_in / D)[:, None]
    )
    over_groups = lax.psum(
        (
            norm_gain_part,
            local_grads[6],
            local_grads[7],
            local_grads[4],
            local_grads[5],
            local_grads[8],
            local_grads[9],
            local_grads[10],
            gain_gate_part,
        ),
        "dp",
    )
    over_ranks = (
        lax.psum(summed_grads[2].astype(jnp.bfloat16), "tensor").astype(jnp.float32),
        lax.psum(over_groups[0].astype(jnp.bfloat16), "tensor").astype(jnp.float32),
        lax.psum(over_groups[1].astype(jnp.bfloat16), "tensor").astype(jnp.float32),
        lax.psum(over_groups[2].astype(jnp.bfloat16), "tensor").astype(jnp.float32),
    )
    new_gate = shampoo(w_gate.astype(jnp.float32), summed_grads[0], stats_gate, roots_gate)
    new_input = shampoo(w_input.astype(jnp.float32), summed_grads[1], stats_input, roots_input)
    new_state = shampoo(w_state.astype(jnp.float32), over_ranks[0], stats_state, roots_state)
    new_out = shampoo(w_out.astype(jnp.float32), summed_grads[4], stats_out, roots_out)
    return (
        block_out,
        tokens_grad,
        over_ranks[1],
        summed_grads[0],
        summed_grads[1],
        over_ranks[0],
        summed_grads[3],
        over_groups[3],
        over_groups[4],
        over_ranks[2],
        over_ranks[3],
        over_groups[5],
        over_groups[6],
        over_groups[7],
        over_groups[8],
        summed_grads[4],
        new_gate[0],
        new_input[0],
        new_state[0],
        new_out[0],
        new_gate[1],
        new_input[1],
        new_state[1],
        new_out[1],
        new_gate[2],
        new_input[2],
        new_state[2],
        new_out[2],
    )


def solution(mesh):
    placed = (
        P(("dp", "tensor"), None),
        P(("dp", "tensor"), None),
        P(),
        P("dp", "tensor"),
        P("dp", "tensor"),
        P("dp", None),
        P("dp", "tensor"),
        P(None, "tensor"),
        P("tensor"),
        P(),
        P(),
        P("tensor"),
        P("tensor"),
        P("tensor"),
        P("tensor"),
        P("dp", "tensor"),
        P("dp", "tensor", None, None, None),
        P("dp", "tensor", None, None, None),
        P("dp", None, None, None, None),
        P("dp", "tensor", None, None, None),
        P("dp", "tensor", None, None, None),
        P("dp", "tensor", None, None, None),
        P("dp", None, None, None, None),
        P("dp", "tensor", None, None, None),
        P("dp", None),
        P("dp"),
        P(("dp", "tensor")),
    )
    return jax.shard_map(
        body,
        mesh=mesh,
        in_specs=placed,
        out_specs=(
            P(("dp", "tensor"), None),
            P(("dp", "tensor"), None),
            P(),
            P("dp", "tensor"),
            P("dp", "tensor"),
            P("dp", None),
            P("dp", "tensor"),
            P(None, "tensor"),
            P("tensor"),
            P(),
            P(),
            P("tensor"),
            P("tensor"),
            P("tensor"),
            P("tensor"),
            P("dp", "tensor"),
            P("dp", "tensor", None, None, None),
            P("dp", "tensor", None, None, None),
            P("dp", None, None, None, None),
            P("dp", "tensor", None, None, None),
            P("dp", "tensor"),
            P("dp", "tensor"),
            P("dp", None),
            P("dp", "tensor"),
            P("dp", "tensor"),
            P("dp", "tensor"),
            P("dp", None),
            P("dp", "tensor"),
        ),
        check_vma=False,
    )
```

profile of v0, /device:TPU:0, one launch (start us, length us, event | category | flops | bytes accessed | tf_op | source)
XLA Modules:
  0.0 1189.0 jit_solution(3767888222029125385)
XLA Ops:
  17.4 32.0 %all_to_all.20 = bf16[16,16,2048]{2,1,0:T(8,128)(2,1)} all-to-all(bf16[16,16,2048]{2,1,0:T(8,128)(2,1)S(1)} %bitcast.518), channel_id=1, replica_groups=mesh['dp'=16,'tensor'=2] {'dp'}, dimensions={0} | all-to-all | bytes 2097152 | tf_op jit(solution)/shard_map/all_to_all | solution.py:170
  51.0 29.7 %all_to_all.21 = bf16[16,16,2048]{2,1,0:T(8,128)(2,1)} all-to-all(bf16[16,16,2048]{2,1,0:T(8,128)(2,1)S(1)} %bitcast.519), channel_id=1, replica_groups=mesh['dp'=16,'tensor'=2] {'dp'}, dimensions={0} | all-to-all | bytes 2097152 | tf_op jit(solution)/shard_map/all_to_all | solution.py:177
  92.1 21.3 %all_gather.27 = bf16[2048,32]{0,1:T(8,128)(2,1)S(1)} all-gather(bf16[128,32]{0,1:T(8,128)(2,1)S(1)} %copy-done.88), channel_id=1, replica_groups=mesh['dp'=16,'tensor'=2] {'dp'}, dimensions={0}, use_global_device_ids=true | all-gather | bytes 139264 | tf_op jit(solution)/shard_map/all_gather | solution.py:202
  133.3 25.8 %all-gather.11.cloned.1.call-done = bf16[2048,256]{1,0:T(8,128)(2,1)} async-done(((bf16[128,256]{1,0:T(8,128)(2,1)}), bf16[2048,256]{1,0:T(8,128)(2,1)}) %all-gather.11.cloned.1.call-update) | async-done | bytes 1048592 | tf_op jit(solution)/shard_map/all_gather | solution.py:201
  163.1 71.4 %all-gather.9.cloned.1.call-done = bf16[2048,2048]{1,0:T(8,128)(2,1)} async-done(((bf16[128,2048]{1,0:T(8,128)(2,1)}), bf16[2048,2048]{1,0:T(8,128)(2,1)}) %all-gather.9.cloned.1.call-update) | async-done | bytes 8388624 | tf_op jit(solution)/shard_map/all_gather | solution.py:200
  267.3 45.6 %while.42 = (s32[]{:T(128)}, f32[32,64,128]{2,1,0:T(8,128)S(1)}, f32[2,256,32,64]{1,3,2,0:T(8,128)}, f32[2,32,64,128]{3,2,1,0:T(8,128)}, f32[2,256,32]{1,2,0:T(8...) while((s32[]{:T(128)}, f32[32,64,128]{2,1,0:T(8,128)S(1)}, ...), condition=%wide.region_10.11_spmd.clone, body=%wide.region_7.10_spmd.clone.sunk | while | flops 3335488000 | bytes 84591224 | solution.py:96
  274.2 11.3 fusion.310
  297.0 11.3 fusion.310
  330.4 15.4 %multiply_reduce_fusion.12 = (f32[512]{0:T(512)S(1)}, f32[512,2048]{1,0:T(8,128)}, f32[512,2048]{1,0:T(8,128)}) fusion(f32[512,2048]{1,0:T(8,128)} %reshape.702, f32[2048]{0:T(1024)S(1)} %mul.1045, f32[512,2048]{1,0:T(8,128)} %get-tuple-element.1095, bf16[512,2048]{1,0:T(8,128)(2,1)} %gather_fusion.1, bf16[2048,2048]{1,0:T(8,128)(2,1)} %all-gather.13.cloned.1.call-done), kind=kOutput, calls=%fused_computation.190 | convolution fusion | flops 4308598272 | bytes 27273216 | tf_op jit(solution)/shard_map/dot_general | solution.py:207
  350.7 33.6 %all-gather.15.cloned.1.call-done = bf16[2048,2048]{1,0:T(8,128)(2,1)} async-done(((bf16[128,2048]{1,0:T(8,128)(2,1)}), bf16[2048,2048]{1,0:T(8,128)(2,1)}) %all-gather.15.cloned.1.call-update) | async-done | bytes 8388624 | tf_op jit(solution)/shard_map/all_gather | solution.py:249
  384.3 12.4 %multiply_reduce_fusion.5 = (f32[2048]{0:T(1024)}, f32[512]{0:T(512)S(1)}, f32[512,2048]{1,0:T(8,128)}) fusion(f32[512,2048]{1,0:T(8,128)} %get-tuple-element.1091, f32[512]{0:T(512)S(1)} %add_rsqrt_fusion, f32[2048]{0:T(1024)S(1)} %convert_element_type.226, bf16[512,2048]{1,0:T(8,128)(2,1)} %gather_fusion.5, ...), kind=kOutput, calls=%fused_computation.180 | convolution fusion | flops 4301256192 | bytes 18894848 | tf_op jit(solution)/shard_map/dot_general | solution.py:252
  401.7 11.6 multiply_reduce_fusion.6
  434.2 183.6 %while.43 = (s32[]{:T(128)}, f32[32,64,128]{2,1,0:T(8,128)S(1)}, f32[2,256,32,64]{1,3,2,0:T(8,128)}, f32[2,256,32]{1,0,2:T(2,128)}, f32[2,256,32]{1,0,2:T(2,128)...) while((s32[]{:T(128)}, f32[32,64,128]{2,1,0:T(8,128)S(1)}, ...), condition=%wide.region_29.30_spmd.clone, body=%wide.region_17.29_spmd.clone.sunk | while | flops 7592780288 | bytes 83838168 | solution.py:96
  463.2 14.2 %fusion.330 = (f32[32,256]{1,0:T(8,128)}, f32[32,256]{1,0:T(8,128)}, f32[256,256]{1,0:T(8,128)}) fusion(f32[256,256]{1,0:T(8,128)S(1)} %fusion.328, f32[32,256]{1,0:T(8,128)} %copy_bitcast_fusion.13, pred[256,256]{1,0:T(8,128)(4,1)} %fusion.329, f32[256,32,64]{0,2,1:T(8,128)} %get-tuple-element.1344, f32[256,32]{0,1:T(8,128)} %get-tuple-element.1345, ...), kind=kOutput, calls=%fused_computation.70.clone.1 | convolution fusion | flops 1634123776 | bytes 4915200 | tf_op jit(solution)/shard_map/transpose(jvp())/while/body/eval_jaxpr/checkpoint/hij,jhp->ihp/dot_general | solution.py:47
  484.5 10.6 multiply_reduce_fusion.22
  550.5 14.2 %fusion.330 = (f32[32,256]{1,0:T(8,128)}, f32[32,256]{1,0:T(8,128)}, f32[256,256]{1,0:T(8,128)}) fusion(f32[256,256]{1,0:T(8,128)S(1)} %fusion.328, f32[32,256]{1,0:T(8,128)} %copy_bitcast_fusion.13, pred[256,256]{1,0:T(8,128)(4,1)} %fusion.329, f32[256,32,64]{0,2,1:T(8,128)} %get-tuple-element.1344, f32[256,32]{0,1:T(8,128)} %get-tuple-element.1345, ...), kind=kOutput, calls=%fused_computation.70.clone.1 | convolution fusion | flops 1634123776 | bytes 4915200 | tf_op jit(solution)/shard_map/transpose(jvp())/while/body/eval_jaxpr/checkpoint/hij,jhp->ihp/dot_general | solution.py:47
  655.6 14.9 %multiply_reduce_fusion.10 = (f32[2048]{0:T(1024)S(1)}, f32[2048]{0:T(1024)}, f32[2048]{0:T(1024)}, f32[2048]{0:T(1024)}, f32[2048]{0:T(1024)S(1)}, /*index=5*/f32[512,2048]{1,0:T(8,128)}) fusion(f32[512,2048]{1,0:T(8,128)} %copy-done.15, f32[512]{0:T(512)S(1)} %copy-done.56, f32[512]{0:T(512)S(1)} %copy-done.54, f32[512]{0:T(512)S(1)} %copy-done.52, ...), kind=kLoop, calls=%fused_computation.185 | loop fusion | flops 25155584 | bytes 21028864 | tf_op jit(solution)/shard_map/transpose(jvp())/reduce_sum | solution.py:34
  734.9 15.9 %reduce-scatter.12.cloned.1.call-done = bf16[256,2048]{1,0:T(8,128)(2,1)} async-done(((bf16[512,2048]{1,0:T(8,128)(2,1)}), bf16[256,2048]{1,0:T(8,128)(2,1)}) %reduce-scatter.12.cloned.1.call-update) | async-done | bytes 1048592 | tf_op jit(solution)/shard_map/reduce_scatter | solution.py:311
  764.4 46.7 %reduce-scatter.22.cloned.1.call-done = bf16[128,32]{1,0:T(8,128)(2,1)} async-done(((bf16[2048,32]{1,0:T(8,128)(2,1)}), bf16[128,32]{1,0:T(8,128)(2,1)}) %reduce-scatter.22.cloned.1.call-update) | async-done | bytes 8208
  812.6 20.8 %all-reduce.27.cloned.1.call-done = bf16[128,256]{1,0:T(8,128)(2,1)} async-done(((bf16[128,256]{1,0:T(8,128)(2,1)}), bf16[128,256]{1,0:T(8,128)(2,1)}) %all-reduce.27.cloned.1.call-update) | async-done | bytes 65552 | tf_op jit(solution)/shard_map/psum | solution.py:357
  845.9 64.1 %all-reduce.23 = (bf16[2048]{0:T(1024)(128)(2,1)S(1)}, f32[4,2048]{1,0:T(4,128)}, f32[2048]{0:T(1024)}, bf16[4,256]{1,0:T(4,128)(2,1)S(1)}, bf16[256]{0:T(256)(1...) all-reduce(f32[2048]{0:T(1024)S(1)} %get-tuple-element.1001, ...), channel_id=1, replica_groups=mesh['dp'=16,'tensor'=2] {'dp'}, use_global_device_ids=true, to_apply=%region_33.34 | all-reduce | flops 15712 | bytes 119040 | tf_op jit(solution)/shard_map/psum | solution.py:342
  921.3 20.0 %reduce-scatter.20.cloned.1.call-done = bf16[128,2048]{1,0:T(8,128)(2,1)} async-done(((bf16[2048,2048]{1,0:T(8,128)(2,1)}), bf16[128,2048]{1,0:T(8,128)(2,1)}) %reduce-scatter.20.cloned.1.call-update) | async-done | bytes 524304 | tf_op jit(solution)/shard_map/reduce_scatter | solution.py:291
  963.7 84.7 %reduce-scatter.14.cloned.1.call-done = bf16[128,2048]{1,0:T(8,128)(2,1)} async-done(((bf16[2048,2048]{1,0:T(8,128)(2,1)}), bf16[128,2048]{1,0:T(8,128)(2,1)}) %reduce-scatter.14.cloned.1.call-update) | async-done | bytes 524304 | tf_op jit(solution)/shard_map/reduce_scatter | solution.py:267
  1072.9 82.5 %reduce-scatter.16.cloned.1.call-done = bf16[128,2048]{1,0:T(8,128)(2,1)} async-done(((bf16[2048,2048]{1,0:T(8,128)(2,1)}), bf16[128,2048]{1,0:T(8,128)(2,1)}) %reduce-scatter.16.cloned.1.call-update) | async-done | bytes 524304 | tf_op jit(solution)/shard_map/reduce_scatter | solution.py:273
  (594 shorter events, 499.0 us)
Async XLA Ops:
  7.2 108.3 %all-gather.7.cloned.1.call-start = ((), (), s32[]{:S(2)}) async-start(), calls=%async_computation.11 | async-start | bytes 3145728 | tf_op jit(solution)/shard_map/all_gather | solution.py:186
  49.5 73.1 %all-gather.17.cloned.1.call-start = ((), (), s32[]{:S(2)}) async-start(), calls=%async_computation.17 | async-start | bytes 3145728 | tf_op jit(solution)/shard_map/all_gather | solution.py:187
  80.8 78.4 %all-gather.11.cloned.1.call-start = ((), (), s32[]{:S(2)}) async-start(), calls=%async_computation.13 | async-start | bytes 1114112 | tf_op jit(solution)/shard_map/all_gather | solution.py:201
  81.5 152.9 %all-gather.9.cloned.1.call-start = ((), (), s32[]{:S(2)}) async-start(), calls=%async_computation.12 | async-start | bytes 8912896 | tf_op jit(solution)/shard_map/all_gather | solution.py:200
  82.1 248.2 %all-gather.13.cloned.1.call-start = ((), (), s32[]{:S(2)}) async-start(), calls=%async_computation.14 | async-start | bytes 8912896 | tf_op jit(solution)/shard_map/all_gather | solution.py:199
  82.7 301.6 %all-gather.15.cloned.1.call-start = ((), (), s32[]{:S(2)}) async-start(), calls=%async_computation.15 | async-start | bytes 8912896 | tf_op jit(solution)/shard_map/all_gather | solution.py:249
  83.3 615.8 %reduce-scatter.18.cloned.1.call-start = ((), (), s32[]{:S(2)}) async-start(), calls=%async_computation.21 | async-start | bytes 1114112 | tf_op jit(solution)/shard_map/reduce_scatter | solution.py:279
  84.3 317.3 %copy-start.69 = (f32[2048]{0:T(1024)}, f32[2048]{0:T(1024)S(1)}, u32[]{:S(2)}) copy-start(f32[2048]{0:T(1024)S(1)} %convert_element_type.226) | copy-start | bytes 24580
  84.5 317.2 %copy-start.57 = (f32[2048]{0:T(1024)}, f32[2048]{0:T(1024)S(1)}, u32[]{:S(2)}) copy-start(f32[2048]{0:T(1024)S(1)} %mul.1045) | copy-start | bytes 24580
  115.4 126.7 %copy-start.49 = (f32[512]{0:T(512)}, f32[512]{0:T(512)S(1)}, u32[]{:S(2)}) copy-start(f32[512]{0:T(512)S(1)} %get-tuple-element.1129) | copy-start | bytes 6148
  115.4 126.7 %copy-start.51 = (f32[512]{0:T(512)}, f32[512]{0:T(512)S(1)}, u32[]{:S(2)}) copy-start(f32[512]{0:T(512)S(1)} %get-tuple-element.1130) | copy-start | bytes 6148
  115.4 126.7 %copy-start.53 = (f32[512]{0:T(512)}, f32[512]{0:T(512)S(1)}, u32[]{:S(2)}) copy-start(f32[512]{0:T(512)S(1)} %get-tuple-element.1131) | copy-start | bytes 6148
  115.4 126.7 %copy-start.55 = (f32[512]{0:T(512)}, f32[512]{0:T(512)S(1)}, u32[]{:S(2)}) copy-start(f32[512]{0:T(512)S(1)} %get-tuple-element.1132) | copy-start | bytes 6148
  115.4 126.7 %copy-start.59 = (f32[1,2048]{1,0:T(1,128)}, f32[1,2048]{1,0:T(1,128)S(1)}, u32[]{:S(2)}) copy-start(f32[1,2048]{1,0:T(1,128)S(1)} %get-tuple-element.1121) | copy-start | bytes 24580
  115.5 126.7 %copy-start.61 = (f32[1,2048]{1,0:T(1,128)}, f32[1,2048]{1,0:T(1,128)S(1)}, u32[]{:S(2)}) copy-start(f32[1,2048]{1,0:T(1,128)S(1)} %get-tuple-element.1122) | copy-start | bytes 24580
  625.9 102.0 %reduce-scatter.10.cloned.1.call-start = ((), (), s32[]{:S(2)}) async-start(), calls=%async_computation.16 | async-start | bytes 3145728 | tf_op jit(solution)/shard_map/reduce_scatter | solution.py:308
  670.6 80.3 %reduce-scatter.12.cloned.1.call-start = ((), (), s32[]{:S(2)}) async-start(), calls=%async_computation.18 | async-start | bytes 3145728 | tf_op jit(solution)/shard_map/reduce_scatter | solution.py:311
  695.7 115.5 %reduce-scatter.22.cloned.1.call-start = ((), (), s32[]{:S(2)}) async-start(), calls=%async_computation.24 | async-start | bytes 557056
  699.0 134.4 %all-reduce.27.cloned.1.call-start = ((), (), s32[]{:S(2)}) async-start(), calls=%async_computation.22 | async-start | bytes 131072 | tf_op jit(solution)/shard_map/psum | solution.py:357
  699.7 241.5 %reduce-scatter.20.cloned.1.call-start = ((), (), s32[]{:S(2)}) async-start(), calls=%async_computation.23 | async-start | bytes 8912896 | tf_op jit(solution)/shard_map/reduce_scatter | solution.py:291
  709.0 339.4 %reduce-scatter.14.cloned.1.call-start = ((), (), s32[]{:S(2)}) async-start(), calls=%async_computation.19 | async-start | bytes 8912896 | tf_op jit(solution)/shard_map/reduce_scatter | solution.py:267
  719.3 436.1 %reduce-scatter.16.cloned.1.call-start = ((), (), s32[]{:S(2)}) async-start(), calls=%async_computation.20 | async-start | bytes 8912896 | tf_op jit(solution)/shard_map/reduce_scatter | solution.py:273
  727.9 26.7 %all-to-all-start.1 = ((bf16[16,16,2048]{2,1,0:T(8,128)(2,1)}), bf16[16,16,2048]{2,1,0:T(8,128)(2,1)S(1)}, u32[]{:S(2)}, u32[]{:S(2)}) async-start(bf16[16,16,2048]{2,1,0:T(8,128)(2,1)} %bitcast.521), calls=%async_computation.2 | async-start | bytes 2097152 | tf_op jit(solution)/shard_map/all_to_all | solution.py:316
  754.6 86.8 %all-to-all-start.3 = ((bf16[16,16,2048]{2,1,0:T(8,128)(2,1)}), bf16[16,16,2048]{2,1,0:T(8,128)(2,1)S(1)}, u32[]{:S(2)}, u32[]{:S(2)}) async-start(bf16[16,16,2048]{2,1,0:T(8,128)(2,1)} %bitcast.520), calls=%async_computation.5 | async-start | bytes 2097152 | tf_op jit(solution)/shard_map/all_to_all | solution.py:323
  (121 other events, 2260.6 us)
Sparse Core Ops, SparseCore 0:
  49.6 33.4 all-gather.6
  84.6 34.3 all-gather.16
  121.2 37.9 all-gather.10
  161.2 73.2 all-gather.8
  236.5 72.8 all-gather.12
  311.4 72.8 all-gather.14
  626.0 56.1 reduce-scatter.17
  685.1 30.9 reduce-scatter.9
  718.9 31.8 reduce-scatter.11
  754.8 56.3 reduce-scatter.21
  813.4 19.9 all-reduce.26
  837.3 103.8 reduce-scatter.19
  945.3 103.0 reduce-scatter.13
  1052.3 103.0 reduce-scatter.15
where the time goes:
time: 1200 us; the launch traced here: 1190 us
  waiting for transfers between devices  408 us (34%)
  matrix products  244 us (20%)
  local copies, waits for them, and re-layouts  206 us (17%)
  blocking collectives  162 us (14%)
  other arithmetic  132 us (11%)
  between operations  15.9 us (1%)
    reduce_scatter x1, waiting for transfers between devices, body(): lax.psum_scatter(contract_rows(normed_bal, d_gate).astype(jnp.bfloat16),...  84.7 us
    reduce_scatter x1, waiting for transfers between devices, body(): lax.psum_scatter(contract_rows(normed_bal, d_inner).astype(jnp.bfloat16),...  82.5 us
    dot_general x6, matrix products, block_scan(): jnp.einsum('hij,jhp->ihp', weights * scores[None], driven, precision=HIGH...  72 us
    all_gather x1, waiting for transfers between devices, body(): lax.all_gather(w_input, 'dp', axis=0, tiled=True)  71.4 us
    psum x1, blocking collectives, body(): lax.psum((norm_gain_part, local_grads[6], local_grads[7], local_grads[4],...  64.1 us
    unnamed x15, waiting for transfers between devices  49.8 us
    unnamed x205, local copies, waits for them, and re-layouts  34.7 us
    all_gather x1, waiting for transfers between devices, body(): lax.all_gather(w_out, 'dp', axis=0, tiled=True)  33.6 us
  transfers between devices with their start and end apart: 16, of which 10 were waited for; matrix products, arithmetic and copies ran while one was open for 26% of the time, Pallas kernels for 0%

commit v1 on v0

--- a/solution.py
+++ b/solution.py
@@ -1,6 +1,8 @@
 import jax
 import jax.numpy as jnp
 from jax import lax
+from jax.experimental import pallas as pl
+from jax.experimental.pallas import tpu as pltpu
 from jax.sharding import PartitionSpec as P
 
 D = 2048
@@ -26,79 +28,414 @@
     return (segment, row_index - seq_begin)
 
 
-def causal_conv(values, kernel, offset_bias, position):
-    summed = jnp.zeros_like(values) + offset_bias[None, :]
-    for offset in range(KCONV):
-        shifted = jnp.pad(values, ((offset, 0), (0, 0)))[: values.shape[0]]
-        inside = (position >= offset).astype(jnp.float32)[:, None]
-        summed = summed + kernel[offset][None, :] * shifted * inside
-    return summed
-
-
-def block_scan(state_in, operands):
-    inner_act, step_len, decay_step, input_map, output_map, segment, alive_mask = operands
-    row_order = jnp.arange(segment.shape[0], dtype=jnp.int32)
-    cumulative = jnp.cumsum(decay_step, axis=0).T
-    allowed = (segment[:, None] == segment[None, :]) & (row_order[:, None] >= row_order[None, :])
-    spread = cumulative[:, :, None] - cumulative[:, None, :]
-    weights = jnp.where(allowed[None], jnp.exp(jnp.where(allowed[None], spread, 0.0)), 0.0)
-    scores = jnp.dot(output_map, input_map.T, precision=HIGHEST, preferred_element_type=jnp.float32)
-    driven = step_len[:, :, None] * inner_act
-    within = jnp.einsum("hij,jhp->ihp", weights * scores[None], driven, precision=HIGHEST)
-    carried = jnp.einsum("in,hpn->ihp", output_map, state_in, precision=HIGHEST)
-    carried = carried * (jnp.exp(cumulative).T * alive_mask[:, None])[:, :, None]
-    last_sum = cumulative[:, -1]
-    same_last = (segment == segment[-1]).astype(jnp.float32)
-    toward = jnp.exp(last_sum[None, :] - cumulative.T) * same_last[:, None]
-    fresh_state = jnp.einsum("jh,jhp,jn->hpn", toward, driven, input_map, precision=HIGHEST)
-    state_out = state_in * (jnp.exp(last_sum) * alive_mask[-1])[:, None, None] + fresh_state
-    return (state_out, within + carried)
-
-
-def mixer_core(
-    gate_proj,
-    inner_proj,
-    state_proj,
-    step_raw,
-    conv_weight,
-    conv_bias,
-    conv_state_weight,
-    conv_state_bias,
-    step_bias,
-    decay_log,
-    skip_gain,
-    segment,
-    position,
+MIX_ROWS = 256
+LANES = 256
+HEADW = 64
+TILEH = LANES // HEADW
+
+
+def _split3(v):
+    hi = v.astype(jnp.bfloat16)
+    r1 = v - hi.astype(jnp.float32)
+    mid = r1.astype(jnp.bfloat16)
+    lo = (r1 - mid.astype(jnp.float32)).astype(jnp.bfloat16)
+    return jnp.concatenate([hi, mid, lo], axis=1)
+
+
+def _dot(a, b):
+    return lax.dot_general(a, b, (((1,), (0,)), ((), ())), preferred_element_type=jnp.float32)
+
+
+def _dot_t(a, b):
+    return lax.dot_general(a, b, (((1,), (1,)), ((), ())), preferred_element_type=jnp.float32)
+
+
+def _dot_tl(a, b):
+    return lax.dot_general(a, b, (((0,), (0,)), ((), ())), preferred_element_type=jnp.float32)
+
+
+def _conv(v, w, b, pos):
+    out = w[0:1, :] * v + b
+    for k in range(1, KCONV):
+        out = out + jnp.where(pos >= k, pltpu.roll(v, k, 0), 0.0) * w[k : k + 1, :]
+    return out
+
+
+def _iota(shape, axis):
+    return lax.broadcasted_iota(jnp.int32, shape, axis)
+
+
+def _lower():
+    return _iota((MIX_ROWS, MIX_ROWS), 0) >= _iota((MIX_ROWS, MIX_ROWS), 1)
+
+
+def _head_masks():
+    lane = _iota((1, LANES), 1) // HEADW
+    return [(lane == h) for h in range(TILEH)]
+
+
+def _spread_lanes(cols):
+    lane = _iota((1, 2 * HEADW), 1)
+    return jnp.concatenate(
+        [jnp.where(lane < HEADW, cols[2 * i], cols[2 * i + 1]) for i in range(TILEH // 2)], axis=1
+    )
+
+
+def _decay_terms(dt_b, rate, tri):
+    a_b = -dt_b * rate
+    parts = _split3(a_b)
+    c = _dot(tri, parts)
+    cum = c[:, 0:TILEH] + c[:, TILEH : 2 * TILEH] + c[:, 2 * TILEH : 3 * TILEH]
+    ct = lax.dot_general(parts, tri, (((0,), (1,)), ((), ())), preferred_element_type=jnp.float32)
+    cum_t = ct[0:TILEH] + ct[TILEH : 2 * TILEH] + ct[2 * TILEH : 3 * TILEH]
+    cols = [jnp.broadcast_to(cum[:, h : h + 1], (MIX_ROWS, 128)) for h in range(TILEH)]
+    return a_b, cols, cum_t
+
+
+def mixer_fwd_kernel(
+    gate_ref, inner_ref, state_ref, dt_ref, rate_ref, cw_ref, cb_ref, csw_ref, csb_ref, skip_ref,
+    segc_ref, segr_ref, posc_ref,
+    mixed_ref, gated_ref, square_ref,
+    bc_ref, bt_ref, s_ref,
 ):
-    row_count = gate_proj.shape[0]
-    head_count = skip_gain.shape[0]
-    head_width = gate_proj.shape[1] // head_count
-    inner_act = jax.nn.silu(causal_conv(inner_proj, conv_weight, conv_bias, position))
-    state_act = jax.nn.silu(causal_conv(state_proj, conv_state_weight, conv_state_bias, position))
-    input_map = state_act[:, :STATE]
-    output_map = state_act[:, STATE:]
-    step_len = jax.nn.softplus(step_raw + step_bias[None, :])
-    decay_step = -step_len * jnp.exp(decay_log)[None, :]
-    block_count = row_count // SPAN
-    seg_blocks = segment.reshape(block_count, SPAN)
-    previous = jnp.concatenate([jnp.full((1,), -1, jnp.int32), seg_blocks[:-1, -1]])
-    alive_mask = (seg_blocks == previous[:, None]).astype(jnp.float32)
-    start_state = jnp.zeros((head_count, head_width, STATE), jnp.float32)
-    operands = (
-        inner_act.reshape(block_count, SPAN, head_count, head_width),
-        step_len.reshape(block_count, SPAN, head_count),
-        decay_step.reshape(block_count, SPAN, head_count),
-        input_map.reshape(block_count, SPAN, STATE),
-        output_map.reshape(block_count, SPAN, STATE),
-        seg_blocks,
-        alive_mask,
-    )
-    final_state, scanned = lax.scan(jax.checkpoint(block_scan), start_state, operands)
-    mixed_out = (
-        scanned.reshape(row_count, head_count * head_width)
-        + inner_act * jnp.repeat(skip_gain, head_width)[None, :]
-    )
-    return mixed_out * jax.nn.silu(gate_proj)
+    rows = inner_ref.shape[0]
+    blocks = rows // MIX_ROWS
+    pos = posc_ref[...]
+    g = pl.program_id(0)
+
+    @pl.when(g == 0)
+    def _():
+        pre = _conv(state_ref[...], csw_ref[...], csb_ref[...], pos)
+        act = pre * jax.nn.sigmoid(pre)
+        bc_ref[...] = act.astype(jnp.bfloat16)
+        low = _lower()
+        for b in range(blocks):
+            r = slice(b * MIX_ROWS, (b + 1) * MIX_ROWS)
+            bt_ref[:, r] = jnp.transpose(act[r, 0:STATE]).astype(jnp.bfloat16)
+            s = _dot_t(bc_ref[r, STATE : 2 * STATE], bc_ref[r, 0:STATE])
+            ok = (segc_ref[r, :] == segr_ref[:, r]) & low
+            s_ref[b] = jnp.where(ok, s, 0.0)
+        square_ref[...] = jnp.zeros_like(square_ref)
+
+    pre = _conv(inner_ref[...], cw_ref[...], cb_ref[...], pos)
+    x_all = pre * jax.nn.sigmoid(pre)
+    tri = jnp.where(_lower(), 1.0, 0.0).astype(jnp.bfloat16)
+    masks = _head_masks()
+    rate = rate_ref[0]
+    skip = skip_ref[...]
+    state = jnp.zeros((STATE, LANES), jnp.float32)
+    for b in range(blocks):
+        r = slice(b * MIX_ROWS, (b + 1) * MIX_ROWS)
+        dt_b = dt_ref[0, r, :]
+        x = x_all[r]
+        dte = _spread_lanes(
+            [jnp.broadcast_to(dt_b[:, h : h + 1], (MIX_ROWS, 128)) for h in range(TILEH)]
+        )
+        u = dte * x
+        ub = u.astype(jnp.bfloat16)
+        _, cols, cum_t = _decay_terms(dt_b, rate, tri)
+        cume = _spread_lanes(cols)
+        seg = segc_ref[r, :]
+        y = jnp.zeros((MIX_ROWS, LANES), jnp.float32)
+        for h in range(TILEH):
+            wide = jnp.concatenate([cols[h], cols[h]], axis=1)
+            w = jnp.exp(jnp.minimum(wide - cum_t[h : h + 1, :], 0.0)) * s_ref[b]
+            y = y + _dot(w.astype(jnp.bfloat16), jnp.where(masks[h], ub, jnp.zeros_like(ub)))
+        if b > 0:
+            alive = seg == segc_ref[b * MIX_ROWS - 1 : b * MIX_ROWS, :]
+            carried = _dot(bc_ref[r, STATE : 2 * STATE], state.astype(jnp.bfloat16))
+            y = y + carried * jnp.where(alive, jnp.exp(cume), 0.0)
+        if b < blocks - 1:
+            last = cume[MIX_ROWS - 1 : MIX_ROWS, :]
+            seg_last = segc_ref[(b + 1) * MIX_ROWS - 1 : (b + 1) * MIX_ROWS, :]
+            toward = jnp.where(seg == seg_last, jnp.exp(last - cume), 0.0)
+            fresh = _dot(bt_ref[:, r], (toward * u).astype(jnp.bfloat16))
+            if b > 0:
+                keep = seg_last == segc_ref[b * MIX_ROWS - 1 : b * MIX_ROWS, :]
+                state = state * jnp.where(keep, jnp.exp(last), 0.0) + fresh
+            else:
+                state = fresh
+        mixed = y + x * skip
+        gate = gate_ref[r, :]
+        gated = mixed * (gate * jax.nn.sigmoid(gate))
+        mixed_ref[r, :] = mixed
+        gated_ref[r, :] = gated
+        square_ref[r, :] += jnp.sum(gated * gated, axis=1, keepdims=True)
+
+
+def mixer_bwd_kernel(
+    gate_ref, inner_ref, mixed_ref, dnorm_ref, gs_ref, coef_ref, gain_ref,
+    state_ref, dt_ref, sig_ref, rate_ref, cw_ref, cb_ref, csw_ref, csb_ref, skip_ref,
+    segc_ref, segr_ref, posc_ref,
+    dgate_ref, dinner_ref, dstep_ref, dstate_ref, rowsum_ref, headsum_ref, stsum_ref,
+    bc_ref, bt_ref, ct_ref, st_ref, dst_acc, dbc_acc, dpre_ref, keep_ref,
+):
+    rows = inner_ref.shape[0]
+    blocks = rows // MIX_ROWS
+    pos = posc_ref[...]
+    g = pl.program_id(0)
+
+    @pl.when(g == 0)
+    def _():
+        pre = _conv(state_ref[...], csw_ref[...], csb_ref[...], pos)
+        act = pre * jax.nn.sigmoid(pre)
+        bc_ref[...] = act.astype(jnp.bfloat16)
+        up = _iota((MIX_ROWS, MIX_ROWS), 0) <= _iota((MIX_ROWS, MIX_ROWS), 1)
+        for b in range(blocks):
+            r = slice(b * MIX_ROWS, (b + 1) * MIX_ROWS)
+            bt_ref[:, r] = jnp.transpose(act[r, 0:STATE]).astype(jnp.bfloat16)
+            ct_ref[:, r] = jnp.transpose(act[r, STATE : 2 * STATE]).astype(jnp.bfloat16)
+            s = _dot_t(bc_ref[r, 0:STATE], bc_ref[r, STATE : 2 * STATE])
+            ok = (segc_ref[r, :] == segr_ref[:, r]) & up
+            st_ref[b] = jnp.where(ok, s, 0.0)
+        dst_acc[...] = jnp.zeros_like(dst_acc)
+        dbc_acc[...] = jnp.zeros_like(dbc_acc)
+
+    inner = inner_ref[...]
+    pre = _conv(inner, cw_ref[...], cb_ref[...], pos)
+    sg_x = jax.nn.sigmoid(pre)
+    x_all = pre * sg_x
+    tri = jnp.where(_lower(), 1.0, 0.0).astype(jnp.bfloat16)
+    tri_up = jnp.where(
+        _iota((MIX_ROWS, MIX_ROWS), 0) <= _iota((MIX_ROWS, MIX_ROWS), 1), 1.0, 0.0
+    ).astype(jnp.bfloat16)
+    masks = _head_masks()
+    pick = jnp.where(
+        _iota((LANES, TILEH), 0) // HEADW == _iota((LANES, TILEH), 1), 1.0, 0.0
+    ).astype(jnp.bfloat16)
+    rate = rate_ref[0]
+    skip = skip_ref[...]
+    gain = gain_ref[...]
+
+    def per_head(v):
+        hi = v.astype(jnp.bfloat16)
+        lo = (v - hi.astype(jnp.float32)).astype(jnp.bfloat16)
+        return _dot(hi, pick) + _dot(lo, pick)
+
+    def entry_of(b):
+        r = slice(b * MIX_ROWS, (b + 1) * MIX_ROWS)
+        dt_b = dt_ref[0, r, :]
+        dte = _spread_lanes(
+            [jnp.broadcast_to(dt_b[:, h : h + 1], (MIX_ROWS, 128)) for h in range(TILEH)]
+        )
+        a_b, cols, cum_t = _decay_terms(dt_b, rate, tri)
+        cume = _spread_lanes(cols)
+        u = dte * x_all[r]
+        seg = segc_ref[r, :]
+        entry = dict(a=a_b, dte=dte, cols=cols, cum_t=cum_t, ub=u.astype(jnp.bfloat16))
+        prev = segc_ref[b * MIX_ROWS - 1 : b * MIX_ROWS, :] if b > 0 else None
+        if b > 0:
+            entry["e"] = jnp.where(seg == prev, jnp.exp(cume), 0.0)
+        if b < blocks - 1:
+            last = cume[MIX_ROWS - 1 : MIX_ROWS, :]
+            seg_last = segc_ref[(b + 1) * MIX_ROWS - 1 : (b + 1) * MIX_ROWS, :]
+            entry["t"] = jnp.where(seg == seg_last, jnp.exp(last - cume), 0.0)
+            entry["tub"] = (entry["t"] * u).astype(jnp.bfloat16)
+            if b > 0:
+                entry["d"] = jnp.where(seg_last == prev, jnp.exp(last), 0.0)
+        return entry
+
+    terms = []
+    state = None
+    for b in range(blocks):
+        r = slice(b * MIX_ROWS, (b + 1) * MIX_ROWS)
+        entry = entry_of(b)
+        if b > 0:
+            keep_ref[b - 1] = state
+        if b < blocks - 1:
+            fresh = _dot(bt_ref[:, r], entry["tub"])
+            state = state * entry["d"] + fresh if b > 0 else fresh
+        terms.append(entry if blocks <= 4 else None)
+
+    skip_row = jnp.zeros((1, LANES), jnp.float32)
+    gain_row = jnp.zeros((1, LANES), jnp.float32)
+    bias_head = jnp.zeros((1, TILEH), jnp.float32)
+    rate_head = jnp.zeros((1, TILEH), jnp.float32)
+    dst = None
+    for b in reversed(range(blocks)):
+        r = slice(b * MIX_ROWS, (b + 1) * MIX_ROWS)
+        tm = terms[b] or entry_of(b)
+        x = x_all[r]
+        ub = tm["ub"]
+        gate = gate_ref[r, :]
+        sg = jax.nn.sigmoid(gate)
+        silu = gate * sg
+        mixed = mixed_ref[r, :]
+        gated = mixed * silu
+        dn = dnorm_ref[r, :] * gs_ref[r, :]
+        dg = dn * gain - gated * coef_ref[r, :]
+        gain_row = gain_row + jnp.sum(dn * gated, axis=0, keepdims=True)
+        dgate_ref[r, :] = (dg * mixed * (sg + silu * (1.0 - sg))).astype(jnp.bfloat16)
+        dm = dg * silu
+        dyb = dm.astype(jnp.bfloat16)
+        skip_row = skip_row + jnp.sum(dm * x, axis=0, keepdims=True)
+        du = jnp.zeros((MIX_ROWS, LANES), jnp.float32)
+        dst_sum = jnp.zeros((MIX_ROWS, MIX_ROWS), jnp.float32)
+        for h in range(TILEH):
+            wide = jnp.concatenate([tm["cols"][h], tm["cols"][h]], axis=1)
+            lt = jnp.exp(jnp.minimum(tm["cum_t"][h : h + 1, :] - wide, 0.0))
+            wt = (lt * st_ref[b]).astype(jnp.bfloat16)
+            dyh = jnp.where(masks[h], dyb, jnp.zeros_like(dyb))
+            du = du + _dot(wt, dyh)
+            dst_sum = dst_sum + lt * _dot_t(ub, dyh)
+        dst_acc[b] += dst_sum
+        ubf = ub.astype(jnp.float32)
+        tail = None
+        if b < blocks - 1:
+            dstb = dst.astype(jnp.bfloat16)
+            duf = tm["t"] * _dot(bc_ref[r, 0:STATE], dstb)
+            dbc_acc[r, 0:STATE] += _dot_t(tm["tub"], dstb)
+            tail = jnp.sum(ubf * duf, axis=0, keepdims=True)
+            if b > 0:
+                tail = tail + jnp.sum(dst * keep_ref[b - 1], axis=0, keepdims=True) * tm["d"]
+            du = du + duf
+        y = mixed - x * skip
+        z = dyb.astype(jnp.float32) * y - ubf * du
+        if tail is not None:
+            z = z + jnp.where(_iota((MIX_ROWS, 1), 0) == MIX_ROWS - 1, tail, 0.0)
+        if b > 0:
+            edy = (tm["e"] * dm).astype(jnp.bfloat16)
+            dbc_acc[r, STATE : 2 * STATE] += _dot_t(edy, keep_ref[b - 1].astype(jnp.bfloat16))
+            step = _dot(ct_ref[:, r], edy)
+            if b < blocks - 1:
+                dst = dst * tm["d"] + step
+            else:
+                dst = step
+        c = _dot(tri_up, _split3(per_head(z)))
+        da = c[:, 0:TILEH] + c[:, TILEH : 2 * TILEH] + c[:, 2 * TILEH : 3 * TILEH]
+        ddt = per_head(du * x) - da * rate
+        dsr = ddt * sig_ref[0, r, :]
+        dstep_ref[0, r, :] = dsr
+        bias_head = bias_head + jnp.sum(dsr, axis=0, keepdims=True)
+        rate_head = rate_head + jnp.sum(da * tm["a"], axis=0, keepdims=True)
+        s_b = sg_x[r]
+        dpre_ref[r, :] = (tm["dte"] * du + skip * dm) * (s_b + x * (1.0 - s_b))
+
+    def conv_back(dpre, v, w):
+        out = w[0:1, :] * dpre
+        sums = [jnp.sum(dpre * v, axis=0, keepdims=True)]
+        for k in range(1, KCONV):
+            held = jnp.where(pos >= k, dpre, 0.0)
+            out = out + w[k : k + 1, :] * pltpu.roll(held, rows - k, 0)
+            sums.append(jnp.sum(held * pltpu.roll(v, k, 0), axis=0, keepdims=True))
+        sums.append(jnp.sum(dpre, axis=0, keepdims=True))
+        return out, sums
+
+    din, sums = conv_back(dpre_ref[...], inner, cw_ref[...])
+    dinner_ref[...] = din.astype(jnp.bfloat16)
+    rowsum_ref[...] = jnp.concatenate(
+        sums + [gain_row, skip_row, jnp.zeros((1, LANES), jnp.float32)], axis=0
+    )
+    headsum_ref[0] = jnp.concatenate([bias_head, rate_head], axis=0)
+
+    @pl.when(g == pl.num_programs(0) - 1)
+    def _():
+        up = _iota((MIX_ROWS, MIX_ROWS), 0) <= _iota((MIX_ROWS, MIX_ROWS), 1)
+        for b in range(blocks):
+            r = slice(b * MIX_ROWS, (b + 1) * MIX_ROWS)
+            ok = (segc_ref[r, :] == segr_ref[:, r]) & up
+            ds = jnp.where(ok, dst_acc[b], 0.0).astype(jnp.bfloat16)
+            dbc_acc[r, 0:STATE] += _dot(ds, bc_ref[r, STATE : 2 * STATE])
+            dbc_acc[r, STATE : 2 * STATE] += _dot_tl(ds, bc_ref[r, 0:STATE])
+        sp = state_ref[...]
+        pre_s = _conv(sp, csw_ref[...], csb_ref[...], pos)
+        sg_s = jax.nn.sigmoid(pre_s)
+        dpre_s = dbc_acc[...] * (sg_s + pre_s * sg_s * (1.0 - sg_s))
+        dsp, sums_s = conv_back(dpre_s, sp, csw_ref[...])
+        dstate_ref[...] = dsp.astype(jnp.bfloat16)
+        stsum_ref[...] = jnp.concatenate(
+            sums_s + [jnp.zeros((3, 2 * STATE), jnp.float32)], axis=0
+        )
+
+
+def _tile(rows):
+    if rows > 4 * MIX_ROWS:
+        return pl.BlockSpec((rows, LANES), lambda g: (0, g), pipeline_mode=pl.Buffered(1))
+    return pl.BlockSpec((rows, LANES), lambda g: (0, g))
+
+
+def _whole(shape):
+    return pl.BlockSpec(shape, lambda g: (0,) * len(shape))
+
+
+def _heads(rows):
+    return pl.BlockSpec((1, rows, TILEH), lambda g: (g, 0, 0))
+
+
+def mixer_consts(conv_w, conv_b, csw, csb, skip, decay_log, segment, position):
+    f = jnp.float32
+    head_count = skip.shape[0]
+    return dict(
+        rate=jnp.exp(decay_log.astype(f)).reshape(head_count // TILEH, 1, TILEH),
+        cw=conv_w.astype(f), cb=conv_b.astype(f)[None, :], csw=csw.astype(f), csb=csb.astype(f)[None, :],
+        skip=jnp.repeat(skip.astype(f), HEADW)[None, :],
+        segc=segment[:, None], segr=segment[None, :], posc=position[:, None],
+    )
+
+
+def mixer_forward(gate, inner, state, dt, k):
+    rows, width = inner.shape
+    blocks = rows // MIX_ROWS
+    f = jnp.float32
+    wide = jax.ShapeDtypeStruct((rows, width), f)
+    return pl.pallas_call(
+        mixer_fwd_kernel,
+        grid=(width // LANES,),
+        in_specs=[
+            _tile(rows), _tile(rows), _whole((rows, 2 * STATE)), _heads(rows), _heads(1),
+            _tile(KCONV), _tile(1), _whole((KCONV, 2 * STATE)), _whole((1, 2 * STATE)), _tile(1),
+            _whole((rows, 1)), _whole((1, rows)), _whole((rows, 1)),
+        ],
+        out_specs=[_tile(rows), _tile(rows), _whole((rows, 1))],
+        out_shape=[wide, wide, jax.ShapeDtypeStruct((rows, 1), f)],
+        scratch_shapes=[
+            pltpu.VMEM((rows, 2 * STATE), jnp.bfloat16),
+            pltpu.VMEM((STATE, rows), jnp.bfloat16),
+            pltpu.VMEM((blocks, MIX_ROWS, MIX_ROWS), f),
+        ],
+        name="mixer_forward",
+    )(gate, inner, state, dt, k["rate"], k["cw"], k["cb"], k["csw"], k["csb"], k["skip"],
+      k["segc"], k["segr"], k["posc"])
+
+
+def mixer_backward(gate, inner, mixed, dnorm, gs, coef, gain, state, dt, sig, k):
+    rows, width = inner.shape
+    blocks = rows // MIX_ROWS
+    tiles = width // LANES
+    f = jnp.float32
+    wide = jax.ShapeDtypeStruct((rows, width), jnp.bfloat16)
+    return pl.pallas_call(
+        mixer_bwd_kernel,
+        grid=(tiles,),
+        in_specs=[
+            _tile(rows), _tile(rows), _tile(rows), _tile(rows), _whole((rows, 1)), _whole((rows, 1)), _tile(1),
+            _whole((rows, 2 * STATE)), _heads(rows), _heads(rows), _heads(1),
+            _tile(KCONV), _tile(1), _whole((KCONV, 2 * STATE)), _whole((1, 2 * STATE)), _tile(1),
+            _whole((rows, 1)), _whole((1, rows)), _whole((rows, 1)),
+        ],
+        out_specs=[
+            _tile(rows), _tile(rows), _heads(rows), _whole((rows, 2 * STATE)),
+            _tile(8), _heads(2), _whole((8, 2 * STATE)),
+        ],
+        out_shape=[
+            wide, wide, jax.ShapeDtypeStruct((tiles, rows, TILEH), f),
+            jax.ShapeDtypeStruct((rows, 2 * STATE), jnp.bfloat16),
+            jax.ShapeDtypeStruct((8, width), f), jax.ShapeDtypeStruct((tiles, 2, TILEH), f),
+            jax.ShapeDtypeStruct((8, 2 * STATE), f),
+        ],
+        scratch_shapes=[
+            pltpu.VMEM((rows, 2 * STATE), jnp.bfloat16),
+            pltpu.VMEM((STATE, rows), jnp.bfloat16),
+            pltpu.VMEM((STATE, rows), jnp.bfloat16),
+            pltpu.VMEM((blocks, MIX_ROWS, MIX_ROWS), f),
+            pltpu.VMEM((blocks, MIX_ROWS, MIX_ROWS), f),
+            pltpu.VMEM((rows, 2 * STATE), f),
+            pltpu.VMEM((rows, LANES), f),
+            pltpu.VMEM((max(blocks - 1, 1), STATE, LANES), f),
+        ],
+        name="mixer_backward",
+    )(gate, inner, mixed, dnorm, gs, coef, gain, state, dt, sig, k["rate"], k["cw"], k["cb"], k["csw"], k["csb"], k["skip"],
+      k["segc"], k["segr"], k["posc"])
 
 
 def shampoo(weight, gradient, stat_pair, root_pair):
@@ -125,6 +462,22 @@
     return lax.dot_general(
         left_side, right_side, (((1,), (1,)), ((), ())), preferred_element_type=jnp.float32
     )
+
+
+def rank_matrix(keys):
+    count = keys.shape[0]
+    rank = jnp.sum((keys[None, :] < keys[:, None]).astype(jnp.int32), axis=1)
+    return (jnp.arange(count, dtype=jnp.int32)[:, None] == rank[None, :]).astype(jnp.bfloat16)
+
+
+def move_rows(choose, values):
+    return jnp.dot(choose, values, preferred_element_type=jnp.float32).astype(jnp.bfloat16)
+
+
+def move_back(choose, values):
+    return lax.dot_general(
+        choose, values, (((0,), (0,)), ((), ())), preferred_element_type=jnp.float32
+    ).astype(jnp.bfloat16)
 
 
 def body(
@@ -165,17 +518,17 @@
     scale_in = lax.rsqrt(jnp.mean(tokens_f * tokens_f, axis=1) + EPSILON)
     gain_in = norm_gain.astype(jnp.float32)
     normed = (tokens_f * scale_in[:, None] * gain_in[None, :]).astype(jnp.bfloat16)
-    send_order = jnp.argsort(inverse_perm)
+    send_choose = rank_matrix(inverse_perm)
     arrived = (
         lax.all_to_all(
-            normed[send_order].reshape(groups, slot_rows, D),
+            move_rows(send_choose, normed).reshape(groups, slot_rows, D),
             "dp",
             split_axis=0,
             concat_axis=0,
             tiled=True,
         ),
         lax.all_to_all(
-            cotangent[send_order].reshape(groups, slot_rows, D),
+            move_rows(send_choose, cotangent).reshape(groups, slot_rows, D),
             "dp",
             split_axis=0,
             concat_axis=0,
@@ -190,10 +543,9 @@
     row_key = (source % tensor_ranks * groups + source // tensor_ranks) * group_rows + jnp.arange(
         group_rows, dtype=jnp.int32
     )
-    layout = jnp.argsort(row_key)
-    placing = jnp.argsort(layout)
-    normed_bal = collected[0].reshape(group_rows, D)[placing]
-    cot_bal = collected[1].reshape(group_rows, D)[placing]
+    place = rank_matrix(row_key)
+    normed_bal = move_back(place, collected[0].reshape(group_rows, D))
+    cot_bal = move_back(place, collected[1].reshape(group_rows, D))
     segment, position = segment_info(seq_lens[0], group_rows)
     pieces = (
         lax.all_gather(w_gate, "dp", axis=0, tiled=True),
@@ -209,40 +561,16 @@
         )
     )
 
-    def local_piece(
-        gate_v, inner_v, state_v, step_v, conv_w, conv_b, conv_sw, conv_sb, step_b, decay_v, skip_v
-    ):
-        return mixer_core(
-            gate_v,
-            inner_v,
-            state_v,
-            step_v,
-            conv_w,
-            conv_b,
-            conv_sw,
-            conv_sb,
-            step_b,
-            decay_v,
-            skip_v,
-            segment,
-            position,
-        )
-
-    gated_out, local_back = jax.vjp(
-        local_piece,
-        gate_proj,
-        inner_proj,
-        state_proj,
-        step_raw,
-        conv_weight.astype(jnp.float32),
-        conv_bias.astype(jnp.float32),
-        conv_state_weight.astype(jnp.float32),
-        conv_state_bias.astype(jnp.float32),
-        step_bias.astype(jnp.float32),
-        decay_log.astype(jnp.float32),
-        skip_gain.astype(jnp.float32),
-    )
-    whole_square = lax.psum(jnp.sum(gated_out * gated_out, axis=1), "tensor")
+    step_full = step_raw + step_bias.astype(jnp.float32)[None, :]
+    tiles = step_full.shape[1] // TILEH
+    step_tiles = step_full.reshape(group_rows, tiles, TILEH).transpose(1, 0, 2)
+    step_len = jax.nn.softplus(step_tiles)
+    step_slope = jax.nn.sigmoid(step_tiles)
+    consts = mixer_consts(
+        conv_weight, conv_bias, conv_state_weight, conv_state_bias, skip_gain, decay_log, segment, position
+    )
+    mixed, gated_out, square = mixer_forward(gate_proj, inner_proj, state_proj, step_len, consts)
+    whole_square = lax.psum(square[:, 0], "tensor")
     gate_scale = lax.rsqrt(whole_square / INNER + EPSILON)
     gain_gate = gate_gain.astype(jnp.float32)
     normal = (gated_out * gate_scale[:, None] * gain_gate[None, :]).astype(jnp.bfloat16)
@@ -252,17 +580,13 @@
     d_normal = jnp.dot(
         columns, lax.all_gather(w_out, "dp", axis=0, tiled=True), preferred_element_type=jnp.float32
     )
-    gain_gate_part = jnp.sum(d_normal * gated_out * gate_scale[:, None], axis=0)
     dot_total = lax.psum(jnp.sum(gated_out * gain_gate[None, :] * d_normal, axis=1), "tensor")
-    d_gated = (
-        d_normal * gate_scale[:, None] * gain_gate[None, :]
-        - gated_out * (gate_scale**3 * dot_total / INNER)[:, None]
-    )
-    local_grads = local_back(d_gated)
-    d_gate = local_grads[0].astype(jnp.bfloat16)
-    d_inner = local_grads[1].astype(jnp.bfloat16)
-    d_state = local_grads[2].astype(jnp.bfloat16)
-    d_step = local_grads[3].astype(jnp.bfloat16)
+    d_gate, d_inner, d_step, d_state, row_sums, head_sums, state_sums = mixer_backward(
+        gate_proj, inner_proj, mixed, d_normal, gate_scale[:, None],
+        (gate_scale**3 * dot_total / INNER)[:, None], gain_gate[None, :],
+        state_proj, step_len, step_slope, consts,
+    )
+    d_step = d_step.transpose(1, 0, 2).reshape(group_rows, tiles * TILEH).astype(jnp.bfloat16)
     summed_grads = (
         lax.psum_scatter(
             contract_rows(normed_bal, d_gate).astype(jnp.bfloat16),
@@ -306,10 +630,10 @@
     )
     row_totals = (
         lax.psum_scatter(
-            partial_out[layout].astype(jnp.bfloat16), "tensor", scatter_dimension=0, tiled=True
+            move_rows(place, partial_out.astype(jnp.bfloat16)), "tensor", scatter_dimension=0, tiled=True
         ).astype(jnp.float32),
         lax.psum_scatter(
-            column_term[layout].astype(jnp.bfloat16), "tensor", scatter_dimension=0, tiled=True
+            move_rows(place, column_term.astype(jnp.bfloat16)), "tensor", scatter_dimension=0, tiled=True
         ).astype(jnp.float32),
     )
     returning = (
@@ -328,9 +652,8 @@
             tiled=True,
         ),
     )
-    back_order = jnp.argsort(send_order)
-    branch = returning[0].reshape(local_rows, D)[back_order].astype(jnp.float32)
-    d_tokens_normed = returning[1].reshape(local_rows, D)[back_order].astype(jnp.float32)
+    branch = move_back(send_choose, returning[0].reshape(local_rows, D)).astype(jnp.float32)
+    d_tokens_normed = move_back(send_choose, returning[1].reshape(local_rows, D)).astype(jnp.float32)
     block_out = tokens_f + branch
     norm_gain_part = jnp.sum(d_tokens_normed * tokens_f * scale_in[:, None], axis=0)
     dot_in = jnp.sum(tokens_f * gain_in[None, :] * d_tokens_normed, axis=1)
@@ -342,14 +665,14 @@
     over_groups = lax.psum(
         (
             norm_gain_part,
-            local_grads[6],
-            local_grads[7],
-            local_grads[4],
-            local_grads[5],
-            local_grads[8],
-            local_grads[9],
-            local_grads[10],
-            gain_gate_part,
+            state_sums[:KCONV],
+            state_sums[KCONV],
+            row_sums[:KCONV],
+            row_sums[KCONV],
+            head_sums[:, 0].reshape(-1),
+            head_sums[:, 1].reshape(-1),
+            row_sums[KCONV + 2].reshape(-1, HEADW).sum(axis=1),
+            row_sums[KCONV + 1],
         ),
         "dp",
     )

time: 1200 us -> 1020 us (0.85)
  local copies, waits for them, and re-layouts: 206 us -> 54.9 us
  waiting for transfers between devices: 408 us -> 539 us
  matrix products: 244 us -> 143 us
  other arithmetic: 132 us -> 35.8 us
  Pallas kernels: 0 us -> 75.1 us
  blocking collectives: 162 us -> 129 us
    dot_general x28 -> x8, matrix products: 125 us -> 32.7 us  [the longest x4 22.8 us: move_rows(): jnp.dot(choose, values, preferred_element_type=jnp.float32)]
    pallas_call x0 -> x2, Pallas kernels: none -> 75.1 us  [the longest x1 44 us: mixer_backward(): pl.pallas_call(mixer_bwd_kernel, grid=(tiles,), in_specs=[_tile(rows), _t...]
    all_gather x1, waiting for transfers between devices: 0.02 us -> 64.4 us  [body(): lax.all_gather(w_gate, 'dp', axis=0, tiled=True)]
    reshape x7 -> x3, local copies, waits for them, and re-layouts: 50.2 us -> 1.35 us  [the longest x1 0.68 us: mixer_consts(): jnp.exp(decay_log.astype(f)).reshape(head_count // TILEH, 1, TILEH)]
    reduce_sum x10 -> x3, other arithmetic: 39.3 us -> 1.81 us  [the longest x2 1.18 us: rank_matrix(): rank = jnp.sum((keys[None, :] < keys[:, None]).astype(jnp.int32), axis=1)]
    all_gather x1, waiting for transfers between devices: 0.01 us -> 30.9 us  [body(): lax.all_gather(arrived[1], 'tensor', axis=0, tiled=True)]
    all_to_all x2 -> x1, blocking collectives: 61.7 us -> 32.1 us  [body(): lax.all_to_all(move_rows(send_choose, normed).reshape(groups, slot_rows,...]
    gather x8 -> x0, local copies, waits for them, and re-layouts: 28.1 us -> none  [the longest x1 7.11 us: body(): cot_bal = collected[1].reshape(group_rows, D)[placing]]
  transfers between devices with their start and end apart: 16 -> 17, of which waited for: 10 -> 14; matrix products, arithmetic and copies ran while one was open for 26% -> 17% of each run, Pallas kernels for 0% -> 3%
where the time goes in v1:
time: 1020 us; the launch traced here: 1010 us
  waiting for transfers between devices  539 us (53%)
  matrix products  143 us (14%)
  blocking collectives  129 us (13%)
  Pallas kernels  75.1 us (7%)
  local copies, waits for them, and re-layouts  54.9 us (5%)
  other arithmetic  35.8 us (4%)
  starting transfers between devices  17.9 us (2%)
  between operations  15.3 us (2%)
    reduce_scatter x1, waiting for transfers between devices, body(): lax.psum_scatter(contract_rows(normed_bal, d_inner).astype(jnp.bfloat16),...  84 us
    reduce_scatter x1, waiting for transfers between devices, body(): lax.psum_scatter(contract_rows(normed_bal, d_gate).astype(jnp.bfloat16),...  81.9 us
    all_gather x1, waiting for transfers between devices, body(): lax.all_gather(w_input, 'dp', axis=0, tiled=True)  68.7 us
    all_gather x1, waiting for transfers between devices, body(): lax.all_gather(w_gate, 'dp', axis=0, tiled=True)  64.4 us
    psum x1, blocking collectives, body(): lax.psum((norm_gain_part, state_sums[:KCONV], state_sums[KCONV], row_sums...  64.1 us
    unnamed x15, waiting for transfers between devices  55.7 us
    pallas_call x1, Pallas kernels, mixer_backward(): pl.pallas_call(mixer_bwd_kernel, grid=(tiles,), in_specs=[_tile(rows), _t...  44 us
    all_gather x1, waiting for transfers between devices, body(): lax.all_gather(w_out, 'dp', axis=0, tiled=True)  33.1 us
  transfers between devices with their start and end apart: 17, of which 14 were waited for; matrix products, arithmetic and copies ran while one was open for 17% of the time, Pallas kernels for 3%

profile of v1, /device:TPU:0, one launch (start us, length us, event | category | flops | bytes accessed | tf_op | source)
XLA Modules:
  0.0 1010.6 jit_solution(2783970865533469529)
XLA Ops:
  12.8 32.1 %all_to_all.20 = bf16[16,16,2048]{2,1,0:T(8,128)(2,1)} all-to-all(bf16[16,16,2048]{2,1,0:T(8,128)(2,1)S(1)} %bitcast.217), channel_id=1, replica_groups=mesh['dp'=16,'tensor'=2] {'dp'}, dimensions={0} | all-to-all | bytes 2097152 | tf_op jit(solution)/shard_map/all_to_all | solution.py:523
  52.4 22.1 %all-to-all-done.2 = bf16[16,16,2048]{2,1,0:T(8,128)(2,1)S(1)} async-done(((bf16[16,16,2048]{2,1,0:T(8,128)(2,1)}), bf16[16,16,2048]{2,1,0:T(8,128)(2,1)S(1)}, u32[]{:S(2)}, u32[]{:S(2)}) %all-to-all-start.2) | async-done | bytes 1048608 | tf_op jit(solution)/shard_map/all_to_all | solution.py:530
  82.5 23.1 %all_gather.30 = bf16[2048,32]{0,1:T(8,128)(2,1)S(1)} all-gather(bf16[128,32]{0,1:T(8,128)(2,1)S(1)} %copy-done.36), channel_id=1, replica_groups=mesh['dp'=16,'tensor'=2] {'dp'}, dimensions={0}, use_global_device_ids=true | all-gather | bytes 139264 | tf_op jit(solution)/shard_map/all_gather | solution.py:554
  122.1 30.9 %all-gather.17.cloned.1.call-done = bf16[32,16,2048]{2,1,0:T(8,128)(2,1)} async-done(((bf16[16,16,2048]{2,1,0:T(8,128)(2,1)}), bf16[32,16,2048]{2,1,0:T(8,128)(2,1)}) %all-gather.17.cloned.1.call-update) | async-done | bytes 2097168 | tf_op jit(solution)/shard_map/all_gather | solution.py:540
  160.6 68.7 %all-gather.11.cloned.1.call-done = bf16[2048,2048]{1,0:T(8,128)(2,1)} async-done(((bf16[128,2048]{1,0:T(8,128)(2,1)}), bf16[2048,2048]{1,0:T(8,128)(2,1)}) %all-gather.11.cloned.1.call-update) | async-done | bytes 8388624 | tf_op jit(solution)/shard_map/all_gather | solution.py:552
  229.3 10.5 %fusion.92.inner_ref = f32[512,2048]{1,0:T(8,128)} fusion(bf16[512,2048]{1,0:T(8,128)(2,1)} %copy-done.1, bf16[2048,2048]{1,0:T(8,128)(2,1)} %all-gather.11.cloned.1.call-done), kind=kOutput, calls=%fused_computation.165 | convolution fusion | flops 4294967296 | bytes 14680064 | tf_op jit(solution)/shard_map/dot_general | solution.py:559
  239.8 64.4 %all-gather.9.cloned.1.call-done = bf16[2048,2048]{1,0:T(8,128)(2,1)} async-done(((bf16[128,2048]{1,0:T(8,128)(2,1)}), bf16[2048,2048]{1,0:T(8,128)(2,1)}) %all-gather.9.cloned.1.call-update) | async-done | bytes 8388624 | tf_op jit(solution)/shard_map/all_gather | solution.py:551
  304.2 9.6 fusion.91.gate_ref
  313.8 31.2 %mixer_forward.1 = (f32[512,2048]{1,0:T(8,128)}, f32[512,2048]{1,0:T(8,128)}, f32[512,1]{1,0:T(8,128)}) custom-call(f32[512,2048]{1,0:T(8,128)} %fusion.91.gate_ref, f32[512,2048]{1,0:T(8,128)} %fusion.92.inner_ref, f32[512,256]{1,0:T(8,128)} %fusion.93.state_ref, f32[8,512,4]{2,1,0:T(8,128)} %get-tuple-element.217.dt_ref, f32[8,1,4]{2,1,0:T(1,128)} %bitcast.220, ...), custom_call_target="tpu_custom_call" | custom-call | tf_op jit(solution)/shard_map/mixer_forward/pallas_call | solution.py:381
  346.0 33.1 %all-gather.15.cloned.1.call-done = bf16[2048,2048]{1,0:T(8,128)(2,1)} async-done(((bf16[128,2048]{1,0:T(8,128)(2,1)}), bf16[2048,2048]{1,0:T(8,128)(2,1)}) %all-gather.15.cloned.1.call-update) | async-done | bytes 8388624 | tf_op jit(solution)/shard_map/all_gather | solution.py:577
  379.1 11.6 %multiply_reduce_fusion = (f32[512]{0:T(512)S(1)}, f32[512,2048]{1,0:T(8,128)}) fusion(f32[512,2048]{1,0:T(8,128)} %get-tuple-element.38, f32[2048]{0:T(1024)S(1)} %convert_element_type.182, bf16[512,2048]{1,0:T(8,128)(2,1)} %convolution_convert_fusion.4, bf16[2048,2048]{1,0:T(8,128)(2,1)} %all-gather.15.cloned.1.call-done), kind=kOutput, calls=%fused_computation.17 | convolution fusion | flops 4298112512 | bytes 18884608 | tf_op jit(solution)/shard_map/dot_general | solution.py:580
  397.4 44.0 %mixer_backward.1 = (bf16[512,2048]{1,0:T(8,128)(2,1)}, bf16[512,2048]{1,0:T(8,128)(2,1)}, f32[8,512,4]{2,1,0:T(8,128)}, bf16[512,256]{1,0:T(8,128)(2,1)}, f32[8...) custom-call(f32[512,2048]{1,0:T(8,128)} %fusion.91.gate_ref, f32[512,2048]{1,0:T(8,128)} %fusion.92.inner_ref, ...), custom_call_target="tpu_custom_call" | custom-call | tf_op jit(solution)/shard_map/mixer_backward/pallas_call | solution.py:407
  450.5 10.9 %fusion.95 = f32[512,2048]{1,0:T(8,128)} fusion(bf16[512,2048]{1,0:T(8,128)(2,1)} %get-tuple-element.42, bf16[2048,2048]{1,0:T(8,128)(2,1)} %all-gather.11.cloned.1.call-done), kind=kOutput, calls=%fused_computation.168 | convolution fusion | flops 4294967296 | bytes 14680064 | tf_op jit(solution)/shard_map/dot_general | solution.py:462
  476.1 11.6 %convolution_convert_fusion.5 = bf16[512,2048]{1,0:T(8,128)(2,1)} fusion(bf16[2048,2048]{1,0:T(8,128)(2,1)} %all-gather.15.cloned.1.call-done, s32[512]{0:T(512)S(1)} %convert_reduce_fusion, f32[512,2048]{1,0:T(8,128)} %get-tuple-element.38, f32[2048]{0:T(1024)S(1)} %copy-done.28, f32[512]{0:T(512)S(1)} %get-tuple-element.222), kind=kOutput, calls=%fused_computation.23 | convolution fusion | flops 5374214144 | bytes 14692352 | tf_op jit(solution)/shard_map/dot_general | solution.py:474
  489.4 13.4 %reduce-scatter.18.cloned.1.call-done = bf16[128,256]{1,0:T(8,128)(2,1)} async-done(((bf16[2048,256]{1,0:T(8,128)(2,1)}), bf16[128,256]{1,0:T(8,128)(2,1)}) %reduce-scatter.18.cloned.1.call-update) | async-done | bytes 65552 | tf_op jit(solution)/shard_map/reduce_scatter | solution.py:603
  502.9 10.8 %convolution_convert_fusion = bf16[2048,2048]{1,0:T(8,128)(2,1)} fusion(bf16[512,2048]{1,0:T(8,128)(2,1)} %convolution_convert_fusion.4, f32[512,2048]{1,0:T(8,128)} %get-tuple-element.38, f32[2048]{0:T(1024)S(1)} %copy-done.28, f32[512]{0:T(512)S(1)} %get-tuple-element.222), kind=kOutput, calls=%fused_computation | convolution fusion | flops 4302307328 | bytes 14690304 | tf_op jit(solution)/shard_map/dot_general | solution.py:456
  522.6 8.4 convolution_convert_fusion.2
  545.4 26.0 %reduce-scatter.10.cloned.1.call-done = bf16[256,2048]{1,0:T(8,128)(2,1)} async-done(((bf16[512,2048]{1,0:T(8,128)(2,1)}), bf16[256,2048]{1,0:T(8,128)(2,1)}) %reduce-scatter.10.cloned.1.call-update) | async-done | bytes 1048592 | tf_op jit(solution)/shard_map/reduce_scatter | solution.py:632
  578.4 53.3 %reduce-scatter.22.cloned.1.call-done = bf16[128,32]{1,0:T(8,128)(2,1)} async-done(((bf16[2048,32]{1,0:T(8,128)(2,1)}), bf16[128,32]{1,0:T(8,128)(2,1)}) %reduce-scatter.22.cloned.1.call-update) | async-done | bytes 8208
  633.1 20.8 %all-reduce.5.cloned.1.call-done = bf16[128,256]{1,0:T(8,128)(2,1)} async-done(((bf16[128,256]{1,0:T(8,128)(2,1)}), bf16[128,256]{1,0:T(8,128)(2,1)}) %all-reduce.5.cloned.1.call-update) | async-done | bytes 65552 | tf_op jit(solution)/shard_map/psum | solution.py:680
  661.0 64.1 %all-reduce = (bf16[2048]{0:T(1024)(128)(2,1)S(1)}, f32[4,2048]{1,0:T(4,128)}, f32[2048]{0:T(1024)}, bf16[4,256]{1,0:T(4,128)(2,1)S(1)}, bf16[256]{0:T(256)(128)...) all-reduce(f32[2048]{0:T(1024)S(1)} %get-tuple-element.188, ...), channel_id=1, replica_groups=mesh['dp'=16,'tensor'=2] {'dp'}, use_global_device_ids=true, to_apply=%region_13.14 | all-reduce | flops 15712 | bytes 119040 | tf_op jit(solution)/shard_map/psum | solution.py:665
  735.6 26.3 %reduce-scatter.20.cloned.1.call-done = bf16[128,2048]{1,0:T(8,128)(2,1)} async-done(((bf16[2048,2048]{1,0:T(8,128)(2,1)}), bf16[128,2048]{1,0:T(8,128)(2,1)}) %reduce-scatter.20.cloned.1.call-update) | async-done | bytes 524304 | tf_op jit(solution)/shard_map/reduce_scatter | solution.py:615
  785.1 84.0 %reduce-scatter.16.cloned.1.call-done = bf16[128,2048]{1,0:T(8,128)(2,1)} async-done(((bf16[2048,2048]{1,0:T(8,128)(2,1)}), bf16[128,2048]{1,0:T(8,128)(2,1)}) %reduce-scatter.16.cloned.1.call-update) | async-done | bytes 524304 | tf_op jit(solution)/shard_map/reduce_scatter | solution.py:597
  894.3 81.9 %reduce-scatter.14.cloned.1.call-done = bf16[128,2048]{1,0:T(8,128)(2,1)} async-done(((bf16[2048,2048]{1,0:T(8,128)(2,1)}), bf16[128,2048]{1,0:T(8,128)(2,1)}) %reduce-scatter.14.cloned.1.call-update) | async-done | bytes 524304 | tf_op jit(solution)/shard_map/reduce_scatter | solution.py:591
  (267 shorter events, 202.6 us)
Async XLA Ops:
  7.2 99.4 %all-gather.7.cloned.1.call-start = ((), (), s32[]{:S(2)}) async-start(), calls=%async_computation.11 | async-start | bytes 3145728 | tf_op jit(solution)/shard_map/all_gather | solution.py:539
  8.2 36.8 %copy-start.32 = (s32[256]{0:T(256)}, s32[256]{0:T(256)S(1)}, u32[]{:S(2)}) copy-start(s32[256]{0:T(256)S(1)} %convert_reduce_fusion.1) | copy-start | bytes 3076
  46.5 28.1 %all-to-all-start.2 = ((bf16[16,16,2048]{2,1,0:T(8,128)(2,1)}), bf16[16,16,2048]{2,1,0:T(8,128)(2,1)S(1)}, u32[]{:S(2)}, u32[]{:S(2)}) async-start(bf16[16,16,2048]{2,1,0:T(8,128)(2,1)} %bitcast.12), calls=%async_computation.3 | async-start | bytes 2097152 | tf_op jit(solution)/shard_map/all_to_all | solution.py:530
  51.6 53.9 %copy-start.48 = (s32[512]{0:T(512)S(1)}, s32[512]{0:T(512)}, u32[]{:S(2)}) copy-start(s32[512]{0:T(512)} %param.52) | copy-start | bytes 6148
  51.7 67.1 %all-gather.13.cloned.1.call-start = ((), (), s32[]{:S(2)}) async-start(), calls=%async_computation.14 | async-start | bytes 1114112 | tf_op jit(solution)/shard_map/all_gather | solution.py:553
  52.4 100.5 %all-gather.17.cloned.1.call-start = ((), (), s32[]{:S(2)}) async-start(), calls=%async_computation.17 | async-start | bytes 3145728 | tf_op jit(solution)/shard_map/all_gather | solution.py:540
  75.5 153.8 %all-gather.11.cloned.1.call-start = ((), (), s32[]{:S(2)}) async-start(), calls=%async_computation.13 | async-start | bytes 8912896 | tf_op jit(solution)/shard_map/all_gather | solution.py:552
  76.1 228.1 %all-gather.9.cloned.1.call-start = ((), (), s32[]{:S(2)}) async-start(), calls=%async_computation.12 | async-start | bytes 8912896 | tf_op jit(solution)/shard_map/all_gather | solution.py:551
  76.7 302.4 %all-gather.15.cloned.1.call-start = ((), (), s32[]{:S(2)}) async-start(), calls=%async_computation.15 | async-start | bytes 8912896 | tf_op jit(solution)/shard_map/all_gather | solution.py:577
  77.2 425.6 %reduce-scatter.18.cloned.1.call-start = ((), (), s32[]{:S(2)}) async-start(), calls=%async_computation.21 | async-start | bytes 1114112 | tf_op jit(solution)/shard_map/reduce_scatter | solution.py:603
  79.2 299.9 %copy-start.27 = (f32[2048]{0:T(1024)}, f32[2048]{0:T(1024)S(1)}, u32[]{:S(2)}) copy-start(f32[2048]{0:T(1024)S(1)} %convert_element_type.182) | copy-start | bytes 24580
  160.6 143.6 %copy-start.2 = (bf16[512,2048]{1,0:T(8,128)(2,1)S(1)}, bf16[512,2048]{1,0:T(8,128)(2,1)}, u32[]{:S(2)}) copy-start(bf16[512,2048]{1,0:T(8,128)(2,1)} %copy-done.1) | copy-start | bytes 6291460
  446.4 90.3 %reduce-scatter.12.cloned.1.call-start = ((), (), s32[]{:S(2)}) async-start(), calls=%async_computation.18 | async-start | bytes 3145728 | tf_op jit(solution)/shard_map/reduce_scatter | solution.py:635
  475.5 96.0 %reduce-scatter.10.cloned.1.call-start = ((), (), s32[]{:S(2)}) async-start(), calls=%async_computation.16 | async-start | bytes 3145728 | tf_op jit(solution)/shard_map/reduce_scatter | solution.py:632
  487.8 143.9 %reduce-scatter.22.cloned.1.call-start = ((), (), s32[]{:S(2)}) async-start(), calls=%async_computation.24 | async-start | bytes 557056
  489.3 164.5 %all-reduce.5.cloned.1.call-start = ((), (), s32[]{:S(2)}) async-start(), calls=%async_computation.22 | async-start | bytes 131072 | tf_op jit(solution)/shard_map/psum | solution.py:680
  502.8 259.1 %reduce-scatter.20.cloned.1.call-start = ((), (), s32[]{:S(2)}) async-start(), calls=%async_computation.23 | async-start | bytes 8912896 | tf_op jit(solution)/shard_map/reduce_scatter | solution.py:615
  513.7 355.4 %reduce-scatter.16.cloned.1.call-start = ((), (), s32[]{:S(2)}) async-start(), calls=%async_computation.20 | async-start | bytes 8912896 | tf_op jit(solution)/shard_map/reduce_scatter | solution.py:597
  522.1 454.1 %reduce-scatter.14.cloned.1.call-start = ((), (), s32[]{:S(2)}) async-start(), calls=%async_computation.19 | async-start | bytes 8912896 | tf_op jit(solution)/shard_map/reduce_scatter | solution.py:591
  536.6 118.2 %copy-start.21 = (f32[2,4,2,64,64]{4,3,2,1,0:T(8,128)S(1)}, f32[2,4,2,64,64]{4,3,2,1,0:T(8,128)}, u32[]{:S(2)}) copy-start(f32[2,4,2,64,64]{4,3,2,1,0:T(8,128)} %param.49) | copy-start | bytes 786436
  536.6 34.8 %all-to-all-start.3 = ((bf16[16,16,2048]{2,1,0:T(8,128)(2,1)}), bf16[16,16,2048]{2,1,0:T(8,128)(2,1)S(1)}, u32[]{:S(2)}, u32[]{:S(2)}) async-start(bf16[16,16,2048]{2,1,0:T(8,128)(2,1)} %bitcast.215), calls=%async_computation.5 | async-start | bytes 2097152 | tf_op jit(solution)/shard_map/all_to_all | solution.py:647
  571.4 84.3 %copy-start.18 = (bf16[16,16,2048]{2,1,0:T(8,128)(2,1)}, bf16[16,16,2048]{2,1,0:T(8,128)(2,1)S(1)}, u32[]{:S(2)}) copy-start(bf16[16,16,2048]{2,1,0:T(8,128)(2,1)S(1)} %all-to-all-done.3) | copy-start | bytes 3145732
  571.4 160.4 %all-to-all-start.1 = ((bf16[16,16,2048]{2,1,0:T(8,128)(2,1)}), bf16[16,16,2048]{2,1,0:T(8,128)(2,1)S(1)}, u32[]{:S(2)}, u32[]{:S(2)}) async-start(bf16[16,16,2048]{2,1,0:T(8,128)(2,1)} %bitcast.214), calls=%async_computation.2 | async-start | bytes 2097152 | tf_op jit(solution)/shard_map/all_to_all | solution.py:640
  660.0 71.8 %copy-start.35 = (f32[256]{0:T(256)S(1)}, f32[256]{0:T(256)}, u32[]{:S(2)}) copy-start(f32[256]{0:T(256)} %copy-done.34) | copy-start | bytes 3076
  (50 other events, 562.4 us)
Sparse Core Ops, SparseCore 0:
  45.1 33.4 all-gather.6
  80.7 37.9 all-gather.12
  120.8 32.0 all-gather.16
  154.9 74.2 all-gather.10
  231.3 72.8 all-gather.8
  306.2 72.8 all-gather.14
  446.5 56.2 reduce-scatter.17
  505.6 30.9 reduce-scatter.11
  539.4 31.9 reduce-scatter.9
  575.4 56.2 reduce-scatter.21
  633.9 19.9 all-reduce.4
  657.8 104.0 reduce-scatter.19
  766.0 103.1 reduce-scatter.15
  873.1 103.0 reduce-scatter.13

commit v2 on v1

--- a/solution.py
+++ b/solution.py
@@ -101,7 +101,7 @@
     rows = inner_ref.shape[0]
     blocks = rows // MIX_ROWS
     pos = posc_ref[...]
-    g = pl.program_id(0)
+    g = pl.program_id(1)
 
     @pl.when(g == 0)
     def _():
@@ -173,7 +173,7 @@
     rows = inner_ref.shape[0]
     blocks = rows // MIX_ROWS
     pos = posc_ref[...]
-    g = pl.program_id(0)
+    g = pl.program_id(1)
 
     @pl.when(g == 0)
     def _():
@@ -328,7 +328,7 @@
     )
     headsum_ref[0] = jnp.concatenate([bias_head, rate_head], axis=0)
 
-    @pl.when(g == pl.num_programs(0) - 1)
+    @pl.when(g == pl.num_programs(1) - 1)
     def _():
         up = _iota((MIX_ROWS, MIX_ROWS), 0) <= _iota((MIX_ROWS, MIX_ROWS), 1)
         for b in range(blocks):
@@ -348,18 +348,38 @@
         )
 
 
+def _block(shape, index, single=False):
+    if single:
+        return pl.BlockSpec(shape, index, pipeline_mode=pl.Buffered(1))
+    return pl.BlockSpec(shape, index)
+
+
 def _tile(rows):
-    if rows > 4 * MIX_ROWS:
-        return pl.BlockSpec((rows, LANES), lambda g: (0, g), pipeline_mode=pl.Buffered(1))
-    return pl.BlockSpec((rows, LANES), lambda g: (0, g))
-
-
-def _whole(shape):
-    return pl.BlockSpec(shape, lambda g: (0,) * len(shape))
+    return _block((rows, LANES), lambda s, g: (s, g), rows > 4 * MIX_ROWS)
+
+
+def _per_lane(rows):
+    return _block((rows, LANES), lambda s, g: (0, g))
+
+
+def _fixed(shape):
+    return _block(shape, lambda s, g: (0,) * len(shape))
+
+
+def _rows(rows, width):
+    return _block((rows, width), lambda s, g: (s, 0), rows > 4 * MIX_ROWS)
+
+
+def _line(rows):
+    return _block((1, rows), lambda s, g: (0, s))
 
 
 def _heads(rows):
-    return pl.BlockSpec((1, rows, TILEH), lambda g: (g, 0, 0))
+    return _block((1, rows, TILEH), lambda s, g: (g, s, 0), rows > 4 * MIX_ROWS)
+
+
+def _rate():
+    return _block((1, 1, TILEH), lambda s, g: (g, 0, 0))
 
 
 def mixer_consts(conv_w, conv_b, csw, csb, skip, decay_log, segment, position):
@@ -373,55 +393,59 @@
     )
 
 
-def mixer_forward(gate, inner, state, dt, k):
-    rows, width = inner.shape
+def mixer_forward(gate, inner, state, dt, k, rows):
+    total, width = inner.shape
     blocks = rows // MIX_ROWS
     f = jnp.float32
-    wide = jax.ShapeDtypeStruct((rows, width), f)
+    wide = jax.ShapeDtypeStruct((total, width), f)
     return pl.pallas_call(
         mixer_fwd_kernel,
-        grid=(width // LANES,),
+        grid=(total // rows, width // LANES),
         in_specs=[
-            _tile(rows), _tile(rows), _whole((rows, 2 * STATE)), _heads(rows), _heads(1),
-            _tile(KCONV), _tile(1), _whole((KCONV, 2 * STATE)), _whole((1, 2 * STATE)), _tile(1),
-            _whole((rows, 1)), _whole((1, rows)), _whole((rows, 1)),
+            _tile(rows), _tile(rows), _rows(rows, 2 * STATE), _heads(rows), _rate(),
+            _per_lane(KCONV), _per_lane(1), _fixed((KCONV, 2 * STATE)), _fixed((1, 2 * STATE)), _per_lane(1),
+            _rows(rows, 1), _line(rows), _rows(rows, 1),
         ],
-        out_specs=[_tile(rows), _tile(rows), _whole((rows, 1))],
-        out_shape=[wide, wide, jax.ShapeDtypeStruct((rows, 1), f)],
+        out_specs=[_tile(rows), _tile(rows), _rows(rows, 1)],
+        out_shape=[wide, wide, jax.ShapeDtypeStruct((total, 1), f)],
         scratch_shapes=[
             pltpu.VMEM((rows, 2 * STATE), jnp.bfloat16),
             pltpu.VMEM((STATE, rows), jnp.bfloat16),
             pltpu.VMEM((blocks, MIX_ROWS, MIX_ROWS), f),
         ],
+        cost_estimate=pl.CostEstimate(flops=total * width * 3000, bytes_accessed=total * width * 16, transcendentals=total * width * 6),
         name="mixer_forward",
     )(gate, inner, state, dt, k["rate"], k["cw"], k["cb"], k["csw"], k["csb"], k["skip"],
       k["segc"], k["segr"], k["posc"])
 
 
-def mixer_backward(gate, inner, mixed, dnorm, gs, coef, gain, state, dt, sig, k):
-    rows, width = inner.shape
+def mixer_backward(gate, inner, mixed, dnorm, gs, coef, gain, state, dt, sig, k, rows):
+    total, width = inner.shape
     blocks = rows // MIX_ROWS
     tiles = width // LANES
+    spans = total // rows
     f = jnp.float32
-    wide = jax.ShapeDtypeStruct((rows, width), jnp.bfloat16)
+    wide = jax.ShapeDtypeStruct((total, width), jnp.bfloat16)
     return pl.pallas_call(
         mixer_bwd_kernel,
-        grid=(tiles,),
+        grid=(spans, tiles),
         in_specs=[
-            _tile(rows), _tile(rows), _tile(rows), _tile(rows), _whole((rows, 1)), _whole((rows, 1)), _tile(1),
-            _whole((rows, 2 * STATE)), _heads(rows), _heads(rows), _heads(1),
-            _tile(KCONV), _tile(1), _whole((KCONV, 2 * STATE)), _whole((1, 2 * STATE)), _tile(1),
-            _whole((rows, 1)), _whole((1, rows)), _whole((rows, 1)),
+            _tile(rows), _tile(rows), _tile(rows), _tile(rows), _rows(rows, 1), _rows(rows, 1), _per_lane(1),
+            _rows(rows, 2 * STATE), _heads(rows), _heads(rows), _rate(),
+            _per_lane(KCONV), _per_lane(1), _fixed((KCONV, 2 * STATE)), _fixed((1, 2 * STATE)), _per_lane(1),
+            _rows(rows, 1), _line(rows), _rows(rows, 1),
         ],
         out_specs=[
-            _tile(rows), _tile(rows), _heads(rows), _whole((rows, 2 * STATE)),
-            _tile(8), _heads(2), _whole((8, 2 * STATE)),
+            _tile(rows), _tile(rows), _heads(rows), _rows(rows, 2 * STATE),
+            _block((8, LANES), lambda s, g: (s, g)),
+            _block((1, 2, TILEH), lambda s, g: (s * tiles + g, 0, 0)),
+            _block((8, 2 * STATE), lambda s, g: (s, 0)),
         ],
         out_shape=[
-            wide, wide, jax.ShapeDtypeStruct((tiles, rows, TILEH), f),
-            jax.ShapeDtypeStruct((rows, 2 * STATE), jnp.bfloat16),
-            jax.ShapeDtypeStruct((8, width), f), jax.ShapeDtypeStruct((tiles, 2, TILEH), f),
-            jax.ShapeDtypeStruct((8, 2 * STATE), f),
+            wide, wide, jax.ShapeDtypeStruct((tiles, total, TILEH), f),
+            jax.ShapeDtypeStruct((total, 2 * STATE), jnp.bfloat16),
+            jax.ShapeDtypeStruct((spans * 8, width), f), jax.ShapeDtypeStruct((spans * tiles, 2, TILEH), f),
+            jax.ShapeDtypeStruct((spans * 8, 2 * STATE), f),
         ],
         scratch_shapes=[
             pltpu.VMEM((rows, 2 * STATE), jnp.bfloat16),
@@ -433,6 +457,7 @@
             pltpu.VMEM((rows, LANES), f),
             pltpu.VMEM((max(blocks - 1, 1), STATE, LANES), f),
         ],
+        cost_estimate=pl.CostEstimate(flops=total * width * 6000, bytes_accessed=total * width * 20, transcendentals=total * width * 10),
         name="mixer_backward",
     )(gate, inner, mixed, dnorm, gs, coef, gain, state, dt, sig, k["rate"], k["cw"], k["cb"], k["csw"], k["csb"], k["skip"],
       k["segc"], k["segr"], k["posc"])
@@ -464,6 +489,10 @@
     )
 
 
+Z_RING = 4
+CORES = 2
+
+
 def rank_matrix(keys):
     count = keys.shape[0]
     rank = jnp.sum((keys[None, :] < keys[:, None]).astype(jnp.int32), axis=1)
@@ -480,241 +509,275 @@
     ).astype(jnp.bfloat16)
 
 
+def place_on():
+    groups = lax.axis_size("dp")
+    ny = groups // (Z_RING * CORES)
+    me = lax.axis_index("dp")
+    return me // (ny * CORES), (me // CORES) % ny, me % CORES, ny
+
+
+def shift(values, dz=0, dy=0, dc=0):
+    groups = lax.axis_size("dp")
+    ny = groups // (Z_RING * CORES)
+    pairs = []
+    for source in range(groups):
+        z, y, c = source // (ny * CORES), (source // CORES) % ny, source % CORES
+        pairs.append((source, (((z + dz) % Z_RING) * ny + (y + dy) % ny) * CORES + (c + dc) % CORES))
+    return lax.ppermute(values, "dp", pairs)
+
+
+def swap_dp(values, distance):
+    groups = lax.axis_size("dp")
+    return lax.ppermute(values, "dp", [(s, s ^ distance) for s in range(groups)])
+
+
+def swap_tensor(values, distance):
+    ranks = lax.axis_size("tensor")
+    return lax.ppermute(values, "tensor", [(s, s ^ distance) for s in range(ranks)])
+
+
+def sum_tensor(values):
+    distance = 1
+    while distance < lax.axis_size("tensor"):
+        values = values + swap_tensor(values, distance)
+        distance *= 2
+    return values
+
+
+def flip_halves(values, axis):
+    first, second = jnp.split(values, 2, axis=axis)
+    return jnp.concatenate([second, first], axis=axis)
+
+
+def by_core(core, own, other, axis):
+    return jnp.where(
+        core == 0, jnp.concatenate([own, other], axis=axis), jnp.concatenate([other, own], axis=axis)
+    )
+
+
+def half_of(values, which, axis):
+    size = values.shape[axis] // CORES
+    return lax.dynamic_slice_in_dim(values, which * size, size, axis)
+
+
+def gather_weight(weight, name):
+    z, y, core, ny = place_on()
+    with jax.named_scope(name + "_core"):
+        got = shift(half_of(weight, 1 - core, 1), dc=1)
+    piece = by_core(core, half_of(weight, core, 1), got, 0)
+    rows, width = piece.shape
+    full = jnp.zeros((Z_RING * ny * rows, width), weight.dtype)
+
+    def put(full, part, dz, dy):
+        at = ((z - dz) % Z_RING * ny + (y - dy) % ny) * rows
+        return lax.dynamic_update_slice_in_dim(full, part, at, 0)
+
+    for dz in range(Z_RING):
+        full = put(full, piece, dz, 0)
+        for dy in range(1, ny):
+            with jax.named_scope(f"{name}_y{dz}"):
+                across = shift(piece, dy=dy)
+            full = put(full, across, dz, dy)
+        if dz < Z_RING - 1:
+            with jax.named_scope(f"{name}_z{dz}"):
+                piece = shift(piece, dz=1)
+    return full
+
+
+def reduce_weight(partial, name):
+    z, y, core, ny = place_on()
+    rows = partial.shape[0] // (Z_RING * ny)
+    f = jnp.float32
+
+    def part(dz, dy):
+        at = ((z - dz) % Z_RING * ny + (y + dy) % ny) * rows
+        return lax.dynamic_slice_in_dim(partial, at, rows, 0)
+
+    run = None
+    for dz in range(1, Z_RING + 1):
+        own = part(dz, 0).astype(f)
+        for dy in range(1, ny):
+            with jax.named_scope(f"{name}_y{dz}"):
+                own = own + shift(part(dz, dy), dy=dy).astype(f)
+        if run is None:
+            run = own
+        else:
+            with jax.named_scope(f"{name}_z{dz}"):
+                run = shift(run.astype(jnp.bfloat16), dz=1).astype(f) + own
+    with jax.named_scope(name + "_core"):
+        got = shift(half_of(run, 1 - core, 0).astype(jnp.bfloat16), dc=1).astype(f)
+    return by_core(core, half_of(run, core, 0), got, 1)
+
+
 def body(
-    tokens,
-    cotangent,
-    norm_gain,
-    w_gate,
-    w_input,
-    w_state,
-    w_step,
-    conv_weight,
-    conv_bias,
-    conv_state_weight,
-    conv_state_bias,
-    step_bias,
-    decay_log,
-    skip_gain,
-    gate_gain,
-    w_out,
-    stats_gate,
-    stats_input,
-    stats_state,
-    stats_out,
-    roots_gate,
-    roots_input,
-    roots_state,
-    roots_out,
-    seq_lens,
-    balance_perm,
-    inverse_perm,
+    tokens, cotangent, norm_gain, w_gate, w_input, w_state, w_step, conv_weight, conv_bias,
+    conv_state_weight, conv_state_bias, step_bias, decay_log, skip_gain, gate_gain, w_out,
+    stats_gate, stats_input, stats_state, stats_out, roots_gate, roots_input, roots_state, roots_out,
+    seq_lens, balance_perm, inverse_perm,
 ):
+    f = jnp.float32
     groups = lax.axis_size("dp")
     tensor_ranks = lax.axis_size("tensor")
+    z, y, core, ny = place_on()
     local_rows = tokens.shape[0]
     slot_rows = local_rows // groups
     group_rows = local_rows * tensor_ranks
-    tokens_f = tokens.astype(jnp.float32)
+    heads = step_bias.shape[0] // CORES
+    width = w_gate.shape[1] // CORES
+
+    tokens_f = tokens.astype(f)
     scale_in = lax.rsqrt(jnp.mean(tokens_f * tokens_f, axis=1) + EPSILON)
-    gain_in = norm_gain.astype(jnp.float32)
+    gain_in = norm_gain.astype(f)
     normed = (tokens_f * scale_in[:, None] * gain_in[None, :]).astype(jnp.bfloat16)
     send_choose = rank_matrix(inverse_perm)
-    arrived = (
-        lax.all_to_all(
-            move_rows(send_choose, normed).reshape(groups, slot_rows, D),
-            "dp",
-            split_axis=0,
-            concat_axis=0,
-            tiled=True,
-        ),
-        lax.all_to_all(
-            move_rows(send_choose, cotangent).reshape(groups, slot_rows, D),
-            "dp",
-            split_axis=0,
-            concat_axis=0,
-            tiled=True,
-        ),
-    )
-    collected = (
-        lax.all_gather(arrived[0], "tensor", axis=0, tiled=True),
-        lax.all_gather(arrived[1], "tensor", axis=0, tiled=True),
-    )
+
+    gate_w = gather_weight(w_gate, "ag_gate")
+    input_w = gather_weight(w_input, "ag_input")
+    out_w = gather_weight(w_out, "ag_out")
+    state_w = lax.all_gather(w_state, "dp", axis=0, tiled=True)
+    step_w = half_of(lax.all_gather(w_step, "dp", axis=0, tiled=True), core, 1)
+
     source = balance_perm // local_rows
     row_key = (source % tensor_ranks * groups + source // tensor_ranks) * group_rows + jnp.arange(
         group_rows, dtype=jnp.int32
     )
     place = rank_matrix(row_key)
-    normed_bal = move_back(place, collected[0].reshape(group_rows, D))
-    cot_bal = move_back(place, collected[1].reshape(group_rows, D))
-    segment, position = segment_info(seq_lens[0], group_rows)
-    pieces = (
-        lax.all_gather(w_gate, "dp", axis=0, tiled=True),
-        lax.all_gather(w_input, "dp", axis=0, tiled=True),
-        lax.all_gather(w_state, "dp", axis=0, tiled=True),
-        lax.all_gather(w_step, "dp", axis=0, tiled=True),
-    )
-    columns = normed_bal
-    gate_proj, inner_proj, state_proj, step_raw = tuple(
-        (
-            jnp.dot(columns, pieces[member], preferred_element_type=jnp.float32)
-            for member in range(4)
-        )
-    )
-
-    step_full = step_raw + step_bias.astype(jnp.float32)[None, :]
-    tiles = step_full.shape[1] // TILEH
-    step_tiles = step_full.reshape(group_rows, tiles, TILEH).transpose(1, 0, 2)
+
+    def dispatch(values):
+        sent = move_rows(send_choose, values).reshape(groups, slot_rows, D)
+        arrived = lax.all_to_all(sent, "dp", split_axis=0, concat_axis=0, tiled=True).reshape(local_rows, D)
+        if tensor_ranks == 2:
+            rank = lax.axis_index("tensor")
+            got = swap_tensor(arrived, 1)
+            both = by_core(rank, arrived, got, 0)
+        else:
+            both = lax.all_gather(arrived, "tensor", axis=0, tiled=True)
+        own = move_back(place, both)
+        return jnp.concatenate([own, shift(own, dc=1)], axis=0)
+
+    normed_bal = dispatch(normed)
+    cot_bal = dispatch(cotangent)
+
+    lens = jnp.concatenate([seq_lens, shift(seq_lens, dc=1)], axis=0)
+    first = segment_info(lens[0], group_rows)
+    second = segment_info(lens[1], group_rows)
+    segment = jnp.concatenate([first[0], second[0]])
+    position = jnp.concatenate([first[1], second[1]])
+
+    d_normal = jnp.dot(cot_bal, out_w, preferred_element_type=f)
+    gate_proj = jnp.dot(normed_bal, gate_w, preferred_element_type=f)
+    inner_proj = jnp.dot(normed_bal, input_w, preferred_element_type=f)
+    state_proj = jnp.dot(normed_bal, state_w, preferred_element_type=f)
+    step_full = jnp.dot(normed_bal, step_w, preferred_element_type=f)
+    step_full = step_full + half_of(step_bias, core, 0).astype(f)[None, :]
+    tiles = heads // TILEH
+    step_tiles = step_full.reshape(CORES * group_rows, tiles, TILEH).transpose(1, 0, 2)
     step_len = jax.nn.softplus(step_tiles)
     step_slope = jax.nn.sigmoid(step_tiles)
     consts = mixer_consts(
-        conv_weight, conv_bias, conv_state_weight, conv_state_bias, skip_gain, decay_log, segment, position
-    )
-    mixed, gated_out, square = mixer_forward(gate_proj, inner_proj, state_proj, step_len, consts)
-    whole_square = lax.psum(square[:, 0], "tensor")
-    gate_scale = lax.rsqrt(whole_square / INNER + EPSILON)
-    gain_gate = gate_gain.astype(jnp.float32)
+        half_of(conv_weight, core, 1), half_of(conv_bias, core, 0), conv_state_weight, conv_state_bias,
+        half_of(skip_gain, core, 0), half_of(decay_log, core, 0), segment, position,
+    )
+    gain_gate = half_of(gate_gain, core, 0).astype(f)
+    mixed, gated_out, square = mixer_forward(gate_proj, inner_proj, state_proj, step_len, consts, group_rows)
+    inner_dot = jnp.sum(gated_out * gain_gate[None, :] * d_normal, axis=1)
+    row_stats = jnp.stack([square[:, 0], inner_dot])
+    row_stats = row_stats + flip_halves(shift(row_stats, dc=1), 1)
+    row_stats = sum_tensor(row_stats)
+    gate_scale = lax.rsqrt(row_stats[0] / INNER + EPSILON)
+    coef = gate_scale**3 * row_stats[1] / INNER
     normal = (gated_out * gate_scale[:, None] * gain_gate[None, :]).astype(jnp.bfloat16)
-    partial_out = contract_cols(normal, lax.all_gather(w_out, "dp", axis=0, tiled=True))
-    w_out_part = contract_rows(cot_bal, normal)
-    columns = cot_bal
-    d_normal = jnp.dot(
-        columns, lax.all_gather(w_out, "dp", axis=0, tiled=True), preferred_element_type=jnp.float32
-    )
-    dot_total = lax.psum(jnp.sum(gated_out * gain_gate[None, :] * d_normal, axis=1), "tensor")
+
     d_gate, d_inner, d_step, d_state, row_sums, head_sums, state_sums = mixer_backward(
-        gate_proj, inner_proj, mixed, d_normal, gate_scale[:, None],
-        (gate_scale**3 * dot_total / INNER)[:, None], gain_gate[None, :],
-        state_proj, step_len, step_slope, consts,
-    )
-    d_step = d_step.transpose(1, 0, 2).reshape(group_rows, tiles * TILEH).astype(jnp.bfloat16)
-    summed_grads = (
-        lax.psum_scatter(
-            contract_rows(normed_bal, d_gate).astype(jnp.bfloat16),
-            "dp",
-            scatter_dimension=0,
-            tiled=True,
-        ).astype(jnp.float32),
-        lax.psum_scatter(
-            contract_rows(normed_bal, d_inner).astype(jnp.bfloat16),
-            "dp",
-            scatter_dimension=0,
-            tiled=True,
-        ).astype(jnp.float32),
-        lax.psum_scatter(
-            contract_rows(normed_bal, d_state).astype(jnp.bfloat16),
-            "dp",
-            scatter_dimension=0,
-            tiled=True,
-        ).astype(jnp.float32),
-        lax.psum_scatter(
-            contract_rows(normed_bal, d_step).astype(jnp.bfloat16),
-            "dp",
-            scatter_dimension=0,
-            tiled=True,
-        ).astype(jnp.float32),
-        lax.psum_scatter(
-            w_out_part.astype(jnp.bfloat16), "dp", scatter_dimension=0, tiled=True
-        ).astype(jnp.float32),
-    )
-    pieces = (
-        lax.all_gather(w_gate, "dp", axis=0, tiled=True),
-        lax.all_gather(w_input, "dp", axis=0, tiled=True),
-        lax.all_gather(w_state, "dp", axis=0, tiled=True),
-        lax.all_gather(w_step, "dp", axis=0, tiled=True),
-    )
+        gate_proj, inner_proj, mixed, d_normal, gate_scale[:, None], coef[:, None], gain_gate[None, :],
+        state_proj, step_len, step_slope, consts, group_rows,
+    )
+    d_step = d_step.transpose(1, 0, 2).reshape(CORES * group_rows, heads).astype(jnp.bfloat16)
+
+    out_grad = reduce_weight(contract_rows(cot_bal, normal).astype(jnp.bfloat16), "rs_out")
+    gate_grad = reduce_weight(contract_rows(normed_bal, d_gate).astype(jnp.bfloat16), "rs_gate")
+    input_grad = reduce_weight(contract_rows(normed_bal, d_inner).astype(jnp.bfloat16), "rs_input")
+
+    def give_back(partial):
+        own, other = jnp.split(partial, 2, axis=0)
+        own = (own.astype(f) + shift(other, dc=1).astype(f)).astype(jnp.bfloat16)
+        arranged = move_rows(place, own)
+        if tensor_ranks == 2:
+            rank = lax.axis_index("tensor")
+            mine = half_of(arranged, rank, 0).astype(f)
+            total = (mine + swap_tensor(half_of(arranged, 1 - rank, 0), 1).astype(f)).astype(jnp.bfloat16)
+        else:
+            total = lax.psum_scatter(arranged, "tensor", scatter_dimension=0, tiled=True)
+        returned = lax.all_to_all(
+            total.reshape(groups, slot_rows, D), "dp", split_axis=0, concat_axis=0, tiled=True
+        )
+        return move_back(send_choose, returned.reshape(local_rows, D)).astype(f)
+
+    branch = give_back(contract_cols(normal, out_w).astype(jnp.bfloat16))
     column_term = (
-        contract_cols(d_gate, pieces[0])
-        + contract_cols(d_inner, pieces[1])
-        + contract_cols(d_state, pieces[2])
-        + contract_cols(d_step, pieces[3])
-    )
-    row_totals = (
-        lax.psum_scatter(
-            move_rows(place, partial_out.astype(jnp.bfloat16)), "tensor", scatter_dimension=0, tiled=True
-        ).astype(jnp.float32),
-        lax.psum_scatter(
-            move_rows(place, column_term.astype(jnp.bfloat16)), "tensor", scatter_dimension=0, tiled=True
-        ).astype(jnp.float32),
-    )
-    returning = (
-        lax.all_to_all(
-            row_totals[0].astype(jnp.bfloat16).reshape(groups, slot_rows, D),
-            "dp",
-            split_axis=0,
-            concat_axis=0,
-            tiled=True,
-        ),
-        lax.all_to_all(
-            row_totals[1].astype(jnp.bfloat16).reshape(groups, slot_rows, D),
-            "dp",
-            split_axis=0,
-            concat_axis=0,
-            tiled=True,
-        ),
-    )
-    branch = move_back(send_choose, returning[0].reshape(local_rows, D)).astype(jnp.float32)
-    d_tokens_normed = move_back(send_choose, returning[1].reshape(local_rows, D)).astype(jnp.float32)
+        contract_cols(d_gate, gate_w)
+        + contract_cols(d_inner, input_w)
+        + contract_cols(d_state, state_w)
+        + contract_cols(d_step, step_w)
+    )
+    norm_gain_part = jnp.sum(column_term * normed_bal.astype(f), axis=0) / gain_in
+    d_tokens_normed = give_back(column_term.astype(jnp.bfloat16))
+
+    state_part = contract_rows(normed_bal, d_state).astype(jnp.bfloat16)
+    step_part = contract_rows(normed_bal, d_step).astype(jnp.bfloat16)
+    step_part = jnp.where(
+        (jnp.arange(CORES * heads, dtype=jnp.int32) // heads == core)[None, :],
+        jnp.concatenate([step_part] * CORES, axis=1),
+        jnp.zeros((), jnp.bfloat16),
+    )
+    thin = lax.psum_scatter(
+        jnp.concatenate([state_part, step_part], axis=1), "dp", scatter_dimension=0, tiled=True
+    )
+    state_grad = sum_tensor(thin[:, : 2 * STATE].astype(f))
+    step_grad = thin[:, 2 * STATE :].astype(f)
+
+    row_sums = jnp.sum(row_sums.reshape(CORES, 8, width), axis=0)
+    head_sums = jnp.sum(head_sums.reshape(CORES, tiles, 2, TILEH), axis=0).transpose(1, 0, 2).reshape(2, heads)
+    skip_sums = jnp.sum(row_sums[KCONV + 2].reshape(heads, HEADW), axis=1)
+    state_sums = jnp.sum(state_sums.reshape(CORES, 8, 2 * STATE), axis=0)[: KCONV + 1]
+    split_part = jnp.concatenate([row_sums[: KCONV + 2].reshape(-1), head_sums.reshape(-1), skip_sums])
+    shared_part = jnp.concatenate([norm_gain_part, state_sums.reshape(-1)])
+    packed = jnp.concatenate([split_part, shared_part])
+    distance = CORES
+    while distance < groups:
+        packed = packed + swap_dp(packed, distance)
+        distance *= 2
+    partner = shift(packed, dc=1)
+    edge = split_part.shape[0]
+    shared = sum_tensor(packed[edge:] + partner[edge:])
+    lanes = (KCONV + 2) * width
+    wide_sums = by_core(
+        core, packed[:lanes].reshape(KCONV + 2, width), partner[:lanes].reshape(KCONV + 2, width), 1
+    )
+    thin_sums = by_core(
+        core, packed[lanes:edge].reshape(3, heads), partner[lanes:edge].reshape(3, heads), 1
+    )
+    norm_gain_grad = shared[:D]
+    conv_state_grads = shared[D:].reshape(KCONV + 1, 2 * STATE)
+
     block_out = tokens_f + branch
-    norm_gain_part = jnp.sum(d_tokens_normed * tokens_f * scale_in[:, None], axis=0)
     dot_in = jnp.sum(tokens_f * gain_in[None, :] * d_tokens_normed, axis=1)
     tokens_grad = (
-        cotangent.astype(jnp.float32)
+        cotangent.astype(f)
         + d_tokens_normed * scale_in[:, None] * gain_in[None, :]
         - tokens_f * (scale_in**3 * dot_in / D)[:, None]
     )
-    over_groups = lax.psum(
-        (
-            norm_gain_part,
-            state_sums[:KCONV],
-            state_sums[KCONV],
-            row_sums[:KCONV],
-            row_sums[KCONV],
-            head_sums[:, 0].reshape(-1),
-            head_sums[:, 1].reshape(-1),
-            row_sums[KCONV + 2].reshape(-1, HEADW).sum(axis=1),
-            row_sums[KCONV + 1],
-        ),
-        "dp",
-    )
-    over_ranks = (
-        lax.psum(summed_grads[2].astype(jnp.bfloat16), "tensor").astype(jnp.float32),
-        lax.psum(over_groups[0].astype(jnp.bfloat16), "tensor").astype(jnp.float32),
-        lax.psum(over_groups[1].astype(jnp.bfloat16), "tensor").astype(jnp.float32),
-        lax.psum(over_groups[2].astype(jnp.bfloat16), "tensor").astype(jnp.float32),
-    )
-    new_gate = shampoo(w_gate.astype(jnp.float32), summed_grads[0], stats_gate, roots_gate)
-    new_input = shampoo(w_input.astype(jnp.float32), summed_grads[1], stats_input, roots_input)
-    new_state = shampoo(w_state.astype(jnp.float32), over_ranks[0], stats_state, roots_state)
-    new_out = shampoo(w_out.astype(jnp.float32), summed_grads[4], stats_out, roots_out)
+    new_gate = shampoo(w_gate.astype(f), gate_grad, stats_gate, roots_gate)
+    new_input = shampoo(w_input.astype(f), input_grad, stats_input, roots_input)
+    new_state = shampoo(w_state.astype(f), state_grad, stats_state, roots_state)
+    new_out = shampoo(w_out.astype(f), out_grad, stats_out, roots_out)
     return (
-        block_out,
-        tokens_grad,
-        over_ranks[1],
-        summed_grads[0],
-        summed_grads[1],
-        over_ranks[0],
-        summed_grads[3],
-        over_groups[3],
-        over_groups[4],
-        over_ranks[2],
-        over_ranks[3],
-        over_groups[5],
-        over_groups[6],
-        over_groups[7],
-        over_groups[8],
-        summed_grads[4],
-        new_gate[0],
-        new_input[0],
-        new_state[0],
-        new_out[0],
-        new_gate[1],
-        new_input[1],
-        new_state[1],
-        new_out[1],
-        new_gate[2],
-        new_input[2],
-        new_state[2],
-        new_out[2],
+        block_out, tokens_grad, norm_gain_grad, gate_grad, input_grad, state_grad, step_grad,
+        wide_sums[:KCONV], wide_sums[KCONV], conv_state_grads[:KCONV], conv_state_grads[KCONV],
+        thin_sums[0], thin_sums[1], thin_sums[2], wide_sums[KCONV + 1], out_grad,
+        new_gate[0], new_input[0], new_state[0], new_out[0],
+        new_gate[1], new_input[1], new_state[1], new_out[1],
+        new_gate[2], new_input[2], new_state[2], new_out[2],
     )
 
 

time: 1020 us -> 783 us (0.77)
  waiting for transfers between devices: 539 us -> 164 us
  blocking collectives: 129 us -> 24.2 us
  starting transfers between devices: 17.9 us -> 113 us
  local copies, waits for them, and re-layouts: 54.9 us -> 109 us
  matrix products: 143 us -> 197 us
  other arithmetic: 35.8 us -> 73.7 us
    reduce_scatter x6 -> x0, waiting for transfers between devices: 237 us -> none  [the longest x1 84 us: body(): lax.psum_scatter(contract_rows(normed_bal, d_inner).astype(jnp.bfloat16),...]
    all_gather x6 -> x1, waiting for transfers between devices: 204 us -> 0.01 us  [body(): state_w = lax.all_gather(w_state, 'dp', axis=0, tiled=True)]
    ppermute x0 -> x65, waiting for transfers between devices: none -> 122 us  [the longest x55 115 us: shift(): return lax.ppermute(values, 'dp', pairs)]
    ppermute x0 -> x65, starting transfers between devices: none -> 90.2 us  [the longest x55 76.5 us: shift(): return lax.ppermute(values, 'dp', pairs)]
    psum x3 -> x0, blocking collectives: 73.9 us -> none  [the longest x1 64.1 us: body(): lax.psum((norm_gain_part, state_sums[:KCONV], state_sums[KCONV], row_sums...]
    all_to_all x1 -> x0, blocking collectives: 32.1 us -> none  [body(): lax.all_to_all(move_rows(send_choose, normed).reshape(groups, slot_rows,...]
    unnamed x15 -> x3, waiting for transfers between devices: 55.7 us -> 24 us
    dynamic_update_slice x0 -> x21, local copies, waits for them, and re-layouts: none -> 24.8 us  [put(): return lax.dynamic_update_slice_in_dim(full, part, at, 0)]
  transfers between devices with their start and end apart: 17 -> 71, of which waited for: 14 -> 24; matrix products, arithmetic and copies ran while one was open for 17% -> 39% of each run, Pallas kernels for 3% -> 4%
where the time goes in v2:
time: 783 us; the launch traced here: 774 us
  matrix products  197 us (25%)
  waiting for transfers between devices  164 us (21%)
  starting transfers between devices  113 us (14%)
  local copies, waits for them, and re-layouts  109 us (14%)
  Pallas kernels  78 us (10%)
  other arithmetic  73.7 us (9%)
  blocking collectives  24.2 us (3%)
  between operations  16 us (2%)
    ppermute x55, waiting for transfers between devices, shift(): return lax.ppermute(values, 'dp', pairs)  115 us
    ppermute x55, starting transfers between devices, shift(): return lax.ppermute(values, 'dp', pairs)  76.5 us
    pallas_call x1, Pallas kernels, mixer_backward(): pl.pallas_call(mixer_bwd_kernel, grid=(spans, tiles), in_specs=[_tile(row...  45.7 us
    dot_general x5, matrix products, contract_cols(): lax.dot_general(left_side, right_side, (((1,), (1,)), ((), ())), preferre...  43.3 us
    pallas_call x1, Pallas kernels, mixer_forward(): pl.pallas_call(mixer_fwd_kernel, grid=(total // rows, width // LANES), in...  32.3 us
    dot_general x5, matrix products, contract_rows(): lax.dot_general(left_side, right_side, (((0,), (0,)), ((), ())), preferre...  27.2 us
    unnamed x173, local copies, waits for them, and re-layouts  26.2 us
    dynamic_update_slice x21, local copies, waits for them, and re-layouts, put(): return lax.dynamic_update_slice_in_dim(full, part, at, 0)  24.8 us
  transfers between devices with their start and end apart: 71, of which 24 were waited for; matrix products, arithmetic and copies ran while one was open for 39% of the time, Pallas kernels for 4%

profile of v2, /device:TPU:0, one launch (start us, length us, event | category | flops | bytes accessed | tf_op | source)
XLA Modules:
  0.0 774.5 jit_solution(1706609110582611071)
XLA Ops:
  17.6 7.3 all-to-all-start
  35.5 24.2 %all_gather.7 = bf16[2048,32]{0,1:T(8,128)(2,1)S(1)} all-gather(bf16[128,32]{0,1:T(8,128)(2,1)S(1)} %copy-done.62), channel_id=1, replica_groups=mesh['dp'=16,'tensor'=2] {'dp'}, dimensions={0}, use_global_device_ids=true | all-gather | bytes 139264 | tf_op jit(solution)/shard_map/all_gather | solution.py:638
  98.1 11.3 %collective-permute-done.11 = bf16[256,1024]{1,0:T(8,128)(2,1)S(1)} collective-permute-done((bf16[256,1024]{1,0:T(8,128)(2,1)}, bf16[256,1024]{1,0:T(8,128)(2,1)S(1)}, u32[]{:S(2)}, u32[]{:S(2)}) %collective-permute-start.11) | collective-permute-done | bytes 524320 | tf_op jit(solution)/shard_map/ag_input_y0/ppermute | solution.py:526
  115.3 8.4 %collective-permute-done.12 = bf16[256,1024]{1,0:T(8,128)(2,1)S(1)} collective-permute-done((bf16[256,1024]{1,0:T(8,128)(2,1)}, bf16[256,1024]{1,0:T(8,128)(2,1)S(1)}, u32[]{:S(2)}, u32[]{:S(2)}) %collective-permute-start.12) | collective-permute-done | bytes 524320 | tf_op jit(solution)/shard_map/ag_input_z0/ppermute | solution.py:526
  148.9 8.6 %collective-permute-done.14 = bf16[256,1024]{1,0:T(8,128)(2,1)} collective-permute-done((bf16[256,1024]{1,0:T(8,128)(2,1)S(1)}, bf16[256,1024]{1,0:T(8,128)(2,1)}, u32[]{:S(2)}, u32[]{:S(2)}) %collective-permute-start.14) | collective-permute-done | bytes 524320 | tf_op jit(solution)/shard_map/ag_input_z1/ppermute | solution.py:526
  177.2 15.5 %all-to-all-done.1 = bf16[16,16,2048]{2,1,0:T(8,128)(2,1)} async-done(((bf16[16,16,2048]{2,1,0:T(8,128)(2,1)}), bf16[16,16,2048]{2,1,0:T(8,128)(2,1)}, u32[]{:S(2)}, u32[]{:S(2)}) %all-to-all-start.1) | async-done | bytes 1048608 | tf_op jit(solution)/shard_map/all_to_all | solution.py:648
  211.8 10.4 %collective-permute-done.9 = bf16[256,1024]{1,0:T(8,128)(2,1)S(1)} collective-permute-done((bf16[256,1024]{1,0:T(8,128)(2,1)S(1)}, bf16[256,1024]{1,0:T(8,128)(2,1)S(1)}, u32[]{:S(2)}, u32[]{:S(2)}) %collective-permute-start.9) | collective-permute-done | bytes 524320 | tf_op jit(solution)/shard_map/ag_gate_y3/ppermute | solution.py:526
  223.1 9.5 %collective-permute-done.17 = bf16[256,1024]{1,0:T(8,128)(2,1)S(1)} collective-permute-done((bf16[256,1024]{1,0:T(8,128)(2,1)}, bf16[256,1024]{1,0:T(8,128)(2,1)S(1)}, u32[]{:S(2)}, u32[]{:S(2)}) %collective-permute-start.17) | collective-permute-done | bytes 524320 | tf_op jit(solution)/shard_map/ag_input_y3/ppermute | solution.py:526
  249.5 9.3 %fusion.148.gate_ref = f32[1024,1024]{1,0:T(8,128)} fusion(bf16[2048,1024]{1,0:T(8,128)(2,1)} %constant_dynamic-update-slice_fusion.16, bf16[512,2048]{1,0:T(8,128)(2,1)} %collective-permute-done.1, bf16[512,2048]{1,0:T(8,128)(2,1)S(1)} %copy-done.40), kind=kOutput, calls=%fused_computation.311 | convolution fusion | flops 4303355904 | bytes 12582912 | tf_op jit(solution)/shard_map/dot_general | solution.py:668
  258.8 9.3 %fusion.147.inner_ref = f32[1024,1024]{1,0:T(8,128)} fusion(bf16[2048,1024]{1,0:T(8,128)(2,1)} %constant_dynamic-update-slice_fusion.8, bf16[512,2048]{1,0:T(8,128)(2,1)} %collective-permute-done.1, bf16[512,2048]{1,0:T(8,128)(2,1)S(1)} %copy-done.40), kind=kOutput, calls=%fused_computation.310 | convolution fusion | flops 4303355904 | bytes 12582912 | tf_op jit(solution)/shard_map/dot_general | solution.py:669
  268.1 32.3 %mixer_forward.1 = (f32[1024,1024]{1,0:T(8,128)}, f32[1024,1024]{1,0:T(8,128)}, f32[1024,1]{1,0:T(8,128)}) custom-call(f32[1024,1024]{1,0:T(8,128)} %fusion.148.gate_ref, f32[1024,1024]{1,0:T(8,128)} %fusion.147.inner_ref, f32[1024,256]{1,0:T(8,128)} %fusion.146.state_ref, f32[4,1024,4]{2,1,0:T(8,128)} %get-tuple-element.223.dt_ref, f32[4,1,4]{2,1,0:T(1,128)} %bitcast.260, ...), custom_call_target="tpu_custom_call" | custom-call | flops 3145728000 | bytes 16777216 | tf_op jit(solution)/shard_map/mixer_forward/pallas_call | solution.py:401
  301.7 11.2 %multiply_reduce_fusion.1 = (f32[1024]{0:T(1024)S(1)}, f32[1024,1024]{1,0:T(8,128)}) fusion(f32[1024,1024]{1,0:T(8,128)} %get-tuple-element.38, f32[1024]{0:T(1024)S(1)} %dynamic-slice_convert_fusion.3, bf16[2048,1024]{1,0:T(8,128)(2,1)} %constant_dynamic-update-slice_fusion, bf16[512,2048]{1,0:T(8,128)(2,1)} %collective-permute-done.20, ...), kind=kOutput, calls=%fused_computation.14 | convolution fusion | flops 4306500608 | bytes 16785408 | tf_op jit(solution)/shard_map/dot_general | solution.py:667
  318.1 8.0 %convolution_convert_fusion.3 = bf16[1024,2048]{1,0:T(8,128)(2,1)S(1)} fusion(bf16[2048,1024]{1,0:T(8,128)(2,1)} %constant_dynamic-update-slice_fusion, f32[1024,1024]{1,0:T(8,128)} %get-tuple-element.38, f32[1024]{0:T(1024)S(1)} %bitcast.262, f32[1024]{0:T(1024)S(1)} %dynamic-slice_convert_fusion.3), kind=kOutput, calls=%fused_computation.23 | convolution fusion | flops 4300210176 | bytes 12591104 | tf_op jit(solution)/shard_map/dot_general | solution.py:487
  331.6 45.7 %mixer_backward.1 = (bf16[1024,1024]{1,0:T(8,128)(2,1)}, bf16[1024,1024]{1,0:T(8,128)(2,1)}, f32[4,1024,4]{2,1,0:T(8,128)}, bf16[1024,256]{1,0:T(8,128)(2,1)}, f...) custom-call(f32[1024,1024]{1,0:T(8,128)} %fusion.148.gate_ref, f32[1024,1024]{1,0:T(8,128)} %fusion.147.inner_ref, ...), custom_call_target="tpu_custom_call" | custom-call | flops 6291456000 | bytes 20971520 | tf_op jit(solution)/shard_map/mixer_backward/pallas_call | solution.py:429
  384.1 9.0 %fusion.156 = f32[1024,2048]{1,0:T(8,128)} fusion(bf16[1024,1024]{1,0:T(8,128)(2,1)S(1)} %copy-done.74, bf16[2048,1024]{1,0:T(8,128)(2,1)} %constant_dynamic-update-slice_fusion.8), kind=kOutput, calls=%fused_computation.318 | convolution fusion | flops 4294967296 | bytes 14680064 | tf_op jit(solution)/shard_map/dot_general | solution.py:487
  399.5 15.7 %multiply_reduce_fusion = (f32[2048]{0:T(1024)S(1)}, bf16[1024,2048]{1,0:T(8,128)(2,1)}) fusion(bf16[512,2048]{1,0:T(8,128)(2,1)} %collective-permute-done.1, bf16[512,2048]{1,0:T(8,128)(2,1)S(1)} %copy-done.41, f32[1024,2048]{1,0:T(8,128)} %fusion.123, f32[1024,2048]{1,0:T(8,128)} %fusion.157, f32[1024,2048]{1,0:T(8,128)} %fusion.156, ...), kind=kOutput, calls=%fused_computation | convolution fusion | flops 4315936768 | bytes 39854080 | tf_op jit(solution)/shard_map/dot_general | solution.py:487
  417.0 7.4 convolution_convert_fusion.2
  494.6 11.1 %collective-permute-done.49 = bf16[256,1024]{0,1:T(8,128)(2,1)S(1)} collective-permute-done((bf16[256,1024]{0,1:T(8,128)(2,1)}, bf16[256,1024]{0,1:T(8,128)(2,1)S(1)}, u32[]{:S(2)}, u32[]{:S(2)}) %collective-permute-start.49) | collective-permute-done | bytes 524320 | tf_op jit(solution)/shard_map/rs_input_z2/ppermute | solution.py:526
  509.6 9.8 %collective-permute-done.58 = bf16[256,1024]{0,1:T(8,128)(2,1)S(1)} collective-permute-done((bf16[256,1024]{0,1:T(8,128)(2,1)S(1)}, bf16[256,1024]{0,1:T(8,128)(2,1)S(1)}, u32[]{:S(2)}, u32[]{:S(2)}) %collective-permute-start.58) | collective-permute-done | bytes 524320 | tf_op jit(solution)/shard_map/rs_out_z2/ppermute | solution.py:526
  523.2 7.4 collective-permute-done.43
  543.9 24.0 %reduce-scatter.4.cloned.1.call-done = bf16[128,288]{1,0:T(8,128)(2,1)} async-done(((bf16[2048,288]{1,0:T(8,128)(2,1)}), bf16[128,288]{1,0:T(8,128)(2,1)}) %reduce-scatter.4.cloned.1.call-update) | async-done | bytes 73744
  604.5 7.7 collective-permute-done.53
  643.2 7.8 %fusion.75 = f32[2,32,1,64,64]{4,3,1,0,2:T(8,128)} fusion(f32[2,64,32,64]{1,0,3,2:T(2,128)} %copy-done.1), kind=kOutput, calls=%fused_computation.118 | convolution fusion | flops 201326592 | bytes 2097152 | tf_op jit(solution)/shard_map/abij,abkj->abik/dot_general | solution.py:469
  665.5 7.1 fusion.81
  (508 shorter events, 440.5 us)
Async XLA Ops:
  9.1 50.7 %collective-permute-start.21 = (bf16[128,1024]{1,0:T(8,128)(2,1)}, bf16[128,1024]{1,0:T(8,128)(2,1)}, u32[]{:S(2)}, u32[]{:S(2)}) collective-permute-start(bf16[128,1024]{1,0:T(8,128)(2,1)} %get-tuple-element.228), channel_id=1, source_target_pairs={{0,2},{2,0},{4,6},{6,4},{8,10},{10,8},{12,14},{14,12},{16,18},{18,... | collective-permute-start | bytes 786440 | tf_op jit(solution)/shard_map/ag_out_core/ppermute | solution.py:526
  11.5 58.8 %collective-permute-start.2 = (bf16[128,1024]{1,0:T(8,128)(2,1)}, bf16[128,1024]{1,0:T(8,128)(2,1)}, u32[]{:S(2)}, u32[]{:S(2)}) collective-permute-start(bf16[128,1024]{1,0:T(8,128)(2,1)} %get-tuple-element.226), channel_id=1, source_target_pairs={{0,2},{2,0},{4,6},{6,4},{8,10},{10,8},{12,14},{14,12},{16,18},{18,... | collective-permute-start | bytes 786440 | tf_op jit(solution)/shard_map/ag_gate_core/ppermute | solution.py:526
  17.6 65.8 %all-to-all-start = ((bf16[16,16,2048]{2,1,0:T(8,128)(2,1)}), bf16[16,16,2048]{2,1,0:T(8,128)(2,1)S(1)}, u32[]{:S(2)}, u32[]{:S(2)}) async-start(bf16[16,16,2048]{2,1,0:T(8,128)(2,1)} %bitcast.250), calls=%async_computation | async-start | bytes 2097152 | tf_op jit(solution)/shard_map/all_to_all | solution.py:648
  24.9 219.7 %all-gather.2.cloned.1.call-start = ((), (), s32[]{:S(2)}) async-start(), calls=%async_computation.5 | async-start | bytes 1114112 | tf_op jit(solution)/shard_map/all_gather | solution.py:637
  25.7 52.1 %collective-permute-start.10 = (bf16[128,1024]{1,0:T(8,128)(2,1)}, bf16[128,1024]{1,0:T(8,128)(2,1)}, u32[]{:S(2)}, u32[]{:S(2)}) collective-permute-start(bf16[128,1024]{1,0:T(8,128)(2,1)} %get-tuple-element.224), channel_id=1, source_target_pairs={{0,2},{2,0},{4,6},{6,4},{8,10},{10,8},{12,14},{14,12},{16,18},{18,... | collective-permute-start | bytes 786440 | tf_op jit(solution)/shard_map/ag_input_core/ppermute | solution.py:526
  83.4 109.3 %all-to-all-start.1 = ((bf16[16,16,2048]{2,1,0:T(8,128)(2,1)}), bf16[16,16,2048]{2,1,0:T(8,128)(2,1)}, u32[]{:S(2)}, u32[]{:S(2)}) async-start(bf16[16,16,2048]{2,1,0:T(8,128)(2,1)} %bitcast.11), calls=%async_computation.1 | async-start | bytes 2097152 | tf_op jit(solution)/shard_map/all_to_all | solution.py:648
  87.9 480.0 %reduce-scatter.4.cloned.1.call-start = ((), (), s32[]{:S(2)}) async-start(), calls=%async_computation.6 | async-start | bytes 1671168
  88.0 53.9 %collective-permute-start = (bf16[256,2048]{1,0:T(8,128)(2,1)S(1)}, bf16[256,2048]{1,0:T(8,128)(2,1)}, u32[]{:S(2)}, u32[]{:S(2)}) collective-permute-start(bf16[256,2048]{1,0:T(8,128)(2,1)S(1)} %bitcast.248), channel_id=1, source_target_pairs={{0,1},{1,0},{2,3},{3,2},{4,5},{5,4},{6,7},{7,6},{8,9},{9,8},{10,11... | collective-permute-start | bytes 3145736 | tf_op jit(solution)/shard_map/ppermute | solution.py:536
  148.1 89.7 %collective-permute-start.1 = (bf16[512,2048]{1,0:T(8,128)(2,1)S(1)}, bf16[512,2048]{1,0:T(8,128)(2,1)}, u32[]{:S(2)}, u32[]{:S(2)}) collective-permute-start(bf16[512,2048]{1,0:T(8,128)(2,1)S(1)} %convolution_convert_fusion.7), channel_id=1, source_target_pairs={{0,2},{2,0},{4,6},{6,4},{8,10},{10,8},{12,14},{14,12},{16,18},{18,... | collective-permute-start | bytes 6291464 | tf_op jit(solution)/shard_map/ppermute | solution.py:526
  192.7 40.8 %collective-permute-start.19 = (bf16[256,2048]{1,0:T(8,128)(2,1)}, bf16[256,2048]{1,0:T(8,128)(2,1)S(1)}, u32[]{:S(2)}, u32[]{:S(2)}) collective-permute-start(bf16[256,2048]{1,0:T(8,128)(2,1)} %bitcast.12), channel_id=1, source_target_pairs={{0,1},{1,0},{2,3},{3,2},{4,5},{5,4},{6,7},{7,6},{8,9},{9,8},{10,11... | collective-permute-start | bytes 3145736 | tf_op jit(solution)/shard_map/ppermute | solution.py:536
  237.8 64.0 %collective-permute-start.20 = (bf16[512,2048]{1,0:T(8,128)(2,1)}, bf16[512,2048]{1,0:T(8,128)(2,1)}, u32[]{:S(2)}, u32[]{:S(2)}) collective-permute-start(bf16[512,2048]{1,0:T(8,128)(2,1)} %convolution_convert_fusion.6), channel_id=1, source_target_pairs={{0,2},{2,0},{4,6},{6,4},{8,10},{10,8},{12,14},{14,12},{16,18},{18,... | collective-permute-start | bytes 6291464 | tf_op jit(solution)/shard_map/ppermute | solution.py:526
  415.2 40.4 %collective-permute-start.35 = (f32[9520]{0:T(1024)S(1)}, f32[9520]{0:T(1024)S(1)}, u32[]{:S(2)}, u32[]{:S(2)}) collective-permute-start(f32[9520]{0:T(1024)S(1)} %concatenate.99), channel_id=1, source_target_pairs={{0,4},{2,6},{4,0},{6,2},{8,12},{10,14},{12,8},{14,10},{16,20},{18,... | collective-permute-start | bytes 114248 | tf_op jit(solution)/shard_map/ppermute | solution.py:531
  425.9 59.4 %collective-permute-start.42 = (bf16[256,1024]{0,1:T(8,128)(2,1)}, bf16[256,1024]{0,1:T(8,128)(2,1)}, u32[]{:S(2)}, u32[]{:S(2)}) collective-permute-start(bf16[256,1024]{0,1:T(8,128)(2,1)} %get-tuple-element.221), channel_id=1, source_target_pairs={{0,4},{2,6},{4,0},{6,2},{8,12},{10,14},{12,8},{14,10},{16,20},{18,... | collective-permute-start | bytes 1572872 | tf_op jit(solution)/shard_map/rs_gate_y2/ppermute | solution.py:526
  427.6 42.8 %collective-permute-start.40 = (bf16[256,1024]{0,1:T(8,128)(2,1)}, bf16[256,1024]{0,1:T(8,128)(2,1)}, u32[]{:S(2)}, u32[]{:S(2)}) collective-permute-start(bf16[256,1024]{0,1:T(8,128)(2,1)} %get-tuple-element.218), channel_id=1, source_target_pairs={{0,4},{2,6},{4,0},{6,2},{8,12},{10,14},{12,8},{14,10},{16,20},{18,... | collective-permute-start | bytes 1572872 | tf_op jit(solution)/shard_map/rs_gate_y1/ppermute | solution.py:526
  437.4 57.1 %collective-permute-start.50 = (bf16[256,1024]{0,1:T(8,128)(2,1)}, bf16[256,1024]{0,1:T(8,128)(2,1)}, u32[]{:S(2)}, u32[]{:S(2)}) collective-permute-start(bf16[256,1024]{0,1:T(8,128)(2,1)} %get-tuple-element.217), channel_id=1, source_target_pairs={{0,4},{2,6},{4,0},{6,2},{8,12},{10,14},{12,8},{14,10},{16,20},{18,... | collective-permute-start | bytes 1572872 | tf_op jit(solution)/shard_map/rs_input_y2/ppermute | solution.py:526
  483.9 100.2 %collective-permute-start.31 = (bf16[512,2048]{1,0:T(8,128)(2,1)S(1)}, bf16[512,2048]{1,0:T(8,128)(2,1)}, u32[]{:S(2)}, u32[]{:S(2)}) collective-permute-start(bf16[512,2048]{1,0:T(8,128)(2,1)S(1)} %split.27), channel_id=1, source_target_pairs={{0,2},{2,0},{4,6},{6,4},{8,10},{10,8},{12,14},{14,12},{16,18},{18,... | collective-permute-start | bytes 6291464 | tf_op jit(solution)/shard_map/ppermute | solution.py:526
  523.1 45.7 %collective-permute-start.61 = (bf16[256,1024]{0,1:T(8,128)(2,1)}, bf16[256,1024]{0,1:T(8,128)(2,1)S(1)}, u32[]{:S(2)}, u32[]{:S(2)}) collective-permute-start(bf16[256,1024]{0,1:T(8,128)(2,1)} %get-tuple-element.212), channel_id=1, source_target_pairs={{0,4},{2,6},{4,0},{6,2},{8,12},{10,14},{12,8},{14,10},{16,20},{18,... | collective-permute-start | bytes 1572872 | tf_op jit(solution)/shard_map/rs_out_y3/ppermute | solution.py:526
  530.6 39.6 %collective-permute-start.60 = (bf16[256,1024]{0,1:T(8,128)(2,1)S(1)}, bf16[256,1024]{0,1:T(8,128)(2,1)}, u32[]{:S(2)}, u32[]{:S(2)}) collective-permute-start(bf16[256,1024]{0,1:T(8,128)(2,1)S(1)} %add_convert_fusion.7), channel_id=1, source_target_pairs={{0,8},{2,10},{4,12},{6,14},{8,16},{10,18},{12,20},{14,22},{16,24},... | collective-permute-start | bytes 1572872 | tf_op jit(solution)/shard_map/rs_out_z3/ppermute | solution.py:526
  535.3 53.7 %collective-permute-start.33 = (bf16[512,2048]{1,0:T(8,128)(2,1)}, bf16[512,2048]{1,0:T(8,128)(2,1)}, u32[]{:S(2)}, u32[]{:S(2)}) collective-permute-start(bf16[512,2048]{1,0:T(8,128)(2,1)} %split.29), channel_id=1, source_target_pairs={{0,2},{2,0},{4,6},{6,4},{8,10},{10,8},{12,14},{14,12},{16,18},{18,... | collective-permute-start | bytes 6291464 | tf_op jit(solution)/shard_map/ppermute | solution.py:526
  541.9 53.2 %collective-permute-start.46 = (bf16[256,1024]{0,1:T(8,128)(2,1)}, bf16[256,1024]{0,1:T(8,128)(2,1)}, u32[]{:S(2)}, u32[]{:S(2)}) collective-permute-start(bf16[256,1024]{0,1:T(8,128)(2,1)} %get-tuple-element.219), channel_id=1, source_target_pairs={{0,4},{2,6},{4,0},{6,2},{8,12},{10,14},{12,8},{14,10},{16,20},{18,... | collective-permute-start | bytes 1572872 | tf_op jit(solution)/shard_map/rs_gate_y4/ppermute | solution.py:526
  575.2 39.1 %collective-permute-start.63 = (bf16[256,1024]{0,1:T(8,128)(2,1)}, bf16[256,1024]{0,1:T(8,128)(2,1)}, u32[]{:S(2)}, u32[]{:S(2)}) collective-permute-start(bf16[256,1024]{0,1:T(8,128)(2,1)} %get-tuple-element.211), channel_id=1, source_target_pairs={{0,4},{2,6},{4,0},{6,2},{8,12},{10,14},{12,8},{14,10},{16,20},{18,... | collective-permute-start | bytes 1572872 | tf_op jit(solution)/shard_map/rs_out_y4/ppermute | solution.py:526
  600.9 80.1 %collective-permute-start.32 = (bf16[256,2048]{1,0:T(8,128)(2,1)}, bf16[256,2048]{1,0:T(8,128)(2,1)}, u32[]{:S(2)}, u32[]{:S(2)}) collective-permute-start(bf16[256,2048]{1,0:T(8,128)(2,1)} %constant_dynamic-slice_fusion.16), channel_id=1, source_target_pairs={{0,1},{1,0},{2,3},{3,2},{4,5},{5,4},{6,7},{7,6},{8,9},{9,8},{10,11... | collective-permute-start | bytes 3145736 | tf_op jit(solution)/shard_map/ppermute | solution.py:536
  603.7 102.7 %collective-permute-start.34 = (bf16[256,2048]{1,0:T(8,128)(2,1)}, bf16[256,2048]{1,0:T(8,128)(2,1)}, u32[]{:S(2)}, u32[]{:S(2)}) collective-permute-start(bf16[256,2048]{1,0:T(8,128)(2,1)} %constant_dynamic-slice_fusion.15), channel_id=1, source_target_pairs={{0,1},{1,0},{2,3},{3,2},{4,5},{5,4},{6,7},{7,6},{8,9},{9,8},{10,11... | collective-permute-start | bytes 3145736 | tf_op jit(solution)/shard_map/ppermute | solution.py:536
  710.8 52.5 %all-to-all-start.3 = ((bf16[16,16,2048]{2,1,0:T(8,128)(2,1)}), bf16[16,16,2048]{2,1,0:T(8,128)(2,1)}, u32[]{:S(2)}, u32[]{:S(2)}) async-start(bf16[16,16,2048]{2,1,0:T(8,128)(2,1)} %bitcast.22), calls=%async_computation.3 | async-start | bytes 2097152 | tf_op jit(solution)/shard_map/all_to_all | solution.py:711
  (128 other events, 2273.9 us)
Sparse Core Ops, SparseCore 0:
  27.9 44.2 all-gather.1
  468.2 99.6 reduce-scatter.3

commit v3 on v2

--- a/solution.py
+++ b/solution.py
@@ -5,10 +5,10 @@
 from jax.experimental.pallas import tpu as pltpu
 from jax.sharding import PartitionSpec as P
 
+
 D = 2048
 STATE = 128
 KCONV = 4
-SPAN = 256
 BLK = 64
 INNER = 4096
 
@@ -16,7 +16,6 @@
 EPSILON = 1e-05
 DECAY_RATE = 0.5
 LEARN_RATE = 0.2
-HIGHEST = lax.Precision.HIGHEST
 
 
 def segment_info(lengths, row_count):
@@ -167,7 +166,7 @@
     gate_ref, inner_ref, mixed_ref, dnorm_ref, gs_ref, coef_ref, gain_ref,
     state_ref, dt_ref, sig_ref, rate_ref, cw_ref, cb_ref, csw_ref, csb_ref, skip_ref,
     segc_ref, segr_ref, posc_ref,
-    dgate_ref, dinner_ref, dstep_ref, dstate_ref, rowsum_ref, headsum_ref, stsum_ref,
+    dinner_ref, dstep_ref, dstate_ref, rowsum_ref, headsum_ref, stsum_ref,
     bc_ref, bt_ref, ct_ref, st_ref, dst_acc, dbc_acc, dpre_ref, keep_ref,
 ):
     rows = inner_ref.shape[0]
@@ -265,7 +264,6 @@
         dn = dnorm_ref[r, :] * gs_ref[r, :]
         dg = dn * gain - gated * coef_ref[r, :]
         gain_row = gain_row + jnp.sum(dn * gated, axis=0, keepdims=True)
-        dgate_ref[r, :] = (dg * mixed * (sg + silu * (1.0 - sg))).astype(jnp.bfloat16)
         dm = dg * silu
         dyb = dm.astype(jnp.bfloat16)
         skip_row = skip_row + jnp.sum(dm * x, axis=0, keepdims=True)
@@ -354,8 +352,8 @@
     return pl.BlockSpec(shape, index)
 
 
-def _tile(rows):
-    return _block((rows, LANES), lambda s, g: (s, g), rows > 4 * MIX_ROWS)
+def _tile(rows, first=0):
+    return _block((rows, LANES), lambda s, g: (s + first, g), rows > 4 * MIX_ROWS)
 
 
 def _per_lane(rows):
@@ -366,16 +364,20 @@
     return _block(shape, lambda s, g: (0,) * len(shape))
 
 
-def _rows(rows, width):
-    return _block((rows, width), lambda s, g: (s, 0), rows > 4 * MIX_ROWS)
-
-
-def _line(rows):
-    return _block((1, rows), lambda s, g: (0, s))
-
-
-def _heads(rows):
-    return _block((1, rows, TILEH), lambda s, g: (g, s, 0), rows > 4 * MIX_ROWS)
+def _rows(rows, width, first=0):
+    return _block((rows, width), lambda s, g: (s + first, 0), rows > 4 * MIX_ROWS)
+
+
+def _state(rows, at, first=0):
+    return _block((rows, 2 * STATE), lambda s, g: (s + first, at), rows > 4 * MIX_ROWS)
+
+
+def _line(rows, first=0):
+    return _block((1, rows), lambda s, g: (0, s + first))
+
+
+def _heads(rows, first=0):
+    return _block((1, rows, TILEH), lambda s, g: (g, s + first, 0), rows > 4 * MIX_ROWS)
 
 
 def _rate():
@@ -393,8 +395,9 @@
     )
 
 
-def mixer_forward(gate, inner, state, dt, k, rows):
-    total, width = inner.shape
+def mixer_forward(gate, joined, dt, k, rows):
+    total, width = gate.shape
+    at = width // (2 * STATE)
     blocks = rows // MIX_ROWS
     f = jnp.float32
     wide = jax.ShapeDtypeStruct((total, width), f)
@@ -402,7 +405,7 @@
         mixer_fwd_kernel,
         grid=(total // rows, width // LANES),
         in_specs=[
-            _tile(rows), _tile(rows), _rows(rows, 2 * STATE), _heads(rows), _rate(),
+            _tile(rows), _tile(rows), _state(rows, at), _heads(rows), _rate(),
             _per_lane(KCONV), _per_lane(1), _fixed((KCONV, 2 * STATE)), _fixed((1, 2 * STATE)), _per_lane(1),
             _rows(rows, 1), _line(rows), _rows(rows, 1),
         ],
@@ -415,35 +418,37 @@
         ],
         cost_estimate=pl.CostEstimate(flops=total * width * 3000, bytes_accessed=total * width * 16, transcendentals=total * width * 6),
         name="mixer_forward",
-    )(gate, inner, state, dt, k["rate"], k["cw"], k["cb"], k["csw"], k["csb"], k["skip"],
+    )(gate, joined, joined, dt, k["rate"], k["cw"], k["cb"], k["csw"], k["csb"], k["skip"],
       k["segc"], k["segr"], k["posc"])
 
 
-def mixer_backward(gate, inner, mixed, dnorm, gs, coef, gain, state, dt, sig, k, rows):
-    total, width = inner.shape
+def mixer_backward(gate, joined, mixed, dnorm, gs, coef, gain, dt, sig, k, rows, first):
+    _, width = gate.shape
+    at = width // (2 * STATE)
     blocks = rows // MIX_ROWS
     tiles = width // LANES
-    spans = total // rows
+    spans = 1
     f = jnp.float32
-    wide = jax.ShapeDtypeStruct((total, width), jnp.bfloat16)
+    wide = jax.ShapeDtypeStruct((rows, width), jnp.bfloat16)
     return pl.pallas_call(
         mixer_bwd_kernel,
         grid=(spans, tiles),
         in_specs=[
-            _tile(rows), _tile(rows), _tile(rows), _tile(rows), _rows(rows, 1), _rows(rows, 1), _per_lane(1),
-            _rows(rows, 2 * STATE), _heads(rows), _heads(rows), _rate(),
+            _tile(rows, first), _tile(rows, first), _tile(rows, first), _tile(rows, first),
+            _rows(rows, 1, first), _rows(rows, 1, first), _per_lane(1),
+            _state(rows, at, first), _heads(rows, first), _heads(rows, first), _rate(),
             _per_lane(KCONV), _per_lane(1), _fixed((KCONV, 2 * STATE)), _fixed((1, 2 * STATE)), _per_lane(1),
-            _rows(rows, 1), _line(rows), _rows(rows, 1),
+            _rows(rows, 1, first), _line(rows, first), _rows(rows, 1, first),
         ],
         out_specs=[
-            _tile(rows), _tile(rows), _heads(rows), _rows(rows, 2 * STATE),
+            _tile(rows), _heads(rows), _rows(rows, 2 * STATE),
             _block((8, LANES), lambda s, g: (s, g)),
             _block((1, 2, TILEH), lambda s, g: (s * tiles + g, 0, 0)),
             _block((8, 2 * STATE), lambda s, g: (s, 0)),
         ],
         out_shape=[
-            wide, wide, jax.ShapeDtypeStruct((tiles, total, TILEH), f),
-            jax.ShapeDtypeStruct((total, 2 * STATE), jnp.bfloat16),
+            wide, jax.ShapeDtypeStruct((tiles, rows, TILEH), f),
+            jax.ShapeDtypeStruct((rows, 2 * STATE), jnp.bfloat16),
             jax.ShapeDtypeStruct((spans * 8, width), f), jax.ShapeDtypeStruct((spans * tiles, 2, TILEH), f),
             jax.ShapeDtypeStruct((spans * 8, 2 * STATE), f),
         ],
@@ -457,24 +462,67 @@
             pltpu.VMEM((rows, LANES), f),
             pltpu.VMEM((max(blocks - 1, 1), STATE, LANES), f),
         ],
-        cost_estimate=pl.CostEstimate(flops=total * width * 6000, bytes_accessed=total * width * 20, transcendentals=total * width * 10),
+        cost_estimate=pl.CostEstimate(flops=rows * width * 6000, bytes_accessed=rows * width * 20, transcendentals=rows * width * 10),
         name="mixer_backward",
-    )(gate, inner, mixed, dnorm, gs, coef, gain, state, dt, sig, k["rate"], k["cw"], k["cb"], k["csw"], k["csb"], k["skip"],
+    )(gate, joined, mixed, dnorm, gs, coef, gain, joined, dt, sig, k["rate"], k["cw"], k["cb"], k["csw"], k["csb"], k["skip"],
       k["segc"], k["segr"], k["posc"])
 
 
+def shampoo_kernel(w_ref, g_ref, stats_ref, roots_ref, new_ref, master_ref, copy_ref):
+    high, across = stats_ref.shape[0], stats_ref.shape[1]
+    span = across * BLK
+    lane = lax.broadcasted_iota(jnp.int32, (BLK, span), 1) // BLK
+    zero = jnp.zeros((), jnp.bfloat16)
+    empty = jnp.zeros((BLK, BLK), jnp.bfloat16)
+    for a in range(high):
+        rows = slice(a * BLK, (a + 1) * BLK)
+        tile = g_ref[rows, :].astype(jnp.bfloat16)
+        apart = jnp.concatenate([jnp.where(lane == b, tile, zero) for b in range(across)], axis=0)
+        left = _dot_t(apart, tile)
+        right = _dot_tl(tile, tile)
+        firsts = jnp.concatenate([roots_ref[a, b, 0].astype(jnp.bfloat16) for b in range(across)], axis=0)
+        turned = _dot(firsts, tile)
+        half = turned[0:BLK]
+        for b in range(1, across):
+            half = jnp.where(lane == b, turned[b * BLK : (b + 1) * BLK], half)
+        joint = jnp.concatenate(
+            [
+                jnp.concatenate(
+                    [roots_ref[a, b, 1].astype(jnp.bfloat16) if c == b else empty for c in range(across)], axis=1
+                )
+                for b in range(across)
+            ],
+            axis=0,
+        )
+        step = _dot(half.astype(jnp.bfloat16), joint)
+        for b in range(across):
+            part = slice(b * BLK, (b + 1) * BLK)
+            new_ref[a, b, 0] = DECAY_RATE * stats_ref[a, b, 0] + (1.0 - DECAY_RATE) * left[part, :]
+            new_ref[a, b, 1] = DECAY_RATE * stats_ref[a, b, 1] + (1.0 - DECAY_RATE) * right[part, part]
+        master = w_ref[rows, :].astype(jnp.float32) - LEARN_RATE * step
+        master_ref[rows, :] = master
+        copy_ref[rows, :] = master.astype(jnp.bfloat16)
+
+
 def shampoo(weight, gradient, stat_pair, root_pair):
-    row_count, col_count = gradient.shape
-    blocks = gradient.reshape(row_count // BLK, BLK, col_count // BLK, BLK).transpose(0, 2, 1, 3)
-    left_stat = jnp.einsum("abij,abkj->abik", blocks, blocks, precision=HIGHEST)
-    right_stat = jnp.einsum("abji,abjk->abik", blocks, blocks, precision=HIGHEST)
-    fresh_stats = jnp.stack([left_stat, right_stat], axis=2)
-    new_stats = DECAY_RATE * stat_pair + (1.0 - DECAY_RATE) * fresh_stats
-    turned = jnp.einsum("abij,abjk->abik", root_pair[:, :, 0], blocks, precision=HIGHEST)
-    turned = jnp.einsum("abij,abjk->abik", turned, root_pair[:, :, 1], precision=HIGHEST)
-    update_step = turned.transpose(0, 2, 1, 3).reshape(row_count, col_count)
-    master = weight - LEARN_RATE * update_step
-    return (new_stats, master, master.astype(jnp.bfloat16))
+    rows, cols = gradient.shape
+    step = min(cols, 256)
+    plain = pl.BlockSpec((rows, step), lambda i: (0, i))
+    pairs = pl.BlockSpec((rows // BLK, step // BLK, 2, BLK, BLK), lambda i: (0, i, 0, 0, 0))
+    return pl.pallas_call(
+        shampoo_kernel,
+        grid=(cols // step,),
+        in_specs=[plain, plain, pairs, pairs],
+        out_specs=[pairs, plain, plain],
+        out_shape=[
+            jax.ShapeDtypeStruct(stat_pair.shape, jnp.float32),
+            jax.ShapeDtypeStruct((rows, cols), jnp.float32),
+            jax.ShapeDtypeStruct((rows, cols), jnp.bfloat16),
+        ],
+        cost_estimate=pl.CostEstimate(flops=rows * cols * 512, bytes_accessed=rows * cols * 40, transcendentals=0),
+        compiler_params=pltpu.CompilerParams(vmem_limit_bytes=24 * 2**20),
+        name="shampoo",
+    )(weight, gradient, stat_pair, root_pair)
 
 
 def contract_rows(left_side, right_side):
@@ -526,11 +574,6 @@
     return lax.ppermute(values, "dp", pairs)
 
 
-def swap_dp(values, distance):
-    groups = lax.axis_size("dp")
-    return lax.ppermute(values, "dp", [(s, s ^ distance) for s in range(groups)])
-
-
 def swap_tensor(values, distance):
     ranks = lax.axis_size("tensor")
     return lax.ppermute(values, "tensor", [(s, s ^ distance) for s in range(ranks)])
@@ -560,31 +603,83 @@
     return lax.dynamic_slice_in_dim(values, which * size, size, axis)
 
 
-def gather_weight(weight, name):
+def scale_rows_kernel(v_ref, square_ref, gain_ref, o_ref, scale_ref):
+    scale = lax.rsqrt(square_ref[...] / INNER + EPSILON)
+    scale_ref[...] = scale
+    o_ref[...] = (v_ref[...] * scale * gain_ref[...]).astype(jnp.bfloat16)
+
+
+def scale_rows(values, square, gain):
+    rows, cols = values.shape
+    step = 256
+    wide = pl.BlockSpec((step, cols), lambda i: (i, 0))
+    thin = pl.BlockSpec((step, 1), lambda i: (i, 0))
+    return pl.pallas_call(
+        scale_rows_kernel,
+        grid=(rows // step,),
+        in_specs=[wide, thin, pl.BlockSpec((1, cols), lambda i: (0, 0))],
+        out_specs=[wide, thin],
+        out_shape=[
+            jax.ShapeDtypeStruct((rows, cols), jnp.bfloat16), jax.ShapeDtypeStruct((rows, 1), jnp.float32),
+        ],
+        cost_estimate=pl.CostEstimate(flops=2 * rows * cols, bytes_accessed=6 * rows * cols, transcendentals=0),
+        name="scale_rows",
+    )(values, square, gain)
+
+
+def blank_kernel(*refs):
+    pass
+
+
+def blanks(*shapes):
+    return pl.pallas_call(
+        blank_kernel,
+        out_shape=[jax.ShapeDtypeStruct(s, jnp.bfloat16) for s in shapes],
+        out_specs=[pl.BlockSpec(memory_space=pl.ANY) for _ in shapes],
+        name="blanks",
+    )()
+
+
+def gather_weight(full, weight, shared=None, halves=None, merge=1):
     z, y, core, ny = place_on()
-    with jax.named_scope(name + "_core"):
-        got = shift(half_of(weight, 1 - core, 1), dc=1)
-    piece = by_core(core, half_of(weight, core, 1), got, 0)
-    rows, width = piece.shape
-    full = jnp.zeros((Z_RING * ny * rows, width), weight.dtype)
+
+    def columns(which):
+        parts = [half_of(weight, which, 1)]
+        if shared is not None:
+            parts += [shared, half_of(halves, which, 1)]
+            spare = -sum(p.shape[1] for p in parts) % 128
+            parts.append(jnp.zeros((weight.shape[0], spare), weight.dtype))
+        return jnp.concatenate(parts, axis=1)
+
+    got = shift(columns(1 - core), dc=1)
+    piece = by_core(core, columns(core), got, 0)
+    rows = piece.shape[0]
 
     def put(full, part, dz, dy):
         at = ((z - dz) % Z_RING * ny + (y - dy) % ny) * rows
         return lax.dynamic_update_slice_in_dim(full, part, at, 0)
 
-    for dz in range(Z_RING):
-        full = put(full, piece, dz, 0)
+    ring = [piece]
+    for dz in range(Z_RING - 1):
+        ring.append(shift(ring[dz], dz=1))
+    for send in range(Z_RING // merge):
+        span = range(send * merge, (send + 1) * merge)
+        both = jnp.concatenate([ring[i] for i in span], axis=0)
         for dy in range(1, ny):
-            with jax.named_scope(f"{name}_y{dz}"):
-                across = shift(piece, dy=dy)
-            full = put(full, across, dz, dy)
-        if dz < Z_RING - 1:
-            with jax.named_scope(f"{name}_z{dz}"):
-                piece = shift(piece, dz=1)
+            across = shift(both, dy=dy)
+            for k, i in enumerate(span):
+                full = put(full, across[k * rows : (k + 1) * rows], i, dy)
+        for i in span:
+            full = put(full, ring[i], i, 0)
     return full
 
 
-def reduce_weight(partial, name):
+def swap_rows(run, core):
+    got = shift(half_of(run, 1 - core, 0).astype(jnp.bfloat16), dc=1).astype(jnp.float32)
+    return half_of(run, core, 0), got
+
+
+def reduce_weight(partial, sends):
     z, y, core, ny = place_on()
     rows = partial.shape[0] // (Z_RING * ny)
     f = jnp.float32
@@ -593,20 +688,30 @@
         at = ((z - dz) % Z_RING * ny + (y + dy) % ny) * rows
         return lax.dynamic_slice_in_dim(partial, at, rows, 0)
 
-    run = None
-    for dz in range(1, Z_RING + 1):
-        own = part(dz, 0).astype(f)
+    if not sends:
+        def line(dz):
+            return lax.dynamic_slice_in_dim(partial, (z + dz) % Z_RING * ny * rows, ny * rows, 0)
+
+        run = line(0).astype(f)
+        for dz in range(1, Z_RING):
+            run = run + shift(line(dz), dz=dz).astype(f)
+        total = lax.dynamic_slice_in_dim(run, y * rows, rows, 0)
         for dy in range(1, ny):
-            with jax.named_scope(f"{name}_y{dz}"):
-                own = own + shift(part(dz, dy), dy=dy).astype(f)
-        if run is None:
-            run = own
-        else:
-            with jax.named_scope(f"{name}_z{dz}"):
-                run = shift(run.astype(jnp.bfloat16), dz=1).astype(f) + own
-    with jax.named_scope(name + "_core"):
-        got = shift(half_of(run, 1 - core, 0).astype(jnp.bfloat16), dc=1).astype(f)
-    return by_core(core, half_of(run, core, 0), got, 1)
+            there = lax.dynamic_slice_in_dim(run, (y + dy) % ny * rows, rows, 0)
+            total = total + shift(there.astype(jnp.bfloat16), dy=dy).astype(f)
+        return swap_rows(total, core)
+    owns = [part(dz, 0).astype(f) for dz in range(1, Z_RING + 1)]
+    for send, size in enumerate(sends):
+        begin = sum(sends[:send])
+        span = range(begin, begin + size)
+        for dy in range(1, ny):
+            across = shift(jnp.concatenate([part(i + 1, dy) for i in span], axis=0), dy=dy)
+            for k, i in enumerate(span):
+                owns[i] = owns[i] + across[k * rows : (k + 1) * rows].astype(f)
+    run = owns[0]
+    for dz in range(1, Z_RING):
+        run = shift(run.astype(jnp.bfloat16), dz=1).astype(f) + owns[dz]
+    return swap_rows(run, core)
 
 
 def body(
@@ -618,7 +723,7 @@
     f = jnp.float32
     groups = lax.axis_size("dp")
     tensor_ranks = lax.axis_size("tensor")
-    z, y, core, ny = place_on()
+    _, _, core, ny = place_on()
     local_rows = tokens.shape[0]
     slot_rows = local_rows // groups
     group_rows = local_rows * tensor_ranks
@@ -631,11 +736,12 @@
     normed = (tokens_f * scale_in[:, None] * gain_in[None, :]).astype(jnp.bfloat16)
     send_choose = rank_matrix(inverse_perm)
 
-    gate_w = gather_weight(w_gate, "ag_gate")
-    input_w = gather_weight(w_input, "ag_input")
-    out_w = gather_weight(w_out, "ag_out")
-    state_w = lax.all_gather(w_state, "dp", axis=0, tiled=True)
-    step_w = half_of(lax.all_gather(w_step, "dp", axis=0, tiled=True), core, 1)
+    edge = width + 2 * STATE
+    spare = -(edge + heads) % 128
+    all_gate, all_input, all_out = blanks((D, width), (D, edge + heads + spare), (D, width))
+    gate_w = gather_weight(all_gate, w_gate)
+    input_w = gather_weight(all_input, w_input, w_state, w_step)
+    out_w = gather_weight(all_out, w_out)
 
     source = balance_perm // local_rows
     row_key = (source % tensor_ranks * groups + source // tensor_ranks) * group_rows + jnp.arange(
@@ -645,7 +751,8 @@
 
     def dispatch(values):
         sent = move_rows(send_choose, values).reshape(groups, slot_rows, D)
-        arrived = lax.all_to_all(sent, "dp", split_axis=0, concat_axis=0, tiled=True).reshape(local_rows, D)
+        arrived = lax.all_to_all(sent, "dp", split_axis=0, concat_axis=0, tiled=True)
+        arrived = arrived.reshape(local_rows, D)
         if tensor_ranks == 2:
             rank = lax.axis_index("tensor")
             got = swap_tensor(arrived, 1)
@@ -653,7 +760,8 @@
         else:
             both = lax.all_gather(arrived, "tensor", axis=0, tiled=True)
         own = move_back(place, both)
-        return jnp.concatenate([own, shift(own, dc=1)], axis=0)
+        partner = shift(own, dc=1)
+        return jnp.concatenate([own, partner], axis=0)
 
     normed_bal = dispatch(normed)
     cot_bal = dispatch(cotangent)
@@ -666,9 +774,8 @@
 
     d_normal = jnp.dot(cot_bal, out_w, preferred_element_type=f)
     gate_proj = jnp.dot(normed_bal, gate_w, preferred_element_type=f)
-    inner_proj = jnp.dot(normed_bal, input_w, preferred_element_type=f)
-    state_proj = jnp.dot(normed_bal, state_w, preferred_element_type=f)
-    step_full = jnp.dot(normed_bal, step_w, preferred_element_type=f)
+    joined = jnp.dot(normed_bal, input_w, preferred_element_type=f)
+    step_full = jnp.dot(normed_bal, input_w[:, edge : edge + heads], preferred_element_type=f)
     step_full = step_full + half_of(step_bias, core, 0).astype(f)[None, :]
     tiles = heads // TILEH
     step_tiles = step_full.reshape(CORES * group_rows, tiles, TILEH).transpose(1, 0, 2)
@@ -679,84 +786,98 @@
         half_of(skip_gain, core, 0), half_of(decay_log, core, 0), segment, position,
     )
     gain_gate = half_of(gate_gain, core, 0).astype(f)
-    mixed, gated_out, square = mixer_forward(gate_proj, inner_proj, state_proj, step_len, consts, group_rows)
-    inner_dot = jnp.sum(gated_out * gain_gate[None, :] * d_normal, axis=1)
-    row_stats = jnp.stack([square[:, 0], inner_dot])
-    row_stats = row_stats + flip_halves(shift(row_stats, dc=1), 1)
-    row_stats = sum_tensor(row_stats)
-    gate_scale = lax.rsqrt(row_stats[0] / INNER + EPSILON)
-    coef = gate_scale**3 * row_stats[1] / INNER
-    normal = (gated_out * gate_scale[:, None] * gain_gate[None, :]).astype(jnp.bfloat16)
-
-    d_gate, d_inner, d_step, d_state, row_sums, head_sums, state_sums = mixer_backward(
-        gate_proj, inner_proj, mixed, d_normal, gate_scale[:, None], coef[:, None], gain_gate[None, :],
-        state_proj, step_len, step_slope, consts, group_rows,
-    )
-    d_step = d_step.transpose(1, 0, 2).reshape(CORES * group_rows, heads).astype(jnp.bfloat16)
-
-    out_grad = reduce_weight(contract_rows(cot_bal, normal).astype(jnp.bfloat16), "rs_out")
-    gate_grad = reduce_weight(contract_rows(normed_bal, d_gate).astype(jnp.bfloat16), "rs_gate")
-    input_grad = reduce_weight(contract_rows(normed_bal, d_inner).astype(jnp.bfloat16), "rs_input")
-
-    def give_back(partial):
-        own, other = jnp.split(partial, 2, axis=0)
-        own = (own.astype(f) + shift(other, dc=1).astype(f)).astype(jnp.bfloat16)
+    mixed, gated_out, square = mixer_forward(gate_proj, joined, step_len, consts, group_rows)
+
+    def row_total(values):
+        values = values + flip_halves(shift(values, dc=1), 0)
+        return sum_tensor(values)
+
+    inner_dot = row_total(jnp.sum(gated_out * gain_gate[None, :] * d_normal, axis=1))
+    normal, gate_scale = scale_rows(gated_out, row_total(square[:, 0])[:, None], gain_gate[None, :])
+    coef = gate_scale**3 * inner_dot[:, None] / INNER
+
+    def give_back(own, other):
+        got = shift(other, dc=1)
+        own = (own.astype(f) + got.astype(f)).astype(jnp.bfloat16)
         arranged = move_rows(place, own)
         if tensor_ranks == 2:
             rank = lax.axis_index("tensor")
             mine = half_of(arranged, rank, 0).astype(f)
-            total = (mine + swap_tensor(half_of(arranged, 1 - rank, 0), 1).astype(f)).astype(jnp.bfloat16)
+            got = swap_tensor(half_of(arranged, 1 - rank, 0), 1)
+            total = (mine + got.astype(f)).astype(jnp.bfloat16)
         else:
             total = lax.psum_scatter(arranged, "tensor", scatter_dimension=0, tiled=True)
-        returned = lax.all_to_all(
-            total.reshape(groups, slot_rows, D), "dp", split_axis=0, concat_axis=0, tiled=True
+        returned = lax.all_to_all(total.reshape(groups, slot_rows, D), "dp", split_axis=0, concat_axis=0, tiled=True)
+        return move_back(send_choose, returned.reshape(local_rows, D)).astype(f)
+
+    branch_other = contract_cols(normal[group_rows:], out_w).astype(jnp.bfloat16)
+    branch_own = contract_cols(normal[:group_rows], out_w)
+    branch = give_back(branch_own, branch_other)
+    out_part = contract_rows(cot_bal, normal).astype(jnp.bfloat16)
+    out_own, out_got = reduce_weight(out_part, ())
+    out_grad = by_core(core, out_own, out_got, 1)
+
+    sig_gate = jax.nn.sigmoid(gate_proj)
+    silu_gate = gate_proj * sig_gate
+    d_gated = d_normal * gate_scale * gain_gate[None, :] - gated_out * coef
+    d_gate = (d_gated * mixed * (sig_gate + silu_gate * (1.0 - sig_gate))).astype(jnp.bfloat16)
+    gate_own, gate_got = reduce_weight(contract_rows(normed_bal, d_gate).astype(jnp.bfloat16), (4,))
+    gate_grad = by_core(core, gate_own, gate_got, 1)
+
+    def back_half(at):
+        d_inner, d_step, d_state, rows_part, heads_part, state_part = mixer_backward(
+            gate_proj, joined, mixed, d_normal, gate_scale, coef, gain_gate[None, :],
+            step_len, step_slope, consts, group_rows, at,
         )
-        return move_back(send_choose, returned.reshape(local_rows, D)).astype(f)
-
-    branch = give_back(contract_cols(normal, out_w).astype(jnp.bfloat16))
-    column_term = (
-        contract_cols(d_gate, gate_w)
-        + contract_cols(d_inner, input_w)
-        + contract_cols(d_state, state_w)
-        + contract_cols(d_step, step_w)
-    )
-    norm_gain_part = jnp.sum(column_term * normed_bal.astype(f), axis=0) / gain_in
-    d_tokens_normed = give_back(column_term.astype(jnp.bfloat16))
-
-    state_part = contract_rows(normed_bal, d_state).astype(jnp.bfloat16)
-    step_part = contract_rows(normed_bal, d_step).astype(jnp.bfloat16)
-    step_part = jnp.where(
-        (jnp.arange(CORES * heads, dtype=jnp.int32) // heads == core)[None, :],
-        jnp.concatenate([step_part] * CORES, axis=1),
-        jnp.zeros((), jnp.bfloat16),
-    )
-    thin = lax.psum_scatter(
-        jnp.concatenate([state_part, step_part], axis=1), "dp", scatter_dimension=0, tiled=True
-    )
-    state_grad = sum_tensor(thin[:, : 2 * STATE].astype(f))
-    step_grad = thin[:, 2 * STATE :].astype(f)
-
-    row_sums = jnp.sum(row_sums.reshape(CORES, 8, width), axis=0)
-    head_sums = jnp.sum(head_sums.reshape(CORES, tiles, 2, TILEH), axis=0).transpose(1, 0, 2).reshape(2, heads)
+        d_step = d_step.transpose(1, 0, 2).reshape(group_rows, heads).astype(jnp.bfloat16)
+        empty = jnp.zeros((group_rows, spare), jnp.bfloat16)
+        return jnp.concatenate([d_inner, d_state, d_step, empty], axis=1), rows_part, heads_part, state_part
+
+    second_half = back_half(1)
+    first_half = back_half(0)
+    d_joined = jnp.concatenate([first_half[0], second_half[0]], axis=0)
+    row_sums, head_sums, state_sums = [one + two for one, two in zip(first_half[1:], second_half[1:])]
+    joined_own, joined_got = reduce_weight(contract_rows(normed_bal, d_joined).astype(jnp.bfloat16), (1, 1, 2))
+    input_grad = by_core(core, joined_own[:, :width], joined_got[:, :width], 1)
+    state_grad = sum_tensor(joined_own[:, width:edge] + joined_got[:, width:edge])
+    step_grad = by_core(core, joined_own[:, edge : edge + heads], joined_got[:, edge : edge + heads], 1)
+
+    def column_term(at):
+        part = slice(at * group_rows, (at + 1) * group_rows)
+        half = (first_half, second_half)[at][0]
+        return contract_cols(d_gate[part], gate_w) + contract_cols(half, input_w)
+
+    term_other = column_term(1)
+    term_own = column_term(0)
+    norm_gain_part = (
+        jnp.sum(term_own * normed_bal[:group_rows].astype(f), axis=0)
+        + jnp.sum(term_other * normed_bal[group_rows:].astype(f), axis=0)
+    ) / gain_in
+    d_tokens_normed = give_back(term_own, term_other.astype(jnp.bfloat16))
+
+    head_sums = head_sums.transpose(1, 0, 2).reshape(2, heads)
     skip_sums = jnp.sum(row_sums[KCONV + 2].reshape(heads, HEADW), axis=1)
-    state_sums = jnp.sum(state_sums.reshape(CORES, 8, 2 * STATE), axis=0)[: KCONV + 1]
+    state_sums = state_sums[: KCONV + 1]
+    lanes = (KCONV + 2) * width
     split_part = jnp.concatenate([row_sums[: KCONV + 2].reshape(-1), head_sums.reshape(-1), skip_sums])
     shared_part = jnp.concatenate([norm_gain_part, state_sums.reshape(-1)])
-    packed = jnp.concatenate([split_part, shared_part])
-    distance = CORES
-    while distance < groups:
-        packed = packed + swap_dp(packed, distance)
-        distance *= 2
-    partner = shift(packed, dc=1)
-    edge = split_part.shape[0]
-    shared = sum_tensor(packed[edge:] + partner[edge:])
-    lanes = (KCONV + 2) * width
-    wide_sums = by_core(
-        core, packed[:lanes].reshape(KCONV + 2, width), partner[:lanes].reshape(KCONV + 2, width), 1
-    )
-    thin_sums = by_core(
-        core, packed[lanes:edge].reshape(3, heads), partner[lanes:edge].reshape(3, heads), 1
-    )
+    split_at = split_part.shape[0]
+    partner = shift(jnp.concatenate([split_part, shared_part]), dc=1)
+    shared_part = sum_tensor(shared_part + partner[split_at:])
+    wide_part = by_core(
+        core, split_part[:lanes].reshape(KCONV + 2, width), partner[:lanes].reshape(KCONV + 2, width), 1
+    )
+    thin_part = by_core(core, split_part[lanes:].reshape(3, heads), partner[lanes:split_at].reshape(3, heads), 1)
+    packed = jnp.concatenate([wide_part.reshape(-1), thin_part.reshape(-1), shared_part])
+    packed_low = packed.astype(jnp.bfloat16)
+    for dz in range(Z_RING):
+        for dy in range(ny):
+            if (dz, dy) != (0, 0):
+                packed = packed + shift(packed_low, dz=dz, dy=dy).astype(f)
+    lanes, split_at = CORES * lanes, CORES * split_at
+    wide_sums = packed[:lanes].reshape(KCONV + 2, CORES * width)
+    thin_sums = packed[lanes:split_at].reshape(3, CORES * heads)
+    shared = packed[split_at:]
     norm_gain_grad = shared[:D]
     conv_state_grads = shared[D:].reshape(KCONV + 1, 2 * STATE)
 
@@ -767,10 +888,10 @@
         + d_tokens_normed * scale_in[:, None] * gain_in[None, :]
         - tokens_f * (scale_in**3 * dot_in / D)[:, None]
     )
-    new_gate = shampoo(w_gate.astype(f), gate_grad, stats_gate, roots_gate)
-    new_input = shampoo(w_input.astype(f), input_grad, stats_input, roots_input)
-    new_state = shampoo(w_state.astype(f), state_grad, stats_state, roots_state)
-    new_out = shampoo(w_out.astype(f), out_grad, stats_out, roots_out)
+    new_gate = shampoo(w_gate, gate_grad, stats_gate, roots_gate)
+    new_input = shampoo(w_input, input_grad, stats_input, roots_input)
+    new_state = shampoo(w_state, state_grad, stats_state, roots_state)
+    new_out = shampoo(w_out, out_grad, stats_out, roots_out)
     return (
         block_out, tokens_grad, norm_gain_grad, gate_grad, input_grad, state_grad, step_grad,
         wide_sums[:KCONV], wide_sums[KCONV], conv_state_grads[:KCONV], conv_state_grads[KCONV],

time: 783 us -> 761 us (0.972)
  matrix products: 197 us -> 124 us
  waiting for transfers between devices: 164 us -> 237 us
  Pallas kernels: 78 us -> 109 us
  starting transfers between devices: 113 us -> 142 us
  blocking collectives: 24.2 us -> 0 us
  local copies, waits for them, and re-layouts: 109 us -> 86 us
  other arithmetic: 73.7 us -> 52.3 us
  between operations: 16 us -> 2.39 us
    ppermute x55 -> x56, waiting for transfers between devices: 115 us -> 211 us  [shift(): return lax.ppermute(values, 'dp', pairs)]
    dot_general x19 -> x2, matrix products: 82.8 us -> 13.9 us  [the longest x1 10.5 us: body(): joined = jnp.dot(normed_bal, input_w, preferred_element_type=f)]
    pallas_call x0 -> x6, Pallas kernels: none -> 28.1 us  [the longest x4 23.6 us: shampoo(): pl.pallas_call(shampoo_kernel, grid=(cols // step,), in_specs=[plain, pla...]
    all_gather x1 -> x0, blocking collectives: 24.2 us -> none  [body(): step_w = half_of(lax.all_gather(w_step, 'dp', axis=0, tiled=True), core, 1)]
    unnamed x3 -> x0, waiting for transfers between devices: 24 us -> none
    ppermute x7 -> x8, waiting for transfers between devices: 3.11 us -> 26.1 us  [swap_tensor(): lax.ppermute(values, 'tensor', [(s, s ^ distance) for s in range(ranks)])]
    ppermute x55 -> x56, starting transfers between devices: 76.5 us -> 95 us  [shift(): return lax.ppermute(values, 'dp', pairs)]
    mul x8 -> x0, local copies, waits for them, and re-layouts: 15.9 us -> none  [shampoo(): master = weight - LEARN_RATE * update_step]
  transfers between devices with their start and end apart: 71 -> 68, of which waited for: 24 -> 21; matrix products, arithmetic and copies ran while one was open for 39% -> 30% of each run, Pallas kernels for 4% -> 7%
where the time goes in v3:
time: 761 us; the launch traced here: 753 us
  waiting for transfers between devices  237 us (31%)
  starting transfers between devices  142 us (19%)
  matrix products  124 us (16%)
  Pallas kernels  109 us (14%)
  local copies, waits for them, and re-layouts  86 us (11%)
  other arithmetic  52.3 us (7%)
    ppermute x56, waiting for transfers between devices, shift(): return lax.ppermute(values, 'dp', pairs)  211 us
    ppermute x56, starting transfers between devices, shift(): return lax.ppermute(values, 'dp', pairs)  95 us
    pallas_call x2, Pallas kernels, mixer_backward(): pl.pallas_call(mixer_bwd_kernel, grid=(spans, tiles), in_specs=[_tile(row...  49 us
    dynamic_update_slice x24, local copies, waits for them, and re-layouts, put(): return lax.dynamic_update_slice_in_dim(full, part, at, 0)  37.6 us
    dot_general x5, matrix products, contract_cols(): lax.dot_general(left_side, right_side, (((1,), (1,)), ((), ())), preferre...  36.3 us
    pallas_call x1, Pallas kernels, mixer_forward(): pl.pallas_call(mixer_fwd_kernel, grid=(total // rows, width // LANES), in...  31.9 us
    dot_general x3, matrix products, contract_rows(): lax.dot_general(left_side, right_side, (((0,), (0,)), ((), ())), preferre...  27.3 us
    all_to_all x2, starting transfers between devices, dispatch(): lax.all_to_all(sent, 'dp', split_axis=0, concat_axis=0, tiled=True)  27.1 us
  transfers between devices with their start and end apart: 68, of which 21 were waited for; matrix products, arithmetic and copies ran while one was open for 30% of the time, Pallas kernels for 7%

profile of v3, /device:TPU:0, one launch (start us, length us, event | category | flops | bytes accessed | tf_op | source)
XLA Modules:
  0.0 753.0 jit_solution(5391767816554040399)
XLA Ops:
  41.2 12.3 %collective-permute-done.4 = bf16[256,1024]{1,0:T(8,128)(2,1)} collective-permute-done((bf16[256,1024]{1,0:T(8,128)(2,1)S(1)}, bf16[256,1024]{1,0:T(8,128)(2,1)}, u32[]{:S(2)}, u32[]{:S(2)}) %collective-permute-start.4) | collective-permute-done | bytes 524320 | tf_op jit(solution)/shard_map/ppermute | solution.py:574
  65.5 14.0 %collective-permute-done.23 = bf16[256,1024]{1,0:T(8,128)(2,1)} collective-permute-done((bf16[256,1024]{1,0:T(8,128)(2,1)S(1)}, bf16[256,1024]{1,0:T(8,128)(2,1)}, u32[]{:S(2)}, u32[]{:S(2)}) %collective-permute-start.23) | collective-permute-done | bytes 524320 | tf_op jit(solution)/shard_map/ppermute | solution.py:574
  89.4 19.8 %all-to-all-start.2 = ((bf16[16,16,2048]{2,1,0:T(8,128)(2,1)}), bf16[16,16,2048]{2,1,0:T(8,128)(2,1)S(1)}, u32[]{:S(2)}, u32[]{:S(2)}) async-start(bf16[16,16,2048]{2,1,0:T(8,128)(2,1)} %bitcast.15), calls=%async_computation.2 | async-start | bytes 2097152 | tf_op jit(solution)/shard_map/all_to_all | solution.py:754
  129.4 17.8 %collective-permute-done.14 = bf16[256,1408]{1,0:T(8,128)(2,1)S(1)} collective-permute-done((bf16[256,1408]{1,0:T(8,128)(2,1)}, bf16[256,1408]{1,0:T(8,128)(2,1)S(1)}, u32[]{:S(2)}, u32[]{:S(2)}) %collective-permute-start.14) | collective-permute-done | bytes 720928 | tf_op jit(solution)/shard_map/ppermute | solution.py:574
  154.8 14.9 %collective-permute-done.27 = bf16[256,1024]{1,0:T(8,128)(2,1)} collective-permute-done((bf16[256,1024]{1,0:T(8,128)(2,1)S(1)}, bf16[256,1024]{1,0:T(8,128)(2,1)}, u32[]{:S(2)}, u32[]{:S(2)}) %collective-permute-start.27) | collective-permute-done | bytes 524320 | tf_op jit(solution)/shard_map/ppermute | solution.py:574
  176.8 32.9 %collective-permute-done.9 = bf16[256,1024]{1,0:T(8,128)(2,1)} collective-permute-done((bf16[256,1024]{1,0:T(8,128)(2,1)}, bf16[256,1024]{1,0:T(8,128)(2,1)}, u32[]{:S(2)}, u32[]{:S(2)}) %collective-permute-start.9) | collective-permute-done | bytes 524320 | tf_op jit(solution)/shard_map/ppermute | solution.py:574
  224.8 8.1 %collective-permute-done.31 = bf16[256,2048]{1,0:T(8,128)(2,1)S(1)} collective-permute-done((bf16[256,2048]{1,0:T(8,128)(2,1)S(1)}, bf16[256,2048]{1,0:T(8,128)(2,1)S(1)}, u32[]{:S(2)}, u32[]{:S(2)}) %collective-permute-start.31) | collective-permute-done | bytes 1048608 | tf_op jit(solution)/shard_map/ppermute | solution.py:579
  246.6 10.1 %fusion.68.gate_ref = f32[1024,1024]{1,0:T(8,128)} fusion(bf16[2048,1024]{1,0:T(8,128)(2,1)} %constant_dynamic-update-slice_fusion.16, bf16[512,2048]{1,0:T(8,128)(2,1)} %collective-permute-done.1, bf16[512,2048]{1,0:T(8,128)(2,1)} %convolution_convert_fusion.7), kind=kOutput, calls=%fused_computation.226 | convolution fusion | flops 4303355904 | bytes 12582912 | tf_op jit(solution)/shard_map/dot_general | solution.py:776
  256.7 10.5 %fusion.67.inner_ref.state_ref = f32[1024,1408]{1,0:T(8,128)} fusion(bf16[2048,1408]{1,0:T(8,128)(2,1)S(1)} %bitcast.103, bf16[512,2048]{1,0:T(8,128)(2,1)} %collective-permute-done.1, bf16[512,2048]{1,0:T(8,128)(2,1)} %convolution_convert_fusion.7), kind=kOutput, calls=%fused_computation.225 | convolution fusion | flops 5913968640 | bytes 15728640 | tf_op jit(solution)/shard_map/dot_general | solution.py:777
  267.1 31.9 %mixer_forward.1 = (f32[1024,1024]{1,0:T(8,128)}, f32[1024,1024]{1,0:T(8,128)}, f32[1024,1]{1,0:T(8,128)}) custom-call(f32[1024,1024]{1,0:T(8,128)} %fusion.68.gate_ref, f32[1024,1408]{1,0:T(8,128)} %fusion.67.inner_ref.state_ref, f32[1024,1408]{1,0:T(8,128)} %fusion.67.inner_ref.state_ref, f32[4,1024,4]{2,1,0:T(8,128)} %get-tuple-element.168.dt_ref, ...), custom_call_target="tpu_custom_call" | custom-call | flops 3145728000 | bytes 16777216 | tf_op jit(solution)/shard_map/mixer_forward/pallas_call | solution.py:404
  300.4 11.2 %multiply_reduce_fusion.2 = (f32[1024]{0:T(1024)S(1)}, f32[1024,1024]{1,0:T(8,128)}) fusion(f32[1024,1024]{1,0:T(8,128)} %get-tuple-element.62.v_ref, f32[1024]{0:T(1024)S(1)} %dynamic-slice_convert_fusion.4, bf16[2048,1024]{1,0:T(8,128)(2,1)} %constant_dynamic-update-slice_fusion, bf16[512,2048]{1,0:T(8,128)(2,1)} %collective-permute-done.32, ...), kind=kOutput, calls=%fused_computation.8 | convolution fusion | flops 4306500608 | bytes 16785408 | tf_op jit(solution)/shard_map/dot_general | solution.py:775
  324.0 24.3 %mixer_backward.2 = (bf16[512,1024]{1,0:T(8,128)(2,1)}, f32[4,512,4]{2,1,0:T(8,128)}, bf16[512,256]{1,0:T(8,128)(2,1)}, f32[8,1024]{1,0:T(8,128)}, f32[4,2,4]{2,1,0:T(2,128)}, /*index=5*/f32[8,256]{1,0:T(8,128)}) custom-call(f32[1024,1024]{1,0:T(8,128)} %fusion.68.gate_ref, f32[1024,1408]{1,0:T(8,128)} %fusion.67.inner_ref.state_ref, ...), custom_call_target="tpu_custom_call" | custom-call | flops 3145728000 | bytes 10485760 | tf_op jit(solution)/shard_map/mixer_backward/pallas_call | solution.py:433
  348.3 24.7 %mixer_backward.3 = (bf16[512,1024]{1,0:T(8,128)(2,1)}, f32[4,512,4]{2,1,0:T(8,128)}, bf16[512,256]{1,0:T(8,128)(2,1)}, f32[8,1024]{1,0:T(8,128)}, f32[4,2,4]{2,1,0:T(2,128)}, /*index=5*/f32[8,256]{1,0:T(8,128)}) custom-call(f32[1024,1024]{1,0:T(8,128)} %fusion.68.gate_ref, f32[1024,1408]{1,0:T(8,128)} %fusion.67.inner_ref.state_ref, ...), custom_call_target="tpu_custom_call" | custom-call | flops 3145728000 | bytes 10485760 | tf_op jit(solution)/shard_map/mixer_backward/pallas_call | solution.py:433
  409.0 8.2 %fusion.75 = f32[512,2048]{1,0:T(8,128)} fusion(bf16[512,1408]{1,0:T(8,128)(2,1)S(1)} %concatenate.137, bf16[2048,1408]{1,0:T(8,128)(2,1)} %constant_dynamic-update-slice_fusion.8), kind=kOutput, calls=%fused_computation.232 | convolution fusion | flops 2952790016 | bytes 11403264 | tf_op jit(solution)/shard_map/dot_general | solution.py:535
  421.5 8.6 %multiply_reduce_fusion.1 = (f32[2048]{0:T(1024)S(1)}, f32[512,2048]{1,0:T(8,128)}) fusion(bf16[512,2048]{1,0:T(8,128)(2,1)} %convolution_convert_fusion.7, f32[512,2048]{1,0:T(8,128)} %fusion.75, bf16[2048,1024]{1,0:T(8,128)(2,1)} %constant_dynamic-update-slice_fusion.16, bf16[1024,1024]{1,0:T(8,128)(2,1)S(1)} %multiply_convert_fusion), kind=kOutput, calls=%fused_computation.5 | convolution fusion | flops 2151675904 | bytes 15736832 | tf_op jit(solution)/shard_map/dot_general | solution.py:535
  437.1 8.5 %convolution_convert_fusion.2 = bf16[2048,1024]{1,0:T(8,128)(2,1)} fusion(bf16[1024,1024]{1,0:T(8,128)(2,1)S(1)} %multiply_convert_fusion, bf16[512,2048]{1,0:T(8,128)(2,1)} %collective-permute-done.1, bf16[512,2048]{1,0:T(8,128)(2,1)} %convolution_convert_fusion.7), kind=kOutput, calls=%fused_computation.16 | convolution fusion | flops 4305453056 | bytes 10485760 | tf_op jit(solution)/shard_map/dot_general | solution.py:529
  445.6 11.3 %convolution_convert_fusion = bf16[2048,1408]{1,0:T(8,128)(2,1)} fusion(bf16[512,1408]{1,0:T(8,128)(2,1)S(1)} %concatenate.138, bf16[512,1408]{1,0:T(8,128)(2,1)S(1)} %copy-done.32, bf16[512,2048]{1,0:T(8,128)(2,1)} %collective-permute-done.1, bf16[512,2048]{1,0:T(8,128)(2,1)} %convolution_convert_fusion.7), kind=kOutput, calls=%fused_computation | convolution fusion | flops 5922619392 | bytes 12845056 | tf_op jit(solution)/shard_map/dot_general | solution.py:529
  472.0 11.9 %collective-permute-done.45 = bf16[15712]{0:T(1024)(128)(2,1)S(1)} collective-permute-done((bf16[15712]{0:T(1024)(128)(2,1)S(1)}, bf16[15712]{0:T(1024)(128)(2,1)S(1)}, u32[]{:S(2)}, u32[]{:S(2)}) %collective-permute-start.45) | collective-permute-done | bytes 31456 | tf_op jit(solution)/shard_map/ppermute | solution.py:574
  484.0 24.2 %collective-permute-start.43 = (bf16[15712]{0:T(1024)(128)(2,1)S(1)}, bf16[15712]{0:T(1024)(128)(2,1)S(1)}, u32[]{:S(2)}, u32[]{:S(2)}) collective-permute-start(bf16[15712]{0:T(1024)(128)(2,1)S(1)} %convert_element_type.337), channel_id=1, source_target_pairs={{0,20},{2,22},{4,16},{6,18},{8,28},{10,30},{12,24},{14,26},{16,4},... | collective-permute-start | bytes 94280 | tf_op jit(solution)/shard_map/ppermute | solution.py:574
  529.8 10.4 %collective-permute-done.51 = bf16[256,1408]{1,0:T(8,128)(2,1)} collective-permute-done((bf16[256,1408]{1,0:T(8,128)(2,1)}, bf16[256,1408]{1,0:T(8,128)(2,1)}, u32[]{:S(2)}, u32[]{:S(2)}) %collective-permute-start.51) | collective-permute-done | bytes 720928 | tf_op jit(solution)/shard_map/ppermute | solution.py:574
  546.2 65.2 %collective-permute-done.62 = bf16[256,1024]{1,0:T(8,128)(2,1)S(1)} collective-permute-done((bf16[256,1024]{1,0:T(8,128)(2,1)S(1)}, bf16[256,1024]{1,0:T(8,128)(2,1)S(1)}, u32[]{:S(2)}, u32[]{:S(2)}) %collective-permute-start.62) | collective-permute-done | bytes 524320 | tf_op jit(solution)/shard_map/ppermute | solution.py:574
  634.7 11.3 %collective-permute-done.55 = bf16[512,1408]{1,0:T(8,128)(2,1)} collective-permute-done((bf16[512,1408]{1,0:T(8,128)(2,1)}, bf16[512,1408]{1,0:T(8,128)(2,1)}, u32[]{:S(2)}, u32[]{:S(2)}) %collective-permute-start.55) | collective-permute-done | bytes 1441824 | tf_op jit(solution)/shard_map/ppermute | solution.py:574
  672.6 11.3 %collective-permute-done.36 = bf16[256,2048]{1,0:T(8,128)(2,1)S(1)} collective-permute-done((bf16[256,2048]{1,0:T(8,128)(2,1)S(1)}, bf16[256,2048]{1,0:T(8,128)(2,1)S(1)}, u32[]{:S(2)}, u32[]{:S(2)}) %collective-permute-start.36) | collective-permute-done | bytes 1048608 | tf_op jit(solution)/shard_map/ppermute | solution.py:579
  685.3 10.2 %collective-permute-done.48 = bf16[256,1024]{1,0:T(8,128)(2,1)S(1)} collective-permute-done((bf16[256,1024]{1,0:T(8,128)(2,1)S(1)}, bf16[256,1024]{1,0:T(8,128)(2,1)S(1)}, u32[]{:S(2)}, u32[]{:S(2)}) %collective-permute-start.48) | collective-permute-done | bytes 524320 | tf_op jit(solution)/shard_map/ppermute | solution.py:574
  (464 shorter events, 337.0 us)
Async XLA Ops:
  12.2 77.1 %all-to-all-start = ((bf16[16,16,2048]{2,1,0:T(8,128)(2,1)}), bf16[16,16,2048]{2,1,0:T(8,128)(2,1)S(1)}, u32[]{:S(2)}, u32[]{:S(2)}) async-start(bf16[16,16,2048]{2,1,0:T(8,128)(2,1)} %bitcast.78), calls=%async_computation | async-start | bytes 2097152 | tf_op jit(solution)/shard_map/all_to_all | solution.py:754
  38.2 46.0 %collective-permute-start.12 = (bf16[256,1408]{1,0:T(8,128)(2,1)S(1)}, bf16[256,1408]{1,0:T(8,128)(2,1)}, u32[]{:S(2)}, u32[]{:S(2)}) collective-permute-start(bf16[256,1408]{1,0:T(8,128)(2,1)S(1)} %maximum_select_fusion.7), channel_id=1, source_target_pairs={{0,8},{2,10},{4,12},{6,14},{8,16},{10,18},{12,20},{14,22},{16,24},... | collective-permute-start | bytes 2162696 | tf_op jit(solution)/shard_map/ppermute | solution.py:574
  39.7 47.1 %collective-permute-start.11 = (bf16[256,1408]{1,0:T(8,128)(2,1)S(1)}, bf16[256,1408]{1,0:T(8,128)(2,1)}, u32[]{:S(2)}, u32[]{:S(2)}) collective-permute-start(bf16[256,1408]{1,0:T(8,128)(2,1)S(1)} %maximum_select_fusion.7), channel_id=1, source_target_pairs={{0,4},{2,6},{4,0},{6,2},{8,12},{10,14},{12,8},{14,10},{16,20},{18,... | collective-permute-start | bytes 2162696 | tf_op jit(solution)/shard_map/ppermute | solution.py:574
  58.7 51.4 %collective-permute-start.5 = (bf16[256,1024]{1,0:T(8,128)(2,1)}, bf16[256,1024]{1,0:T(8,128)(2,1)}, u32[]{:S(2)}, u32[]{:S(2)}) collective-permute-start(bf16[256,1024]{1,0:T(8,128)(2,1)} %collective-permute-done.4), channel_id=1, source_target_pairs={{0,4},{2,6},{4,0},{6,2},{8,12},{10,14},{12,8},{14,10},{16,20},{18,... | collective-permute-start | bytes 1572872 | tf_op jit(solution)/shard_map/ppermute | solution.py:574
  89.4 87.4 %all-to-all-start.2 = ((bf16[16,16,2048]{2,1,0:T(8,128)(2,1)}), bf16[16,16,2048]{2,1,0:T(8,128)(2,1)S(1)}, u32[]{:S(2)}, u32[]{:S(2)}) async-start(bf16[16,16,2048]{2,1,0:T(8,128)(2,1)} %bitcast.15), calls=%async_computation.2 | async-start | bytes 2097152 | tf_op jit(solution)/shard_map/all_to_all | solution.py:754
  112.0 59.8 %collective-permute-start = (bf16[256,2048]{1,0:T(8,128)(2,1)S(1)}, bf16[256,2048]{1,0:T(8,128)(2,1)S(1)}, u32[]{:S(2)}, u32[]{:S(2)}) collective-permute-start(bf16[256,2048]{1,0:T(8,128)(2,1)S(1)} %bitcast.76), channel_id=1, source_target_pairs={{0,1},{1,0},{2,3},{3,2},{4,5},{5,4},{6,7},{7,6},{8,9},{9,8},{10,11... | collective-permute-start | bytes 3145736 | tf_op jit(solution)/shard_map/ppermute | solution.py:579
  122.4 48.8 %collective-permute-start.8 = (bf16[256,1024]{1,0:T(8,128)(2,1)}, bf16[256,1024]{1,0:T(8,128)(2,1)}, u32[]{:S(2)}, u32[]{:S(2)}) collective-permute-start(bf16[256,1024]{1,0:T(8,128)(2,1)} %collective-permute-done.6), channel_id=1, source_target_pairs={{0,8},{2,10},{4,12},{6,14},{8,16},{10,18},{12,20},{14,22},{16,24},... | collective-permute-start | bytes 1572872 | tf_op jit(solution)/shard_map/ppermute | solution.py:574
  123.9 45.8 %collective-permute-start.27 = (bf16[256,1024]{1,0:T(8,128)(2,1)S(1)}, bf16[256,1024]{1,0:T(8,128)(2,1)}, u32[]{:S(2)}, u32[]{:S(2)}) collective-permute-start(bf16[256,1024]{1,0:T(8,128)(2,1)S(1)} %collective-permute-done.25), channel_id=1, source_target_pairs={{0,8},{2,10},{4,12},{6,14},{8,16},{10,18},{12,20},{14,22},{16,24},... | collective-permute-start | bytes 1572872 | tf_op jit(solution)/shard_map/ppermute | solution.py:574
  148.6 70.9 %collective-permute-start.16 = (bf16[256,1408]{1,0:T(8,128)(2,1)S(1)}, bf16[256,1408]{1,0:T(8,128)(2,1)}, u32[]{:S(2)}, u32[]{:S(2)}) collective-permute-start(bf16[256,1408]{1,0:T(8,128)(2,1)S(1)} %collective-permute-done.14), channel_id=1, source_target_pairs={{0,8},{2,10},{4,12},{6,14},{8,16},{10,18},{12,20},{14,22},{16,24},... | collective-permute-start | bytes 2162696 | tf_op jit(solution)/shard_map/ppermute | solution.py:574
  169.7 52.1 %collective-permute-start.15 = (bf16[256,1408]{1,0:T(8,128)(2,1)S(1)}, bf16[256,1408]{1,0:T(8,128)(2,1)}, u32[]{:S(2)}, u32[]{:S(2)}) collective-permute-start(bf16[256,1408]{1,0:T(8,128)(2,1)S(1)} %collective-permute-done.14), channel_id=1, source_target_pairs={{0,4},{2,6},{4,0},{6,2},{8,12},{10,14},{12,8},{14,10},{16,20},{18,... | collective-permute-start | bytes 2162696 | tf_op jit(solution)/shard_map/ppermute | solution.py:574
  171.2 44.6 %collective-permute-start.28 = (bf16[256,1024]{1,0:T(8,128)(2,1)}, bf16[256,1024]{1,0:T(8,128)(2,1)}, u32[]{:S(2)}, u32[]{:S(2)}) collective-permute-start(bf16[256,1024]{1,0:T(8,128)(2,1)} %collective-permute-done.27), channel_id=1, source_target_pairs={{0,4},{2,6},{4,0},{6,2},{8,12},{10,14},{12,8},{14,10},{16,20},{18,... | collective-permute-start | bytes 1572872 | tf_op jit(solution)/shard_map/ppermute | solution.py:574
  175.9 63.1 %collective-permute-start.1 = (bf16[512,2048]{1,0:T(8,128)(2,1)}, bf16[512,2048]{1,0:T(8,128)(2,1)}, u32[]{:S(2)}, u32[]{:S(2)}) collective-permute-start(bf16[512,2048]{1,0:T(8,128)(2,1)} %convolution_convert_fusion.7), channel_id=1, source_target_pairs={{0,2},{2,0},{4,6},{6,4},{8,10},{10,8},{12,14},{14,12},{16,18},{18,... | collective-permute-start | bytes 6291464 | tf_op jit(solution)/shard_map/ppermute | solution.py:574
  235.5 64.9 %collective-permute-start.32 = (bf16[512,2048]{1,0:T(8,128)(2,1)}, bf16[512,2048]{1,0:T(8,128)(2,1)}, u32[]{:S(2)}, u32[]{:S(2)}) collective-permute-start(bf16[512,2048]{1,0:T(8,128)(2,1)} %convolution_convert_fusion.5), channel_id=1, source_target_pairs={{0,2},{2,0},{4,6},{6,4},{8,10},{10,8},{12,14},{14,12},{16,18},{18,... | collective-permute-start | bytes 6291464 | tf_op jit(solution)/shard_map/ppermute | solution.py:574
  392.9 131.9 %collective-permute-start.59 = (bf16[512,1024]{1,0:T(8,128)(2,1)}, bf16[512,1024]{1,0:T(8,128)(2,1)}, u32[]{:S(2)}, u32[]{:S(2)}) collective-permute-start(bf16[512,1024]{1,0:T(8,128)(2,1)} %get-tuple-element.158), channel_id=1, source_target_pairs={{0,8},{2,10},{4,12},{6,14},{8,16},{10,18},{12,20},{14,22},{16,24},... | collective-permute-start | bytes 3145736 | tf_op jit(solution)/shard_map/ppermute | solution.py:574
  397.1 127.8 %collective-permute-start.61 = (bf16[512,1024]{1,0:T(8,128)(2,1)}, bf16[512,1024]{1,0:T(8,128)(2,1)}, u32[]{:S(2)}, u32[]{:S(2)}) collective-permute-start(bf16[512,1024]{1,0:T(8,128)(2,1)} %get-tuple-element.159), channel_id=1, source_target_pairs={{0,24},{2,26},{4,28},{6,30},{8,0},{10,2},{12,4},{14,6},{16,8},{18,... | collective-permute-start | bytes 3145736 | tf_op jit(solution)/shard_map/ppermute | solution.py:574
  457.1 69.7 %collective-permute-start.60 = (bf16[512,1024]{1,0:T(8,128)(2,1)}, bf16[512,1024]{1,0:T(8,128)(2,1)S(1)}, u32[]{:S(2)}, u32[]{:S(2)}) collective-permute-start(bf16[512,1024]{1,0:T(8,128)(2,1)} %get-tuple-element.160), channel_id=1, source_target_pairs={{0,16},{2,18},{4,20},{6,22},{8,24},{10,26},{12,28},{14,30},{16,0},... | collective-permute-start | bytes 3145736 | tf_op jit(solution)/shard_map/ppermute | solution.py:574
  520.9 96.2 %collective-permute-start.29 = (bf16[512,2048]{1,0:T(8,128)(2,1)}, bf16[512,2048]{1,0:T(8,128)(2,1)}, u32[]{:S(2)}, u32[]{:S(2)}) collective-permute-start(bf16[512,2048]{1,0:T(8,128)(2,1)} %convolution_convert_fusion.3), channel_id=1, source_target_pairs={{0,2},{2,0},{4,6},{6,4},{8,10},{10,8},{12,14},{14,12},{16,18},{18,... | collective-permute-start | bytes 6291464 | tf_op jit(solution)/shard_map/ppermute | solution.py:574
  524.7 102.8 %collective-permute-start.46 = (bf16[1024,1024]{1,0:T(8,128)(2,1)}, bf16[1024,1024]{1,0:T(8,128)(2,1)S(1)}, u32[]{:S(2)}, u32[]{:S(2)}) collective-permute-start(bf16[1024,1024]{1,0:T(8,128)(2,1)} %pad_maximum_fusion.4), channel_id=1, source_target_pairs={{0,4},{2,6},{4,0},{6,2},{8,12},{10,14},{12,8},{14,10},{16,20},{18,... | collective-permute-start | bytes 6291464 | tf_op jit(solution)/shard_map/ppermute | solution.py:574
  524.9 86.7 %collective-permute-start.53 = (bf16[256,1408]{1,0:T(8,128)(2,1)}, bf16[256,1408]{1,0:T(8,128)(2,1)S(1)}, u32[]{:S(2)}, u32[]{:S(2)}) collective-permute-start(bf16[256,1408]{1,0:T(8,128)(2,1)} %get-tuple-element.156), channel_id=1, source_target_pairs={{0,4},{2,6},{4,0},{6,2},{8,12},{10,14},{12,8},{14,10},{16,20},{18,... | collective-permute-start | bytes 2162696 | tf_op jit(solution)/shard_map/ppermute | solution.py:574
  529.6 81.8 %collective-permute-start.62 = (bf16[256,1024]{1,0:T(8,128)(2,1)S(1)}, bf16[256,1024]{1,0:T(8,128)(2,1)S(1)}, u32[]{:S(2)}, u32[]{:S(2)}) collective-permute-start(bf16[256,1024]{1,0:T(8,128)(2,1)S(1)} %dynamic-slice_convert_fusion), channel_id=1, source_target_pairs={{0,4},{2,6},{4,0},{6,2},{8,12},{10,14},{12,8},{14,10},{16,20},{18,... | collective-permute-start | bytes 1572872 | tf_op jit(solution)/shard_map/ppermute | solution.py:574
  541.8 71.7 %collective-permute-start.52 = (bf16[256,1408]{1,0:T(8,128)(2,1)S(1)}, bf16[256,1408]{1,0:T(8,128)(2,1)S(1)}, u32[]{:S(2)}, u32[]{:S(2)}) collective-permute-start(bf16[256,1408]{1,0:T(8,128)(2,1)S(1)} %add_convert_fusion.7), channel_id=1, source_target_pairs={{0,8},{2,10},{4,12},{6,14},{8,16},{10,18},{12,20},{14,22},{16,24},... | collective-permute-start | bytes 2162696 | tf_op jit(solution)/shard_map/ppermute | solution.py:574
  652.8 47.4 %all-to-all-start.1 = ((bf16[16,16,2048]{2,1,0:T(8,128)(2,1)}), bf16[16,16,2048]{2,1,0:T(8,128)(2,1)}, u32[]{:S(2)}, u32[]{:S(2)}) async-start(bf16[16,16,2048]{2,1,0:T(8,128)(2,1)} %bitcast.13), calls=%async_computation.1 | async-start | bytes 2097152 | tf_op jit(solution)/shard_map/all_to_all | solution.py:810
  672.6 46.0 %collective-permute-start.57 = (bf16[128,1408]{1,0:T(8,128)(2,1)}, bf16[128,1408]{1,0:T(8,128)(2,1)S(1)}, u32[]{:S(2)}, u32[]{:S(2)}) collective-permute-start(bf16[128,1408]{1,0:T(8,128)(2,1)} %dynamic-slice_convert_fusion.1), channel_id=1, source_target_pairs={{0,2},{2,0},{4,6},{6,4},{8,10},{10,8},{12,14},{14,12},{16,18},{18,... | collective-permute-start | bytes 1081352 | tf_op jit(solution)/shard_map/ppermute | solution.py:574
  700.2 48.7 %all-to-all-start.3 = ((bf16[16,16,2048]{2,1,0:T(8,128)(2,1)}), bf16[16,16,2048]{2,1,0:T(8,128)(2,1)}, u32[]{:S(2)}, u32[]{:S(2)}) async-start(bf16[16,16,2048]{2,1,0:T(8,128)(2,1)} %bitcast.75), calls=%async_computation.3 | async-start | bytes 2097152 | tf_op jit(solution)/shard_map/all_to_all | solution.py:810
  (122 other events, 2316.9 us)
